TPU v7x, 256 devices: a whole 4x4x8 slice. The times are simulated.
256 devices in a mesh: ctx: 32 (over x, y, core), head: 8 (over z).
Axes of the slice: x: 4, y: 4, z: 8, core: 2. Of those that a mesh axis runs over, the one named last changes fastest.
Arguments:
- queries: bfloat16 [8192, 8192], P(('ctx', 'head')), may hold values from -6 to 6
- key_heads: bfloat16 [8192, 1024], P(('ctx', 'head')), may hold values from -6 to 6
- value_head_array: bfloat16 [8192, 1024], P(('ctx', 'head')), may hold values from -6 to 6
- out_grad: bfloat16 [8192, 8192], P(('ctx', 'head')), may hold values from -6 to 6
- doc_ids: int32 [8192], P('ctx'), may hold values from 0 to 127, never falling along the last dimension, each value on 1 to 1792 neighbouring positions
Outputs:
- attended: bfloat16 [8192, 8192], P(('ctx', 'head'))
- query_grad: bfloat16 [8192, 8192], P(('ctx', 'head'))
- key_grad: bfloat16 [8192, 1024], P(('ctx', 'head'))
- value_grad: bfloat16 [8192, 1024], P(('ctx', 'head'))
Inputs may be any that keep to these rules, and one draw needn't show every extreme that they name: `doc_ids`: document numbers never fall along the batch; each document holds 1 to 1792 consecutive tokens and one holds exactly 1792.
All inputs are finite; a program needn't handle non-finite values.
Results may differ from a plain program's by a relative error of at most 0.022.
Values may be sent and summed in bfloat16 or wider, within the bound.
No kernel may reach another device: no remote copies, remote signals or barrier semaphores. Data moves between devices by JAX's collectives and lax.ppermute only.
A program may use at most 128 MiB of HBM per device.

v0:
```python
import jax
import jax.numpy as jnp
from jax import lax
from jax.sharding import PartitionSpec as P

HEAD_SIZE = 128
WIN_DEV = 6
WINDOW = 1536


def passed_along(value, axis, steps):
    count = lax.axis_size(axis)
    leading, last = (max(0, -steps), min(count, count - steps))
    return lax.ppermute(value, axis, [(source, source + steps) for source in range(leading, last)])


def local(queries, key_heads, value_head_array, out_grad, doc_ids):
    query_loc, grad_loc, key_loc, value_loc = (
        lax.all_to_all(queries, "head", split_axis=1, concat_axis=0, tiled=True),
        lax.all_to_all(out_grad, "head", split_axis=1, concat_axis=0, tiled=True),
        lax.all_to_all(key_heads, "head", split_axis=1, concat_axis=0, tiled=True),
        lax.all_to_all(value_head_array, "head", split_axis=1, concat_axis=0, tiled=True),
    )
    tok_rows = query_loc.shape[0]
    kv_heads = key_loc.shape[1] // HEAD_SIZE
    group_size = query_loc.shape[1] // key_loc.shape[1]
    score_scale = HEAD_SIZE ** (-0.5)
    query_four = query_loc.reshape(tok_rows, kv_heads, group_size, HEAD_SIZE)
    grad_four = grad_loc.reshape(tok_rows, kv_heads, group_size, HEAD_SIZE)
    device = lax.axis_index("ctx")
    query_pos = device * tok_rows + jnp.arange(tok_rows, dtype=jnp.int32)
    query_doc = doc_ids.astype(jnp.float32)
    own_block = (jnp.stack([key_loc, value_loc]), doc_ids.astype(jnp.bfloat16))
    blocks = [own_block]
    for offset in range(1, WIN_DEV + 1):
        blocks.append(passed_along((own_block[0], own_block[1]), "ctx", offset))
    visibles = []
    for offset in range(WIN_DEV + 1):
        key_pos = (device - offset) * tok_rows + jnp.arange(tok_rows, dtype=jnp.int32)
        same_doc = query_doc[:, None] == blocks[offset][1].astype(jnp.float32)[None, :]
        distance = query_pos[:, None] - key_pos[None, :]
        visibles.append(same_doc & (key_pos[None, :] >= 0) & (distance >= 0) & (distance < WINDOW))
    stored = []
    for offset in range(WIN_DEV + 1):

        def scores_of(unused, offset=offset):
            key_three = blocks[offset][0][0].reshape(tok_rows, kv_heads, HEAD_SIZE)
            raw = (
                jnp.einsum(
                    "qgpd,kgd->gpqk", query_four, key_three, preferred_element_type=jnp.float32
                )
                * score_scale
            )
            return jnp.where(visibles[offset], raw, -jnp.inf)

        if offset == 0:
            stored.append(scores_of(0))
        else:
            stored.append(scores_of(0))
    running = jnp.max(stored[0], axis=-1)
    totals = jnp.sum(jnp.where(visibles[0], jnp.exp(stored[0] - running[..., None]), 0.0), axis=-1)
    for offset in range(1, WIN_DEV + 1):

        def extend(carry_state, offset=offset):
            old_max, old_total = carry_state
            masked = stored[offset]
            new_max = jnp.maximum(old_max, jnp.max(masked, axis=-1))
            fresh_total = jnp.sum(
                jnp.where(visibles[offset], jnp.exp(masked - new_max[..., None]), 0.0), axis=-1
            )
            return (new_max, old_total * jnp.exp(old_max - new_max) + fresh_total)

        running, totals = extend((running, totals))
    log_total = running + jnp.log(totals)
    probs = []
    for offset in range(WIN_DEV + 1):

        def probs_of(unused, offset=offset):
            return jnp.where(visibles[offset], jnp.exp(stored[offset] - log_total[..., None]), 0.0)

        probs.append(probs_of(0))
    stored = None
    attended = jnp.zeros((tok_rows, kv_heads, group_size, HEAD_SIZE), jnp.float32)
    for offset in range(WIN_DEV + 1):

        def forward(partial_sum, offset=offset):
            weights = probs[offset].astype(jnp.bfloat16)
            value_three = blocks[offset][0][1].reshape(tok_rows, kv_heads, HEAD_SIZE)
            return partial_sum + jnp.einsum(
                "gpqk,kgd->qgpd", weights, value_three, preferred_element_type=jnp.float32
            )

        attended = forward(attended)
    out_rounded = attended.astype(jnp.bfloat16)
    attended_out = lax.all_to_all(
        out_rounded.reshape(tok_rows, -1), "head", split_axis=0, concat_axis=1, tiled=True
    )
    row_delta = jnp.transpose(
        jnp.sum(grad_four.astype(jnp.float32) * out_rounded.astype(jnp.float32), axis=-1), (1, 2, 0)
    )
    query_total = jnp.zeros((tok_rows, kv_heads, group_size, HEAD_SIZE), jnp.float32)
    empty_grad = jnp.zeros((2, tok_rows, kv_heads * HEAD_SIZE), jnp.float32)
    partials = []
    for offset in range(WIN_DEV + 1):

        def backward(carry_state, offset=offset):
            prob_block = probs[offset]
            weights = prob_block.astype(jnp.bfloat16)
            key_three = blocks[offset][0][0].reshape(tok_rows, kv_heads, HEAD_SIZE)
            value_three = blocks[offset][0][1].reshape(tok_rows, kv_heads, HEAD_SIZE)
            prob_grad = jnp.einsum(
                "qgpd,kgd->gpqk", grad_four, value_three, preferred_element_type=jnp.float32
            )
            score_grad = (prob_block * (prob_grad - row_delta[..., None])).astype(jnp.bfloat16)
            query_term = (
                jnp.einsum(
                    "gpqk,kgd->qgpd", score_grad, key_three, preferred_element_type=jnp.float32
                )
                * score_scale
            )
            key_term = (
                jnp.einsum(
                    "gpqk,qgpd->kgd", score_grad, query_four, preferred_element_type=jnp.float32
                )
                * score_scale
            )
            value_term = jnp.einsum(
                "gpqk,qgpd->kgd", weights, grad_four, preferred_element_type=jnp.float32
            )
            kv_grad = jnp.stack([key_term.reshape(tok_rows, -1), value_term.reshape(tok_rows, -1)])
            return (carry_state[0] + query_term, kv_grad)

        query_total, kv_grad = backward((query_total, empty_grad))
        partials.append(kv_grad)
    carried = partials[WIN_DEV]
    for offset in range(WIN_DEV - 1, -1, -1):
        carried = passed_along(carried, "ctx", -1) + partials[offset]
    kv_rounded = carried.astype(jnp.bfloat16)
    query_rounded = query_total.astype(jnp.bfloat16).reshape(tok_rows, -1)
    query_grad, key_grad, value_grad = (
        lax.all_to_all(query_rounded, "head", split_axis=0, concat_axis=1, tiled=True),
        lax.all_to_all(kv_rounded[0], "head", split_axis=0, concat_axis=1, tiled=True),
        lax.all_to_all(kv_rounded[1], "head", split_axis=0, concat_axis=1, tiled=True),
    )
    return (attended_out, query_grad, key_grad, value_grad)


def solution(mesh):
    placed = (
        P(("ctx", "head"), None),
        P(("ctx", "head"), None),
        P(("ctx", "head"), None),
        P(("ctx", "head"), None),
        P("ctx"),
    )
    return jax.shard_map(
        local,
        mesh=mesh,
        in_specs=placed,
        out_specs=(
            P(("ctx", "head"), None),
            P(("ctx", "head"), None),
            P(("ctx", "head"), None),
            P(("ctx", "head"), None),
        ),
        check_vma=False,
    )
```

profile of v0, /device:TPU:2, one launch (start us, length us, event | category | flops | bytes accessed | tf_op | source)
XLA Modules:
  0.0 233.8 jit_solution(8374698056969620815)
XLA Ops:
  1.4 1.9 collective-permute-start
  3.3 4.8 %collective-permute-start.4 = (bf16[256]{0:T(256)(128)(2,1)S(1)}, bf16[256]{0:T(256)(128)(2,1)S(1)}, u32[]{:S(2)}, u32[]{:S(2)}) collective-permute-start(bf16[256]{0:T(256)(128)(2,1)S(1)} %get-tuple-element.11), channel_id=1, source_target_pairs={{0,24},{8,32},{16,40},{24,48},{32,56},{40,64},{48,72},{56,80},{64,... | collective-permute-start | bytes 1544 | tf_op jit(solution)/shard_map/ppermute | solution.py:14
  8.1 4.4 %collective-permute-start.6 = (bf16[256]{0:T(256)(128)(2,1)S(1)}, bf16[256]{0:T(256)(128)(2,1)S(1)}, u32[]{:S(2)}, u32[]{:S(2)}) collective-permute-start(bf16[256]{0:T(256)(128)(2,1)S(1)} %get-tuple-element.11), channel_id=1, source_target_pairs={{0,32},{8,40},{16,48},{24,56},{32,64},{40,72},{48,80},{56,88},{64,... | collective-permute-start | bytes 1544 | tf_op jit(solution)/shard_map/ppermute | solution.py:14
  12.5 3.7 %collective-permute-start.8 = (bf16[256]{0:T(256)(128)(2,1)S(1)}, bf16[256]{0:T(256)(128)(2,1)S(1)}, u32[]{:S(2)}, u32[]{:S(2)}) collective-permute-start(bf16[256]{0:T(256)(128)(2,1)S(1)} %get-tuple-element.11), channel_id=1, source_target_pairs={{0,40},{8,48},{16,56},{24,64},{32,72},{40,80},{48,88},{56,96},{64,... | collective-permute-start | bytes 1544 | tf_op jit(solution)/shard_map/ppermute | solution.py:14
  16.2 3.6 %collective-permute-start.10 = (bf16[256]{0:T(256)(128)(2,1)S(1)}, bf16[256]{0:T(256)(128)(2,1)S(1)}, u32[]{:S(2)}, u32[]{:S(2)}) collective-permute-start(bf16[256]{0:T(256)(128)(2,1)S(1)} %get-tuple-element.11), channel_id=1, source_target_pairs={{0,48},{8,56},{16,64},{24,72},{32,80},{40,88},{48,96},{56,104},{64... | collective-permute-start | bytes 1544 | tf_op jit(solution)/shard_map/ppermute | solution.py:14
  20.4 8.5 %all-to-all-start = ((bf16[32,8,128]{2,0,1:T(8,128)(2,1)}), bf16[32,8,128]{2,0,1:T(8,128)(2,1)S(1)}, u32[]{:S(2)}, u32[]{:S(2)}) async-start(bf16[32,8,128]{2,0,1:T(8,128)(2,1)} %copy_bitcast_fusion.5), calls=%async_computation | async-start | bytes 131072 | tf_op jit(solution)/shard_map/all_to_all | solution.py:21
  29.0 1.5 copy_bitcast_fusion.4
  30.5 6.8 %all-to-all-done = bf16[32,8,128]{2,0,1:T(8,128)(2,1)S(1)} async-done(((bf16[32,8,128]{2,0,1:T(8,128)(2,1)}), bf16[32,8,128]{2,0,1:T(8,128)(2,1)S(1)}, u32[]{:S(2)}, u32[]{:S(2)}) %all-to-all-start) | async-done | bytes 65568 | tf_op jit(solution)/shard_map/all_to_all | solution.py:21
  37.3 3.4 %all-to-all-start.2 = ((bf16[32,8,128]{2,0,1:T(8,128)(2,1)}), bf16[32,8,128]{2,0,1:T(8,128)(2,1)S(1)}, u32[]{:S(2)}, u32[]{:S(2)}) async-start(bf16[32,8,128]{2,0,1:T(8,128)(2,1)} %copy_bitcast_fusion.4), calls=%async_computation.2 | async-start | bytes 131072 | tf_op jit(solution)/shard_map/all_to_all | solution.py:22
  40.7 1.9 copy.397
  42.5 6.4 %all-to-all-done.2 = bf16[32,8,128]{2,0,1:T(8,128)(2,1)S(1)} async-done(((bf16[32,8,128]{2,0,1:T(8,128)(2,1)}), bf16[32,8,128]{2,0,1:T(8,128)(2,1)S(1)}, u32[]{:S(2)}, u32[]{:S(2)}) %all-to-all-start.2) | async-done | bytes 65568 | tf_op jit(solution)/shard_map/all_to_all | solution.py:22
  48.9 3.5 %all-to-all-start.1 = ((bf16[32,8,1024]{2,0,1:T(8,128)(2,1)}), bf16[32,8,1024]{2,0,1:T(8,128)(2,1)S(1)}, u32[]{:S(2)}, u32[]{:S(2)}) async-start(bf16[32,8,1024]{2,0,1:T(8,128)(2,1)} %bitcast.517), calls=%async_computation.1 | async-start | bytes 1048576 | tf_op jit(solution)/shard_map/all_to_all | solution.py:19
  52.5 2.9 %collective-permute-start.2 = (bf16[256]{0:T(256)(128)(2,1)S(1)}, bf16[256]{0:T(256)(128)(2,1)S(1)}, u32[]{:S(2)}, u32[]{:S(2)}) collective-permute-start(bf16[256]{0:T(256)(128)(2,1)S(1)} %get-tuple-element.11), channel_id=1, source_target_pairs={{0,16},{8,24},{16,32},{24,40},{32,48},{40,56},{48,64},{56,72},{64,... | collective-permute-start | bytes 1544 | tf_op jit(solution)/shard_map/ppermute | solution.py:14
  56.3 3.8 %collective-permute-done.2 = bf16[256]{0:T(256)(128)(2,1)S(1)} collective-permute-done((bf16[256]{0:T(256)(128)(2,1)S(1)}, bf16[256]{0:T(256)(128)(2,1)S(1)}, u32[]{:S(2)}, u32[]{:S(2)}) %collective-permute-start.2) | collective-permute-done | bytes 544 | tf_op jit(solution)/shard_map/ppermute | solution.py:14
  61.9 1.9 collective-permute-start.11
  63.8 1.9 collective-permute-start.9
  65.7 1.9 collective-permute-start.7
  67.6 3.3 %collective-permute-start.5 = (bf16[2,256,128]{2,1,0:T(8,128)(2,1)}, bf16[2,256,128]{2,1,0:T(8,128)(2,1)S(1)}, u32[]{:S(2)}, u32[]{:S(2)}) collective-permute-start(bf16[2,256,128]{2,1,0:T(8,128)(2,1)} %pad_maximum_fusion.1), channel_id=1, source_target_pairs={{0,24},{8,32},{16,40},{24,48},{32,56},{40,64},{48,72},{56,80},{64,... | collective-permute-start | bytes 393224 | tf_op jit(solution)/shard_map/ppermute | solution.py:14
  70.9 3.8 %collective-permute-start.1 = (bf16[2,256,128]{2,1,0:T(8,128)(2,1)}, bf16[2,256,128]{2,1,0:T(8,128)(2,1)S(1)}, u32[]{:S(2)}, u32[]{:S(2)}) collective-permute-start(bf16[2,256,128]{2,1,0:T(8,128)(2,1)} %pad_maximum_fusion.1), channel_id=1, source_target_pairs={{0,8},{8,16},{16,24},{24,32},{32,40},{40,48},{48,56},{56,64},{64,7... | collective-permute-start | bytes 393224 | tf_op jit(solution)/shard_map/ppermute | solution.py:14
  74.7 7.1 %all-to-all-start.4 = ((bf16[32,8,1024]{2,0,1:T(8,128)(2,1)}), bf16[32,8,1024]{2,0,1:T(8,128)(2,1)S(1)}, u32[]{:S(2)}, u32[]{:S(2)}) async-start(bf16[32,8,1024]{2,0,1:T(8,128)(2,1)} %bitcast.516), calls=%async_computation.4 | async-start | bytes 1048576 | tf_op jit(solution)/shard_map/all_to_all | solution.py:20
  82.0 1.8 fusion.149
  83.8 2.1 collective-permute-start.3
  85.9 1.8 fusion.144
  87.8 2.4 %fusion.145 = (f32[8,256]{1,0:T(8,128)}, f32[1,8,256,256]{2,3,1,0:T(8,128)}) fusion(bf16[256,8,128]{2,1,0:T(8,128)(2,1)S(1)} %bitcast.520, bf16[2,256,128]{2,1,0:T(8,128)(2,1)S(1)} %collective-permute-done.9, pred[256,256]{0,1:T(8,128)(4,1)S(1)} %get-tuple-element.17), kind=kOutput, calls=%fused_computation.239 | convolution fusion | flops 135788544 | bytes 2760704 | tf_op jit(solution)/shard_map/qgpd,kgd->gpqk/dot_general | solution.py:49
  90.2 2.4 %fusion.146 = (f32[8,256]{1,0:T(8,128)}, f32[1,8,256,256]{2,3,1,0:T(8,128)}) fusion(bf16[256,8,128]{2,1,0:T(8,128)(2,1)S(1)} %bitcast.521, bf16[2,256,128]{2,1,0:T(8,128)(2,1)S(1)} %collective-permute-done.7, pred[256,256]{0,1:T(8,128)(4,1)S(1)} %get-tuple-element.16), kind=kOutput, calls=%fused_computation.240 | convolution fusion | flops 135788544 | bytes 2760704 | tf_op jit(solution)/shard_map/qgpd,kgd->gpqk/dot_general | solution.py:49
  92.6 2.5 %fusion.147 = (f32[8,256]{1,0:T(8,128)}, f32[1,8,256,256]{2,3,1,0:T(8,128)}) fusion(bf16[256,8,128]{2,1,0:T(8,128)(2,1)S(1)} %bitcast.522, bf16[2,256,128]{2,1,0:T(8,128)(2,1)S(1)} %collective-permute-done.5, pred[256,256]{0,1:T(8,128)(4,1)S(1)} %get-tuple-element.15), kind=kOutput, calls=%fused_computation.241 | convolution fusion | flops 135788544 | bytes 2760704 | tf_op jit(solution)/shard_map/qgpd,kgd->gpqk/dot_general | solution.py:49
  95.1 4.5 %all-to-all-done.4 = bf16[32,8,1024]{2,0,1:T(8,128)(2,1)S(1)} async-done(((bf16[32,8,1024]{2,0,1:T(8,128)(2,1)}), bf16[32,8,1024]{2,0,1:T(8,128)(2,1)S(1)}, u32[]{:S(2)}, u32[]{:S(2)}) %all-to-all-start.4) | async-done | bytes 524320 | tf_op jit(solution)/shard_map/all_to_all | solution.py:20
  99.9 1.4 copy.219
  102.0 1.3 fusion.150
  103.8 1.3 fusion.148
  105.9 1.5 copy-done.2
  112.2 1.4 fusion.85
  117.5 1.6 multiply_reduce_fusion
  119.8 1.1 fusion.45
  123.5 3.9 %collective-permute-start.12 = (f32[2,256,128]{2,1,0:T(8,128)}, f32[2,256,128]{2,1,0:T(8,128)}, u32[]{:S(2)}, u32[]{:S(2)}) collective-permute-start(f32[2,256,128]{2,1,0:T(8,128)} %pad_maximum_fusion), channel_id=1, source_target_pairs={{8,0},{16,8},{24,16},{32,24},{40,32},{48,40},{56,48},{64,56},{72,6... | collective-permute-start | bytes 786440 | tf_op jit(solution)/shard_map/ppermute | solution.py:14
  129.8 1.1 fusion.53
  131.6 1.1 fusion.51
  132.7 1.5 fusion.23
  134.2 1.1 fusion.49
  136.0 1.1 fusion.47
  137.1 1.4 convolution_multiply_fusion.4
  141.4 1.1 copy.245
  142.5 2.1 all_to_all.120
  144.6 4.1 %all-to-all-start.5 = ((bf16[8,32,1024]{2,1,0:T(8,128)(2,1)}), bf16[8,32,1024]{2,1,0:T(8,128)(2,1)}, u32[]{:S(2)}, u32[]{:S(2)}) async-start(bf16[8,32,1024]{2,1,0:T(8,128)(2,1)} %all_to_all.120), calls=%async_computation.5 | async-start | bytes 1048576 | tf_op jit(solution)/shard_map/all_to_all | solution.py:141
  149.8 2.1 all_to_all.113
  151.9 2.2 convolution_bitcast_fusion.11
  155.2 2.6 %collective-permute-start.13 = (f32[2,256,128]{2,1,0:T(8,128)S(1)}, f32[2,256,128]{2,1,0:T(8,128)S(1)}, u32[]{:S(2)}, u32[]{:S(2)}) collective-permute-start(f32[2,256,128]{2,1,0:T(8,128)S(1)} %maximum_add_fusion), channel_id=1, source_target_pairs={{8,0},{16,8},{24,16},{32,24},{40,32},{48,40},{56,48},{64,56},{72,6... | collective-permute-start | bytes 786440 | tf_op jit(solution)/shard_map/ppermute | solution.py:14
  158.3 3.3 %collective-permute-done.13 = f32[2,256,128]{2,1,0:T(8,128)S(1)} collective-permute-done((f32[2,256,128]{2,1,0:T(8,128)S(1)}, f32[2,256,128]{2,1,0:T(8,128)S(1)}, u32[]{:S(2)}, u32[]{:S(2)}) %collective-permute-start.13) | collective-permute-done | bytes 262176 | tf_op jit(solution)/shard_map/ppermute | solution.py:14
  161.7 6.7 %collective-permute-start.14 = (f32[2,256,128]{2,1,0:T(8,128)S(1)}, f32[2,256,128]{2,1,0:T(8,128)S(1)}, u32[]{:S(2)}, u32[]{:S(2)}) collective-permute-start(f32[2,256,128]{2,1,0:T(8,128)S(1)} %maximum_add_fusion.1), channel_id=1, source_target_pairs={{8,0},{16,8},{24,16},{32,24},{40,32},{48,40},{56,48},{64,56},{72,6... | collective-permute-start | bytes 786440 | tf_op jit(solution)/shard_map/ppermute | solution.py:14
  168.9 3.1 %collective-permute-done.14 = f32[2,256,128]{2,1,0:T(8,128)S(1)} collective-permute-done((f32[2,256,128]{2,1,0:T(8,128)S(1)}, f32[2,256,128]{2,1,0:T(8,128)S(1)}, u32[]{:S(2)}, u32[]{:S(2)}) %collective-permute-start.14) | collective-permute-done | bytes 262176 | tf_op jit(solution)/shard_map/ppermute | solution.py:14
  172.1 5.9 %collective-permute-start.15 = (f32[2,256,128]{2,1,0:T(8,128)S(1)}, f32[2,256,128]{2,1,0:T(8,128)S(1)}, u32[]{:S(2)}, u32[]{:S(2)}) collective-permute-start(f32[2,256,128]{2,1,0:T(8,128)S(1)} %maximum_add_fusion.2), channel_id=1, source_target_pairs={{8,0},{16,8},{24,16},{32,24},{40,32},{48,40},{56,48},{64,56},{72,6... | collective-permute-start | bytes 786440 | tf_op jit(solution)/shard_map/ppermute | solution.py:14
  178.5 3.4 %collective-permute-done.15 = f32[2,256,128]{2,1,0:T(8,128)S(1)} collective-permute-done((f32[2,256,128]{2,1,0:T(8,128)S(1)}, f32[2,256,128]{2,1,0:T(8,128)S(1)}, u32[]{:S(2)}, u32[]{:S(2)}) %collective-permute-start.15) | collective-permute-done | bytes 262176 | tf_op jit(solution)/shard_map/ppermute | solution.py:14
  181.9 6.1 %collective-permute-start.16 = (f32[2,256,128]{2,1,0:T(8,128)S(1)}, f32[2,256,128]{2,1,0:T(8,128)S(1)}, u32[]{:S(2)}, u32[]{:S(2)}) collective-permute-start(f32[2,256,128]{2,1,0:T(8,128)S(1)} %maximum_add_fusion.3), channel_id=1, source_target_pairs={{8,0},{16,8},{24,16},{32,24},{40,32},{48,40},{56,48},{64,56},{72,6... | collective-permute-start | bytes 786440 | tf_op jit(solution)/shard_map/ppermute | solution.py:14
  188.0 1.2 convolution_bitcast_fusion.3
  189.1 6.5 %all-to-all-start.3 = ((bf16[8,32,1024]{2,1,0:T(8,128)(2,1)}), bf16[8,32,1024]{2,1,0:T(8,128)(2,1)S(1)}, u32[]{:S(2)}, u32[]{:S(2)}) async-start(bf16[8,32,1024]{2,1,0:T(8,128)(2,1)} %all_to_all.113), calls=%async_computation.3 | async-start | bytes 1048576 | tf_op jit(solution)/shard_map/all_to_all | solution.py:95
  196.7 2.0 collective-permute-start.17
  198.8 2.1 convolution_bitcast_fusion.1
  200.9 1.8 collective-permute-done.17
  203.3 6.5 %all-to-all-done.3 = bf16[8,32,1024]{2,1,0:T(8,128)(2,1)S(1)} async-done(((bf16[8,32,1024]{2,1,0:T(8,128)(2,1)}), bf16[8,32,1024]{2,1,0:T(8,128)(2,1)S(1)}, u32[]{:S(2)}, u32[]{:S(2)}) %all-to-all-start.3) | async-done | bytes 524320 | tf_op jit(solution)/shard_map/all_to_all | solution.py:95
  209.8 3.4 %all-to-all-start.7 = ((bf16[8,32,128]{2,1,0:T(8,128)(2,1)}), bf16[8,32,128]{2,1,0:T(8,128)(2,1)S(1)}, u32[]{:S(2)}, u32[]{:S(2)}) async-start(bf16[8,32,128]{2,1,0:T(8,128)(2,1)} %bitcast.176), calls=%async_computation.7 | async-start | bytes 131072 | tf_op jit(solution)/shard_map/all_to_all | solution.py:143
  213.2 1.9 copy.314
  215.9 5.6 %all-to-all-done.7 = bf16[8,32,128]{2,1,0:T(8,128)(2,1)S(1)} async-done(((bf16[8,32,128]{2,1,0:T(8,128)(2,1)}), bf16[8,32,128]{2,1,0:T(8,128)(2,1)S(1)}, u32[]{:S(2)}, u32[]{:S(2)}) %all-to-all-start.7) | async-done | bytes 65568 | tf_op jit(solution)/shard_map/all_to_all | solution.py:143
  221.5 3.4 %all-to-all-start.6 = ((bf16[8,32,128]{2,1,0:T(8,128)(2,1)}), bf16[8,32,128]{2,1,0:T(8,128)(2,1)S(1)}, u32[]{:S(2)}, u32[]{:S(2)}) async-start(bf16[8,32,128]{2,1,0:T(8,128)(2,1)} %bitcast.174), calls=%async_computation.6 | async-start | bytes 131072 | tf_op jit(solution)/shard_map/all_to_all | solution.py:142
  225.5 7.7 %all-to-all-done.6 = bf16[8,32,128]{2,1,0:T(8,128)(2,1)S(1)} async-done(((bf16[8,32,128]{2,1,0:T(8,128)(2,1)}), bf16[8,32,128]{2,1,0:T(8,128)(2,1)S(1)}, u32[]{:S(2)}, u32[]{:S(2)}) %all-to-all-start.6) | async-done | bytes 65568 | tf_op jit(solution)/shard_map/all_to_all | solution.py:142
  (165 shorter events, 32.6 us)
Async XLA Ops:
  0.6 19.1 %copy-start = (bf16[32,1024]{1,0:T(8,128)(2,1)S(1)}, bf16[32,1024]{1,0:T(8,128)(2,1)}, u32[]{:S(2)}) copy-start(bf16[32,1024]{1,0:T(8,128)(2,1)} %param.6) | copy-start | bytes 196612
  0.6 54.7 %copy-start.23 = (bf16[32,8192]{1,0:T(8,128)(2,1)S(1)}, bf16[32,8192]{1,0:T(8,128)(2,1)}, u32[]{:S(2)}) copy-start(bf16[32,8192]{1,0:T(8,128)(2,1)} %param.8) | copy-start | bytes 1572868
  1.4 51.1 %collective-permute-start = (bf16[256]{0:T(256)(128)(2,1)S(1)}, bf16[256]{0:T(256)(128)(2,1)S(1)}, u32[]{:S(2)}, u32[]{:S(2)}) collective-permute-start(bf16[256]{0:T(256)(128)(2,1)S(1)} %get-tuple-element.11), channel_id=1, source_target_pairs={{0,8},{8,16},{16,24},{24,32},{32,40},{40,48},{48,56},{56,64},{64,7... | collective-permute-start | bytes 1544 | tf_op jit(solution)/shard_map/ppermute | solution.py:14
  3.3 52.9 %collective-permute-start.4 = (bf16[256]{0:T(256)(128)(2,1)S(1)}, bf16[256]{0:T(256)(128)(2,1)S(1)}, u32[]{:S(2)}, u32[]{:S(2)}) collective-permute-start(bf16[256]{0:T(256)(128)(2,1)S(1)} %get-tuple-element.11), channel_id=1, source_target_pairs={{0,24},{8,32},{16,40},{24,48},{32,56},{40,64},{48,72},{56,80},{64,... | collective-permute-start | bytes 1544 | tf_op jit(solution)/shard_map/ppermute | solution.py:14
  8.1 48.1 %collective-permute-start.6 = (bf16[256]{0:T(256)(128)(2,1)S(1)}, bf16[256]{0:T(256)(128)(2,1)S(1)}, u32[]{:S(2)}, u32[]{:S(2)}) collective-permute-start(bf16[256]{0:T(256)(128)(2,1)S(1)} %get-tuple-element.11), channel_id=1, source_target_pairs={{0,32},{8,40},{16,48},{24,56},{32,64},{40,72},{48,80},{56,88},{64,... | collective-permute-start | bytes 1544 | tf_op jit(solution)/shard_map/ppermute | solution.py:14
  12.5 43.8 %collective-permute-start.8 = (bf16[256]{0:T(256)(128)(2,1)S(1)}, bf16[256]{0:T(256)(128)(2,1)S(1)}, u32[]{:S(2)}, u32[]{:S(2)}) collective-permute-start(bf16[256]{0:T(256)(128)(2,1)S(1)} %get-tuple-element.11), channel_id=1, source_target_pairs={{0,40},{8,48},{16,56},{24,64},{32,72},{40,80},{48,88},{56,96},{64,... | collective-permute-start | bytes 1544 | tf_op jit(solution)/shard_map/ppermute | solution.py:14
  16.2 40.1 %collective-permute-start.10 = (bf16[256]{0:T(256)(128)(2,1)S(1)}, bf16[256]{0:T(256)(128)(2,1)S(1)}, u32[]{:S(2)}, u32[]{:S(2)}) collective-permute-start(bf16[256]{0:T(256)(128)(2,1)S(1)} %get-tuple-element.11), channel_id=1, source_target_pairs={{0,48},{8,56},{16,64},{24,72},{32,80},{40,88},{48,96},{56,104},{64... | collective-permute-start | bytes 1544 | tf_op jit(solution)/shard_map/ppermute | solution.py:14
  20.4 16.8 %all-to-all-start = ((bf16[32,8,128]{2,0,1:T(8,128)(2,1)}), bf16[32,8,128]{2,0,1:T(8,128)(2,1)S(1)}, u32[]{:S(2)}, u32[]{:S(2)}) async-start(bf16[32,8,128]{2,0,1:T(8,128)(2,1)} %copy_bitcast_fusion.5), calls=%async_computation | async-start | bytes 131072 | tf_op jit(solution)/shard_map/all_to_all | solution.py:21
  37.3 44.7 %copy-start.17 = (bf16[32,8,128]{2,0,1:T(8,128)(2,1)}, bf16[32,8,128]{2,0,1:T(8,128)(2,1)S(1)}, u32[]{:S(2)}) copy-start(bf16[32,8,128]{2,0,1:T(8,128)(2,1)S(1)} %all-to-all-done) | copy-start | bytes 196612
  37.3 11.7 %all-to-all-start.2 = ((bf16[32,8,128]{2,0,1:T(8,128)(2,1)}), bf16[32,8,128]{2,0,1:T(8,128)(2,1)S(1)}, u32[]{:S(2)}, u32[]{:S(2)}) async-start(bf16[32,8,128]{2,0,1:T(8,128)(2,1)} %copy_bitcast_fusion.4), calls=%async_computation.2 | async-start | bytes 131072 | tf_op jit(solution)/shard_map/all_to_all | solution.py:22
  48.9 25.8 %copy-start.19 = (bf16[32,8,128]{2,0,1:T(8,128)(2,1)}, bf16[32,8,128]{2,0,1:T(8,128)(2,1)S(1)}, u32[]{:S(2)}) copy-start(bf16[32,8,128]{2,0,1:T(8,128)(2,1)S(1)} %all-to-all-done.2) | copy-start | bytes 196612
  48.9 25.8 %all-to-all-start.1 = ((bf16[32,8,1024]{2,0,1:T(8,128)(2,1)}), bf16[32,8,1024]{2,0,1:T(8,128)(2,1)S(1)}, u32[]{:S(2)}, u32[]{:S(2)}) async-start(bf16[32,8,1024]{2,0,1:T(8,128)(2,1)} %bitcast.517), calls=%async_computation.1 | async-start | bytes 1048576 | tf_op jit(solution)/shard_map/all_to_all | solution.py:19
  52.5 7.6 %collective-permute-start.2 = (bf16[256]{0:T(256)(128)(2,1)S(1)}, bf16[256]{0:T(256)(128)(2,1)S(1)}, u32[]{:S(2)}, u32[]{:S(2)}) collective-permute-start(bf16[256]{0:T(256)(128)(2,1)S(1)} %get-tuple-element.11), channel_id=1, source_target_pairs={{0,16},{8,24},{16,32},{24,40},{32,48},{40,56},{48,64},{56,72},{64,... | collective-permute-start | bytes 1544 | tf_op jit(solution)/shard_map/ppermute | solution.py:14
  61.2 22.6 %copy-start.14 = (pred[256,256]{0,1:T(8,128)(4,1)}, pred[256,256]{0,1:T(8,128)(4,1)S(1)}, u32[]{:S(2)}) copy-start(pred[256,256]{0,1:T(8,128)(4,1)S(1)} %get-tuple-element.19) | copy-start | bytes 196612
  61.2 24.7 %copy-start.12 = (pred[256,256]{0,1:T(8,128)(4,1)}, pred[256,256]{0,1:T(8,128)(4,1)S(1)}, u32[]{:S(2)}) copy-start(pred[256,256]{0,1:T(8,128)(4,1)S(1)} %get-tuple-element.18) | copy-start | bytes 196612
  61.9 21.9 %collective-permute-start.11 = (bf16[2,256,128]{2,1,0:T(8,128)(2,1)}, bf16[2,256,128]{2,1,0:T(8,128)(2,1)S(1)}, u32[]{:S(2)}, u32[]{:S(2)}) collective-permute-start(bf16[2,256,128]{2,1,0:T(8,128)(2,1)} %pad_maximum_fusion.1), channel_id=1, source_target_pairs={{0,48},{8,56},{16,64},{24,72},{32,80},{40,88},{48,96},{56,104},{64... | collective-permute-start | bytes 393224 | tf_op jit(solution)/shard_map/ppermute | solution.py:14
  63.8 24.0 %collective-permute-start.9 = (bf16[2,256,128]{2,1,0:T(8,128)(2,1)}, bf16[2,256,128]{2,1,0:T(8,128)(2,1)S(1)}, u32[]{:S(2)}, u32[]{:S(2)}) collective-permute-start(bf16[2,256,128]{2,1,0:T(8,128)(2,1)} %pad_maximum_fusion.1), channel_id=1, source_target_pairs={{0,40},{8,48},{16,56},{24,64},{32,72},{40,80},{48,88},{56,96},{64,... | collective-permute-start | bytes 393224 | tf_op jit(solution)/shard_map/ppermute | solution.py:14
  65.7 24.5 %collective-permute-start.7 = (bf16[2,256,128]{2,1,0:T(8,128)(2,1)}, bf16[2,256,128]{2,1,0:T(8,128)(2,1)S(1)}, u32[]{:S(2)}, u32[]{:S(2)}) collective-permute-start(bf16[2,256,128]{2,1,0:T(8,128)(2,1)} %pad_maximum_fusion.1), channel_id=1, source_target_pairs={{0,32},{8,40},{16,48},{24,56},{32,64},{40,72},{48,80},{56,88},{64,... | collective-permute-start | bytes 393224 | tf_op jit(solution)/shard_map/ppermute | solution.py:14
  67.6 24.9 %collective-permute-start.5 = (bf16[2,256,128]{2,1,0:T(8,128)(2,1)}, bf16[2,256,128]{2,1,0:T(8,128)(2,1)S(1)}, u32[]{:S(2)}, u32[]{:S(2)}) collective-permute-start(bf16[2,256,128]{2,1,0:T(8,128)(2,1)} %pad_maximum_fusion.1), channel_id=1, source_target_pairs={{0,24},{8,32},{16,40},{24,48},{32,56},{40,64},{48,72},{56,80},{64,... | collective-permute-start | bytes 393224 | tf_op jit(solution)/shard_map/ppermute | solution.py:14
  70.9 30.4 %collective-permute-start.1 = (bf16[2,256,128]{2,1,0:T(8,128)(2,1)}, bf16[2,256,128]{2,1,0:T(8,128)(2,1)S(1)}, u32[]{:S(2)}, u32[]{:S(2)}) collective-permute-start(bf16[2,256,128]{2,1,0:T(8,128)(2,1)} %pad_maximum_fusion.1), channel_id=1, source_target_pairs={{0,8},{8,16},{16,24},{24,32},{32,40},{40,48},{48,56},{56,64},{64,7... | collective-permute-start | bytes 393224 | tf_op jit(solution)/shard_map/ppermute | solution.py:14
  74.7 24.8 %all-to-all-start.4 = ((bf16[32,8,1024]{2,0,1:T(8,128)(2,1)}), bf16[32,8,1024]{2,0,1:T(8,128)(2,1)S(1)}, u32[]{:S(2)}, u32[]{:S(2)}) async-start(bf16[32,8,1024]{2,0,1:T(8,128)(2,1)} %bitcast.516), calls=%async_computation.4 | async-start | bytes 1048576 | tf_op jit(solution)/shard_map/all_to_all | solution.py:20
  83.8 6.4 %copy-start.24 = (bf16[2,256,128]{2,1,0:T(8,128)(2,1)}, bf16[2,256,128]{2,1,0:T(8,128)(2,1)S(1)}, u32[]{:S(2)}) copy-start(bf16[2,256,128]{2,1,0:T(8,128)(2,1)S(1)} %collective-permute-done.11) | copy-start | bytes 393220
  83.8 19.9 %collective-permute-start.3 = (bf16[2,256,128]{2,1,0:T(8,128)(2,1)}, bf16[2,256,128]{2,1,0:T(8,128)(2,1)}, u32[]{:S(2)}, u32[]{:S(2)}) collective-permute-start(bf16[2,256,128]{2,1,0:T(8,128)(2,1)} %pad_maximum_fusion.1), channel_id=1, source_target_pairs={{0,16},{8,24},{16,32},{24,40},{32,48},{40,56},{48,64},{56,72},{64,... | collective-permute-start | bytes 393224 | tf_op jit(solution)/shard_map/ppermute | solution.py:14
  87.8 4.8 %copy-start.26 = (bf16[2,256,128]{2,1,0:T(8,128)(2,1)}, bf16[2,256,128]{2,1,0:T(8,128)(2,1)S(1)}, u32[]{:S(2)}) copy-start(bf16[2,256,128]{2,1,0:T(8,128)(2,1)S(1)} %collective-permute-done.9) | copy-start | bytes 393220
  90.2 4.8 %copy-start.28 = (bf16[2,256,128]{2,1,0:T(8,128)(2,1)}, bf16[2,256,128]{2,1,0:T(8,128)(2,1)S(1)}, u32[]{:S(2)}) copy-start(bf16[2,256,128]{2,1,0:T(8,128)(2,1)S(1)} %collective-permute-done.7) | copy-start | bytes 393220
  92.6 7.1 %copy-start.30 = (bf16[2,256,128]{2,1,0:T(8,128)(2,1)}, bf16[2,256,128]{2,1,0:T(8,128)(2,1)S(1)}, u32[]{:S(2)}) copy-start(bf16[2,256,128]{2,1,0:T(8,128)(2,1)S(1)} %collective-permute-done.5) | copy-start | bytes 393220
  101.2 2.1 copy-start.1
  101.2 2.1 copy-start.15
  103.3 1.8 copy-start.37
  103.3 1.8 copy-start.38
  103.4 1.8 copy-start.39
  105.1 27.6 %copy-start.6 = (f32[1,8,256,256]{2,3,1,0:T(8,128)}, f32[1,8,256,256]{2,3,1,0:T(8,128)S(1)}, u32[]{:S(2)}) copy-start(f32[1,8,256,256]{2,3,1,0:T(8,128)S(1)} %get-tuple-element.30) | copy-start | bytes 6291460
  105.1 2.3 copy-start.2
  105.1 2.9 %copy-start.4 = (f32[1,8,256,256]{2,3,1,0:T(8,128)S(1)}, f32[1,8,256,256]{2,3,1,0:T(8,128)}, u32[]{:S(2)}) copy-start(f32[1,8,256,256]{2,3,1,0:T(8,128)} %get-tuple-element.26) | copy-start | bytes 6291460
  108.1 1.6 copy-start.8
  108.1 2.2 copy-start.9
  108.1 2.2 copy-start.13
  112.2 1.4 copy-start.31
  113.6 0.9 copy-start.29
  114.5 0.9 copy-start.27
  115.4 0.9 copy-start.25
  116.3 1.2 copy-start.10
  116.3 1.2 copy-start.22
  119.1 1.8 copy-start.18
  123.5 30.7 %collective-permute-start.12 = (f32[2,256,128]{2,1,0:T(8,128)}, f32[2,256,128]{2,1,0:T(8,128)}, u32[]{:S(2)}, u32[]{:S(2)}) collective-permute-start(f32[2,256,128]{2,1,0:T(8,128)} %pad_maximum_fusion), channel_id=1, source_target_pairs={{8,0},{16,8},{24,16},{32,24},{40,32},{48,40},{56,48},{64,56},{72,6... | collective-permute-start | bytes 786440 | tf_op jit(solution)/shard_map/ppermute | solution.py:14
  141.4 7.4 %copy-start.11 = (bf16[256,1,8,128]{0,3,2,1:T(8,128)(2,1)S(1)}, bf16[256,1,8,128]{0,3,2,1:T(8,128)(2,1)}, u32[]{:S(2)}) copy-start(bf16[256,1,8,128]{0,3,2,1:T(8,128)(2,1)} %get-tuple-element.36) | copy-start | bytes 1572868
  144.6 44.6 %all-to-all-start.5 = ((bf16[8,32,1024]{2,1,0:T(8,128)(2,1)}), bf16[8,32,1024]{2,1,0:T(8,128)(2,1)}, u32[]{:S(2)}, u32[]{:S(2)}) async-start(bf16[8,32,1024]{2,1,0:T(8,128)(2,1)} %all_to_all.120), calls=%async_computation.5 | async-start | bytes 1048576 | tf_op jit(solution)/shard_map/all_to_all | solution.py:141
  149.8 4.4 %copy-start.36 = (f32[1,256,128]{2,1,0:T(8,128)S(1)}, f32[1,256,128]{2,1,0:T(8,128)}, u32[]{:S(2)}) copy-start(f32[1,256,128]{2,1,0:T(8,128)} %fusion.55) | copy-start | bytes 393220
  151.9 5.9 %copy-start.5 = (f32[1,8,256,256]{2,3,1,0:T(8,128)S(1)}, f32[1,8,256,256]{2,3,1,0:T(8,128)}, u32[]{:S(2)}) copy-start(f32[1,8,256,256]{2,3,1,0:T(8,128)} %get-tuple-element.26) | copy-start | bytes 6291460
  154.1 7.5 %copy-start.35 = (f32[1,256,128]{2,1,0:T(8,128)S(1)}, f32[1,256,128]{2,1,0:T(8,128)}, u32[]{:S(2)}) copy-start(f32[1,256,128]{2,1,0:T(8,128)} %fusion.53) | copy-start | bytes 393220
  155.2 13.2 %copy-start.3 = (f32[1,8,256,256]{2,3,1,0:T(8,128)S(1)}, f32[1,8,256,256]{2,3,1,0:T(8,128)}, u32[]{:S(2)}) copy-start(f32[1,8,256,256]{2,3,1,0:T(8,128)} %get-tuple-element.28) | copy-start | bytes 6291460
  155.2 6.5 %collective-permute-start.13 = (f32[2,256,128]{2,1,0:T(8,128)S(1)}, f32[2,256,128]{2,1,0:T(8,128)S(1)}, u32[]{:S(2)}, u32[]{:S(2)}) collective-permute-start(f32[2,256,128]{2,1,0:T(8,128)S(1)} %maximum_add_fusion), channel_id=1, source_target_pairs={{8,0},{16,8},{24,16},{32,24},{40,32},{48,40},{56,48},{64,56},{72,6... | collective-permute-start | bytes 786440 | tf_op jit(solution)/shard_map/ppermute | solution.py:14
  158.3 13.7 %copy-start.34 = (f32[1,256,128]{2,1,0:T(8,128)S(1)}, f32[1,256,128]{2,1,0:T(8,128)}, u32[]{:S(2)}) copy-start(f32[1,256,128]{2,1,0:T(8,128)} %fusion.51) | copy-start | bytes 393220
  161.7 16.3 %copy-start.7 = (f32[1,8,256,256]{2,3,1,0:T(8,128)S(1)}, f32[1,8,256,256]{2,3,1,0:T(8,128)}, u32[]{:S(2)}) copy-start(f32[1,8,256,256]{2,3,1,0:T(8,128)} %copy-done.6) | copy-start | bytes 6291460
  161.7 10.3 %collective-permute-start.14 = (f32[2,256,128]{2,1,0:T(8,128)S(1)}, f32[2,256,128]{2,1,0:T(8,128)S(1)}, u32[]{:S(2)}, u32[]{:S(2)}) collective-permute-start(f32[2,256,128]{2,1,0:T(8,128)S(1)} %maximum_add_fusion.1), channel_id=1, source_target_pairs={{8,0},{16,8},{24,16},{32,24},{40,32},{48,40},{56,48},{64,56},{72,6... | collective-permute-start | bytes 786440 | tf_op jit(solution)/shard_map/ppermute | solution.py:14
  168.9 12.9 %copy-start.33 = (f32[1,256,128]{2,1,0:T(8,128)S(1)}, f32[1,256,128]{2,1,0:T(8,128)}, u32[]{:S(2)}) copy-start(f32[1,256,128]{2,1,0:T(8,128)} %fusion.49) | copy-start | bytes 393220
  172.1 9.8 %collective-permute-start.15 = (f32[2,256,128]{2,1,0:T(8,128)S(1)}, f32[2,256,128]{2,1,0:T(8,128)S(1)}, u32[]{:S(2)}, u32[]{:S(2)}) collective-permute-start(f32[2,256,128]{2,1,0:T(8,128)S(1)} %maximum_add_fusion.2), channel_id=1, source_target_pairs={{8,0},{16,8},{24,16},{32,24},{40,32},{48,40},{56,48},{64,56},{72,6... | collective-permute-start | bytes 786440 | tf_op jit(solution)/shard_map/ppermute | solution.py:14
  181.9 16.9 %copy-start.16 = (pred[256,256]{0,1:T(8,128)(4,1)S(1)}, pred[256,256]{0,1:T(8,128)(4,1)}, u32[]{:S(2)}) copy-start(pred[256,256]{0,1:T(8,128)(4,1)} %copy-done.14) | copy-start | bytes 196612
  181.9 13.8 %collective-permute-start.16 = (f32[2,256,128]{2,1,0:T(8,128)S(1)}, f32[2,256,128]{2,1,0:T(8,128)S(1)}, u32[]{:S(2)}, u32[]{:S(2)}) collective-permute-start(f32[2,256,128]{2,1,0:T(8,128)S(1)} %maximum_add_fusion.3), channel_id=1, source_target_pairs={{8,0},{16,8},{24,16},{32,24},{40,32},{48,40},{56,48},{64,56},{72,6... | collective-permute-start | bytes 786440 | tf_op jit(solution)/shard_map/ppermute | solution.py:14
  189.1 20.7 %all-to-all-start.3 = ((bf16[8,32,1024]{2,1,0:T(8,128)(2,1)}), bf16[8,32,1024]{2,1,0:T(8,128)(2,1)S(1)}, u32[]{:S(2)}, u32[]{:S(2)}) async-start(bf16[8,32,1024]{2,1,0:T(8,128)(2,1)} %all_to_all.113), calls=%async_computation.3 | async-start | bytes 1048576 | tf_op jit(solution)/shard_map/all_to_all | solution.py:95
  195.7 7.0 %copy-start.32 = (f32[1,256,128]{2,1,0:T(8,128)S(1)}, f32[1,256,128]{2,1,0:T(8,128)}, u32[]{:S(2)}) copy-start(f32[1,256,128]{2,1,0:T(8,128)} %fusion.45) | copy-start | bytes 393220
  196.7 5.9 %collective-permute-start.17 = (f32[2,256,128]{2,1,0:T(8,128)S(1)}, f32[2,256,128]{2,1,0:T(8,128)S(1)}, u32[]{:S(2)}, u32[]{:S(2)}) collective-permute-start(f32[2,256,128]{2,1,0:T(8,128)S(1)} %maximum_add_fusion.4), channel_id=1, source_target_pairs={{8,0},{16,8},{24,16},{32,24},{40,32},{48,40},{56,48},{64,56},{72,6... | collective-permute-start | bytes 786440 | tf_op jit(solution)/shard_map/ppermute | solution.py:14
  209.8 11.7 %all-to-all-start.7 = ((bf16[8,32,128]{2,1,0:T(8,128)(2,1)}), bf16[8,32,128]{2,1,0:T(8,128)(2,1)S(1)}, u32[]{:S(2)}, u32[]{:S(2)}) async-start(bf16[8,32,128]{2,1,0:T(8,128)(2,1)} %bitcast.176), calls=%async_computation.7 | async-start | bytes 131072 | tf_op jit(solution)/shard_map/all_to_all | solution.py:143
  221.5 11.7 %all-to-all-start.6 = ((bf16[8,32,128]{2,1,0:T(8,128)(2,1)}), bf16[8,32,128]{2,1,0:T(8,128)(2,1)S(1)}, u32[]{:S(2)}, u32[]{:S(2)}) async-start(bf16[8,32,128]{2,1,0:T(8,128)(2,1)} %bitcast.174), calls=%async_computation.6 | async-start | bytes 131072 | tf_op jit(solution)/shard_map/all_to_all | solution.py:142
  (2 other events, 1.5 us)
where the time goes:
time: 236 us; the launch traced here: 234 us
  starting transfers between devices  103 us (44%)
  waiting for transfers between devices  52.7 us (22%)
  matrix products  44.1 us (19%)
  local copies, waits for them, and re-layouts  23.8 us (10%)
  other arithmetic  8.36 us (4%)
    ppermute x18, starting transfers between devices, passed_along(): lax.ppermute(value, axis, [(source, source + steps) for source in range(l...  63.3 us
    ppermute x18, waiting for transfers between devices, passed_along(): lax.ppermute(value, axis, [(source, source + steps) for source in range(l...  15.3 us
    dot_general x7, matrix products, scores_of(): jnp.einsum('qgpd,kgd->gpqk', query_four, key_three, preferred_element_typ...  13.5 us
    all_to_all x1, starting transfers between devices, local(): lax.all_to_all(key_heads, 'head', split_axis=1, concat_axis=0, tiled=True)  8.47 us
    all_to_all x1, waiting for transfers between devices, local(): lax.all_to_all(kv_rounded[0], 'head', split_axis=0, concat_axis=1, tiled=...  7.66 us
    dot_general x7, matrix products, backward(): jnp.einsum('gpqk,qgpd->kgd', weights, grad_four, preferred_element_type=j...  7.51 us
    all_to_all x1, starting transfers between devices, local(): lax.all_to_all(out_grad, 'head', split_axis=1, concat_axis=0, tiled=True)  7.13 us
    dot_general x7, matrix products, backward(): jnp.einsum('gpqk,qgpd->kgd', score_grad, query_four, preferred_element_ty...  6.95 us
  transfers between devices with their start and end apart: 26, of which 11 were waited for; matrix products, arithmetic and copies ran while one was open for 22% of the time, Pallas kernels for 0%

commit v1 on v0

v1 whole, which is shorter than its diff:
```python
import functools
import math

import jax
import jax.numpy as jnp
from jax import lax
from jax.experimental import pallas as pl
from jax.experimental.pallas import tpu as pltpu
from jax.sharding import PartitionSpec as P


HEAD = 128
WINDOW = 1536
BLOCK = 256
SLOTS = 4
OFFSETS = (0, 2, 4, 6, 1, 3, 5)
CHUNKS = len(OFFSETS)
DOC_ROWS = 16
SCALE = HEAD ** (-0.5)
EXP2_SCALE = SCALE * math.log2(math.e)
MASKED = -1e30
NT = (((1,), (1,)), ((), ()))
VMEM = pl.BlockSpec(memory_space=pltpu.VMEM)


def dot(a, b, dims=(((1,), (0,)), ((), ()))):
    return lax.dot_general(a, b, dims, preferred_element_type=jnp.float32)


def pack_body(width, parts, a_ref, b_ref, o_ref):
    per = width // HEAD // parts
    for part in range(parts):
        for h in range(per):
            source = slice((part * per + h) * HEAD, (part * per + h + 1) * HEAD)
            o_ref[part, :, 2 * h * HEAD : (2 * h + 1) * HEAD] = a_ref[:, source]
            o_ref[part, :, (2 * h + 1) * HEAD : (2 * h + 2) * HEAD] = b_ref[:, source]


def pack(a, b, parts):
    rows, width = a.shape
    return pl.pallas_call(
        functools.partial(pack_body, width, parts),
        out_shape=jax.ShapeDtypeStruct((parts, rows, 2 * width // parts), a.dtype),
        in_specs=[VMEM, VMEM],
        out_specs=VMEM,
        compiler_params=pltpu.CompilerParams(vmem_limit_bytes=8 * 1024 * 1024),
        cost_estimate=pl.CostEstimate(flops=rows * width, bytes_accessed=8 * rows * width, transcendentals=0),
    )(a, b)


def unpack_body(width, parts, i_ref, a_ref, b_ref):
    per = width // HEAD // parts
    for part in range(parts):
        for h in range(per):
            target = slice((part * per + h) * HEAD, (part * per + h + 1) * HEAD)
            a_ref[:, target] = i_ref[part, :, 2 * h * HEAD : (2 * h + 1) * HEAD]
            b_ref[:, target] = i_ref[part, :, (2 * h + 1) * HEAD : (2 * h + 2) * HEAD]


def unpack(both):
    parts, rows, columns = both.shape
    width = parts * columns // 2
    out = jax.ShapeDtypeStruct((rows, width), both.dtype)
    return pl.pallas_call(
        functools.partial(unpack_body, width, parts),
        out_shape=(out, out),
        in_specs=[VMEM],
        out_specs=(VMEM, VMEM),
        compiler_params=pltpu.CompilerParams(vmem_limit_bytes=8 * 1024 * 1024),
        cost_estimate=pl.CostEstimate(flops=rows * width, bytes_accessed=8 * rows * width, transcendentals=0),
    )(both)


def prepare(core, own, two, four, six, mate, k_s, v_s, kt_s, vt_s, bias_s, dk_s, dv_s):
    first = 1 - core
    docs = []
    for c in range(CHUNKS):
        if c < SLOTS:
            ref = (own, two, four, six)[c]
            rows, doc = ref[:BLOCK, :], ref[BLOCK:, :]
        else:
            slot = first + (c - SLOTS)
            rows, doc = mate[slot, :BLOCK, :], mate[slot, BLOCK:, :]
        docs.append(doc[0:1, :].astype(jnp.float32))
        key, value = rows[:, :HEAD], rows[:, HEAD:]
        k_s[c] = key
        v_s[c] = value
        kt_s[c] = key.astype(jnp.float32).T.astype(jnp.bfloat16)
        vt_s[c] = value.astype(jnp.float32).T.astype(jnp.bfloat16)
    mine = docs[0]
    by_key = jnp.broadcast_to(mine, (BLOCK, BLOCK)).T
    row = lax.broadcasted_iota(jnp.int32, (BLOCK, BLOCK), 0)
    lane = lax.broadcasted_iota(jnp.int32, (BLOCK, BLOCK), 1)
    before = jnp.sum(jnp.where((by_key == mine) & (row < lane), 1.0, 0.0), axis=0, keepdims=True)
    opening = mine[:, 0:1]
    carried = jnp.zeros((1, 1), jnp.float32)
    for c in range(1, CHUNKS):
        carried = carried + jnp.sum(jnp.where(docs[c] == opening, 1.0, 0.0), axis=1, keepdims=True)
    before = before + jnp.where(mine == opening, carried, 0.0)
    before = jnp.minimum(before, WINDOW - 1.0).astype(jnp.int32)
    for c in range(CHUNKS):
        back = lane - row + OFFSETS[c] * BLOCK
        bias_s[c] = jnp.where((back >= 0) & (back <= before), 0.0, MASKED)
    dk_s[...] = jnp.zeros_like(dk_s)
    dv_s[...] = jnp.zeros_like(dv_s)


def attention_body(core_ref, x_ref, own, two, four, six, mate, y_ref, mine_ref, mate_ref, k_s, v_s, kt_s, vt_s, bias_s, s_s, dk_s, dv_s):
    head = pl.program_id(0)
    core = core_ref[0]

    @pl.when(head == 0)
    def _():
        prepare(core, own, two, four, six, mate, k_s, v_s, kt_s, vt_s, bias_s, dk_s, dv_s)

    query, grad = x_ref[:, :HEAD], x_ref[:, HEAD:]
    top = None
    for c in range(CHUNKS):
        s = dot(k_s[c], query, NT) + bias_s[c]
        s_s[c] = s
        most = jnp.max(s, axis=0, keepdims=True)
        top = most if top is None else jnp.maximum(top, most)
    total = None
    for c in range(CHUNKS):
        p = jnp.exp2((s_s[c] - top) * EXP2_SCALE)
        s_s[c] = p
        part = jnp.sum(p, axis=0, keepdims=True)
        total = part if total is None else total + part
    inverse = 1.0 / total
    out = None
    for c in range(CHUNKS):
        p16 = (s_s[c] * inverse).astype(jnp.bfloat16)
        term = dot(vt_s[c], p16)
        out = term if out is None else out + term
        dv_s[c] += dot(p16, grad)
    out16 = out.astype(jnp.bfloat16).astype(jnp.float32)
    y_ref[:, :HEAD] = out16.T.astype(jnp.bfloat16)
    delta = jnp.sum(grad.astype(jnp.float32).T * out16, axis=0, keepdims=True)
    dq = None
    for c in range(CHUNKS):
        dp = dot(v_s[c], grad, NT)
        ds = (s_s[c] * ((dp - delta) * inverse)).astype(jnp.bfloat16)
        term = dot(kt_s[c], ds)
        dq = term if dq is None else dq + term
        dk_s[c] += dot(ds, query)
    y_ref[:, HEAD:] = (dq * SCALE).T.astype(jnp.bfloat16)

    @pl.when(head == pl.num_programs(0) - 1)
    def _():
        for t in range(SLOTS):
            mine_ref[t, :, :HEAD] = dk_s[t] * SCALE
            mine_ref[t, :, HEAD:] = dv_s[t]
        first = 1 - core
        mate_ref[3 - 3 * first] = jnp.zeros((BLOCK, 2 * HEAD), jnp.bfloat16)
        for t in range(SLOTS - 1):
            mate_ref[first + t, :, :HEAD] = (dk_s[SLOTS + t] * SCALE).astype(jnp.bfloat16)
            mate_ref[first + t, :, HEAD:] = dv_s[SLOTS + t].astype(jnp.bfloat16)


def attention(core, x, own, two, four, six, mate):
    heads = x.shape[1] // (2 * HEAD)
    flops = heads * 6 * 2 * CHUNKS * BLOCK * BLOCK * HEAD
    whole = lambda shape: pl.BlockSpec(shape, lambda h, _: (0,) * len(shape))
    block = whole((BLOCK + DOC_ROWS, 2 * HEAD))
    return pl.pallas_call(
        attention_body,
        out_shape=(
            jax.ShapeDtypeStruct(x.shape, jnp.bfloat16),
            jax.ShapeDtypeStruct((SLOTS, BLOCK, 2 * HEAD), jnp.float32),
            jax.ShapeDtypeStruct((SLOTS, BLOCK, 2 * HEAD), jnp.bfloat16),
        ),
        grid_spec=pltpu.PrefetchScalarGridSpec(
            num_scalar_prefetch=1,
            grid=(heads,),
            in_specs=[
                pl.BlockSpec((BLOCK, 2 * HEAD), lambda h, _: (0, h)),
                block,
                block,
                block,
                block,
                whole((SLOTS, BLOCK + DOC_ROWS, 2 * HEAD)),
            ],
            out_specs=(
                pl.BlockSpec((BLOCK, 2 * HEAD), lambda h, _: (0, h)),
                whole((SLOTS, BLOCK, 2 * HEAD)),
                whole((SLOTS, BLOCK, 2 * HEAD)),
            ),
            scratch_shapes=[
                pltpu.VMEM((CHUNKS, BLOCK, HEAD), jnp.bfloat16),
                pltpu.VMEM((CHUNKS, BLOCK, HEAD), jnp.bfloat16),
                pltpu.VMEM((CHUNKS, HEAD, BLOCK), jnp.bfloat16),
                pltpu.VMEM((CHUNKS, HEAD, BLOCK), jnp.bfloat16),
                pltpu.VMEM((CHUNKS, BLOCK, BLOCK), jnp.float32),
                pltpu.VMEM((CHUNKS, BLOCK, BLOCK), jnp.float32),
                pltpu.VMEM((CHUNKS, BLOCK, HEAD), jnp.float32),
                pltpu.VMEM((CHUNKS, BLOCK, HEAD), jnp.float32),
            ],
        ),
        compiler_params=pltpu.CompilerParams(dimension_semantics=("arbitrary",), vmem_limit_bytes=20 * 1024 * 1024),
        cost_estimate=pl.CostEstimate(flops=flops, bytes_accessed=5 * 1024 * 1024, transcendentals=heads * CHUNKS * BLOCK * BLOCK),
        name="attention",
    )(core, x, own, two, four, six, mate)


def shift(value, steps):
    count = lax.axis_size("ctx")
    return lax.ppermute(value, "ctx", [(s, s + steps) for s in range(max(0, -steps), min(count, count - steps))])


def swap(value):
    count = lax.axis_size("ctx")
    return lax.ppermute(value, "ctx", [(s, s ^ 1) for s in range(count)])


def over_head(value):
    return lax.all_to_all(value, "head", split_axis=0, concat_axis=0, tiled=True)


def local(queries, key_heads, value_head_array, out_grad, doc_ids):
    parts = lax.axis_size("head")
    core = (lax.axis_index("ctx") % 2).astype(jnp.int32).reshape(1)
    kv = over_head(pack(key_heads, value_head_array, parts))
    kv = kv.reshape(BLOCK, 2 * HEAD)
    docs = jnp.pad((doc_ids + 1).astype(jnp.bfloat16)[None, :], ((0, DOC_ROWS - 1), (0, 0)))
    own = jnp.concatenate([kv, docs], axis=0)
    packed = pack(queries, out_grad, parts)
    x = over_head(packed).reshape(BLOCK, -1)
    two, four, six = (shift(own, steps) for steps in (2, 4, 6))
    mate = swap(jnp.stack([own, two, four, six]))
    y, mine, sent = attention(core, x, own, two, four, six, mate)
    y = over_head(y.reshape(parts, -1, y.shape[1]))
    sent = swap(sent)
    sums = mine + sent.astype(jnp.float32)
    rounded = sums.astype(jnp.bfloat16)
    back = [shift(rounded[t], -2 * t) for t in range(1, SLOTS)]
    grads = sums[0] + sum(b.astype(jnp.float32) for b in back)
    grads = grads.astype(jnp.bfloat16)
    grads = over_head(grads.reshape(parts, -1, 2 * HEAD))
    attended, query_grad = unpack(y)
    key_grad, value_grad = unpack(grads)
    return attended, query_grad, key_grad, value_grad


def solution(mesh):
    rows = P(("ctx", "head"), None)

    return jax.shard_map(
        local,
        mesh=mesh,
        in_specs=(rows, rows, rows, rows, P("ctx")),
        out_specs=(rows, rows, rows, rows),
        check_vma=False,
    )
```

time: 236 us -> 136 us (0.58)
  starting transfers between devices: 103 us -> 35.7 us
  matrix products: 44.1 us -> 0 us
  Pallas kernels: 0 us -> 26.3 us
  local copies, waits for them, and re-layouts: 23.8 us -> 3.79 us
  blocking collectives: 0 us -> 11.5 us
  other arithmetic: 8.36 us -> 0.34 us
  waiting for transfers between devices: 52.7 us -> 57.3 us
    dot_general x42 -> x0, matrix products: 44.1 us -> none  [the longest x7 13.5 us: scores_of(): jnp.einsum('qgpd,kgd->gpqk', query_four, key_three, preferred_element_typ...]
    ppermute x18 -> x8, starting transfers between devices: 63.3 us -> 20.1 us  [the longest x6 20 us: shift(): lax.ppermute(value, 'ctx', [(s, s + steps) for s in range(max(0, -steps),...]
    pallas_call x0 -> x5, Pallas kernels: none -> 26.3 us  [the longest x1 22.6 us: attention(): pl.pallas_call(attention_body, out_shape=(jax.ShapeDtypeStruct(x.shape, j...]
    all_to_all x8 -> x3, starting transfers between devices: 39.8 us -> 15.6 us  [over_head(): lax.all_to_all(value, 'head', split_axis=0, concat_axis=0, tiled=True)]
    all_to_all x10 -> x0, local copies, waits for them, and re-layouts: 13 us -> none  [the longest x2 3.93 us: local(): lax.all_to_all(query_rounded, 'head', split_axis=0, concat_axis=1, tiled=...]
    all_to_all x0 -> x1, blocking collectives: none -> 11.5 us  [over_head(): lax.all_to_all(value, 'head', split_axis=0, concat_axis=0, tiled=True)]
    convert_element_type x3 -> x0, local copies, waits for them, and re-layouts: 3.57 us -> none  [the longest x1 1.36 us: local(): grad_four.astype(jnp.float32) * out_rounded.astype(jnp.float32)]
    unnamed x83 -> x10, local copies, waits for them, and re-layouts: 6.62 us -> 3.75 us
  transfers between devices with their start and end apart: 26 -> 11, of which waited for: 11 -> 8; matrix products, arithmetic and copies ran while one was open for 22% -> 0% of each run, Pallas kernels for 0% -> 1%
where the time goes in v1:
time: 136 us
  waiting for transfers between devices  57.3 us (42%)
  starting transfers between devices  35.7 us (26%)
  Pallas kernels  26.3 us (19%)
  blocking collectives  11.5 us (8%)
  local copies, waits for them, and re-layouts  3.79 us (3%)
    all_to_all x3, waiting for transfers between devices, over_head(): lax.all_to_all(value, 'head', split_axis=0, concat_axis=0, tiled=True)  40 us
    pallas_call x1, Pallas kernels, attention(): pl.pallas_call(attention_body, out_shape=(jax.ShapeDtypeStruct(x.shape, j...  22.6 us
    ppermute x6, starting transfers between devices, shift(): lax.ppermute(value, 'ctx', [(s, s + steps) for s in range(max(0, -steps),...  20 us
    all_to_all x3, starting transfers between devices, over_head(): lax.all_to_all(value, 'head', split_axis=0, concat_axis=0, tiled=True)  15.6 us
    ppermute x6, waiting for transfers between devices, shift(): lax.ppermute(value, 'ctx', [(s, s + steps) for s in range(max(0, -steps),...  13.5 us
    all_to_all x1, blocking collectives, over_head(): lax.all_to_all(value, 'head', split_axis=0, concat_axis=0, tiled=True)  11.5 us
    ppermute x2, waiting for transfers between devices, swap(): return lax.ppermute(value, 'ctx', [(s, s ^ 1) for s in range(count)])  3.84 us
    unnamed x10, local copies, waits for them, and re-layouts  3.75 us
  transfers between devices with their start and end apart: 11, of which 8 were waited for; matrix products, arithmetic and copies ran while one was open for 0% of the time, Pallas kernels for 1%

profile of v1, /device:TPU:2, one launch (start us, length us, event | category | flops | bytes accessed | tf_op | source)
XLA Modules:
  0.0 135.6 jit_solution(16750917892922964309)
XLA Ops:
  0.6 0.0 copy-start.2
  0.6 0.8 copy-done.2
  1.5 0.0 copy-start.3
  1.5 0.8 copy-done.3
  2.3 0.7 shard_map.85
  3.0 8.5 %all-to-all-start.1 = ((bf16[8,32,256]{2,1,0:T(8,128)(2,1)}), bf16[8,32,256]{2,1,0:T(8,128)(2,1)S(1)}, u32[]{:S(2)}, u32[]{:S(2)}) async-start(bf16[8,32,256]{2,1,0:T(8,128)(2,1)} %shard_map.85), calls=%async_computation.1 | async-start | bytes 262144 | tf_op jit(solution)/shard_map/all_to_all | solution.py:216
  11.5 0.0 copy-start
  11.5 1.0 copy-done
  12.5 0.0 copy-start.1
  12.5 1.0 copy-done.1
  13.5 1.2 shard_map.84
  14.7 0.0 copy-start.4
  14.7 5.8 %all-to-all-done.1 = bf16[8,32,256]{2,1,0:T(8,128)(2,1)S(1)} async-done(((bf16[8,32,256]{2,1,0:T(8,128)(2,1)}), bf16[8,32,256]{2,1,0:T(8,128)(2,1)S(1)}, u32[]{:S(2)}, u32[]{:S(2)}) %all-to-all-start.1) | async-done | bytes 131104 | tf_op jit(solution)/shard_map/all_to_all | solution.py:216
  20.6 3.6 %all-to-all-start = ((bf16[8,32,2048]{2,1,0:T(8,128)(2,1)}), bf16[8,32,2048]{2,1,0:T(8,128)(2,1)S(1)}, u32[]{:S(2)}, u32[]{:S(2)}) async-start(bf16[8,32,2048]{2,1,0:T(8,128)(2,1)} %shard_map.84), calls=%async_computation | async-start | bytes 2097152 | tf_op jit(solution)/shard_map/all_to_all | solution.py:216
  24.1 0.0 copy-done.4
  24.2 4.9 %collective-permute-start.2 = (bf16[272,256]{1,0:T(8,128)(2,1)S(1)}, bf16[272,256]{1,0:T(8,128)(2,1)S(1)}, u32[]{:S(2)}, u32[]{:S(2)}) collective-permute-start(bf16[272,256]{1,0:T(8,128)(2,1)S(1)} %get-tuple-element.24.own), channel_id=1, source_target_pairs={{0,48},{8,56},{16,64},{24,72},{32,80},{40,88},{48,96},{56,104},{64... | collective-permute-start | bytes 417800 | tf_op jit(solution)/shard_map/ppermute | solution.py:207
  29.1 3.5 %collective-permute-start.1 = (bf16[272,256]{1,0:T(8,128)(2,1)S(1)}, bf16[272,256]{1,0:T(8,128)(2,1)S(1)}, u32[]{:S(2)}, u32[]{:S(2)}) collective-permute-start(bf16[272,256]{1,0:T(8,128)(2,1)S(1)} %get-tuple-element.24.own), channel_id=1, source_target_pairs={{0,32},{8,40},{16,48},{24,56},{32,64},{40,72},{48,80},{56,88},{64,... | collective-permute-start | bytes 417800 | tf_op jit(solution)/shard_map/ppermute | solution.py:207
  32.6 2.9 %collective-permute-start = (bf16[272,256]{1,0:T(8,128)(2,1)S(1)}, bf16[272,256]{1,0:T(8,128)(2,1)S(1)}, u32[]{:S(2)}, u32[]{:S(2)}) collective-permute-start(bf16[272,256]{1,0:T(8,128)(2,1)S(1)} %get-tuple-element.24.own), channel_id=1, source_target_pairs={{0,16},{8,24},{16,32},{24,40},{32,48},{40,56},{48,64},{56,72},{64,... | collective-permute-start | bytes 417800 | tf_op jit(solution)/shard_map/ppermute | solution.py:207
  35.5 0.0 collective-permute-done.2.six
  35.5 4.0 %collective-permute-done.1.four = bf16[272,256]{1,0:T(8,128)(2,1)S(1)} collective-permute-done((bf16[272,256]{1,0:T(8,128)(2,1)S(1)}, bf16[272,256]{1,0:T(8,128)(2,1)S(1)}, u32[]{:S(2)}, u32[]{:S(2)}) %collective-permute-start.1) | collective-permute-done | bytes 139296 | tf_op jit(solution)/shard_map/ppermute | solution.py:207
  39.5 2.1 %collective-permute-done.two = bf16[272,256]{1,0:T(8,128)(2,1)S(1)} collective-permute-done((bf16[272,256]{1,0:T(8,128)(2,1)S(1)}, bf16[272,256]{1,0:T(8,128)(2,1)S(1)}, u32[]{:S(2)}, u32[]{:S(2)}) %collective-permute-start) | collective-permute-done | bytes 139296 | tf_op jit(solution)/shard_map/ppermute | solution.py:207
  41.6 0.1 pad_maximum_fusion
  41.7 0.1 collective-permute-start.3
  41.8 1.9 %collective-permute-done.3.mate = bf16[4,272,256]{2,1,0:T(8,128)(2,1)S(1)} collective-permute-done((bf16[4,272,256]{2,1,0:T(8,128)(2,1)S(1)}, bf16[4,272,256]{2,1,0:T(8,128)(2,1)S(1)}, u32[]{:S(2)}, u32[]{:S(2)}) %collective-permute-start.3) | collective-permute-done | bytes 557088 | tf_op jit(solution)/shard_map/ppermute | solution.py:212
  43.8 7.7 %all-to-all-done = bf16[8,32,2048]{2,1,0:T(8,128)(2,1)S(1)} async-done(((bf16[8,32,2048]{2,1,0:T(8,128)(2,1)}), bf16[8,32,2048]{2,1,0:T(8,128)(2,1)S(1)}, u32[]{:S(2)}, u32[]{:S(2)}) %all-to-all-start) | async-done | bytes 1048608 | tf_op jit(solution)/shard_map/all_to_all | solution.py:216
  51.4 22.6 %attention.1 = (bf16[256,2048]{1,0:T(8,128)(2,1)}, f32[4,256,256]{2,1,0:T(8,128)S(1)}, bf16[4,256,256]{2,1,0:T(8,128)(2,1)S(1)}) custom-call(s32[1]{0:T(128)} %bitcast.core_ref, bf16[256,2048]{1,0:T(8,128)(2,1)S(1)} %bitcast.22, bf16[272,256]{1,0:T(8,128)(2,1)S(1)} %get-tuple-element.24.own, bf16[272,256]{1,0:T(8,128)(2,1)S(1)} %collective-permute-done.two, ...), custom_call_target="tpu_custom_call" | custom-call | flops 5637144576 | bytes 5242880 | tf_op jit(solution)/shard_map/attention/pallas_call | solution.py:165
  74.0 0.0 collective-permute-start.4
  74.0 1.9 %collective-permute-done.4 = bf16[4,256,256]{2,1,0:T(8,128)(2,1)S(1)} collective-permute-done((bf16[4,256,256]{2,1,0:T(8,128)(2,1)S(1)}, bf16[4,256,256]{2,1,0:T(8,128)(2,1)S(1)}, u32[]{:S(2)}, u32[]{:S(2)}) %collective-permute-start.4) | collective-permute-done | bytes 524320 | tf_op jit(solution)/shard_map/ppermute | solution.py:212
  75.9 0.2 fusion.5
  76.1 4.9 %collective-permute-start.5 = (bf16[256,256]{1,0:T(8,128)(2,1)S(1)}, bf16[256,256]{1,0:T(8,128)(2,1)S(1)}, u32[]{:S(2)}, u32[]{:S(2)}) collective-permute-start(bf16[256,256]{1,0:T(8,128)(2,1)S(1)} %get-tuple-element.20), channel_id=1, source_target_pairs={{16,0},{24,8},{32,16},{40,24},{48,32},{56,40},{64,48},{72,56},{80,... | collective-permute-start | bytes 393224 | tf_op jit(solution)/shard_map/ppermute | solution.py:207
  81.0 1.9 %collective-permute-start.7 = (bf16[256,256]{1,0:T(8,128)(2,1)S(1)}, bf16[256,256]{1,0:T(8,128)(2,1)S(1)}, u32[]{:S(2)}, u32[]{:S(2)}) collective-permute-start(bf16[256,256]{1,0:T(8,128)(2,1)S(1)} %get-tuple-element.21), channel_id=1, source_target_pairs={{48,0},{56,8},{64,16},{72,24},{80,32},{88,40},{96,48},{104,56},{11... | collective-permute-start | bytes 393224 | tf_op jit(solution)/shard_map/ppermute | solution.py:207
  83.0 1.9 %collective-permute-start.6 = (bf16[256,256]{1,0:T(8,128)(2,1)S(1)}, bf16[256,256]{1,0:T(8,128)(2,1)S(1)}, u32[]{:S(2)}, u32[]{:S(2)}) collective-permute-start(bf16[256,256]{1,0:T(8,128)(2,1)S(1)} %get-tuple-element.22), channel_id=1, source_target_pairs={{32,0},{40,8},{48,16},{56,24},{64,32},{72,40},{80,48},{88,56},{96,... | collective-permute-start | bytes 393224 | tf_op jit(solution)/shard_map/ppermute | solution.py:207
  84.9 0.0 collective-permute-done.5
  84.9 7.3 %collective-permute-done.7 = bf16[256,256]{1,0:T(8,128)(2,1)S(1)} collective-permute-done((bf16[256,256]{1,0:T(8,128)(2,1)S(1)}, bf16[256,256]{1,0:T(8,128)(2,1)S(1)}, u32[]{:S(2)}, u32[]{:S(2)}) %collective-permute-start.7) | collective-permute-done | bytes 131104 | tf_op jit(solution)/shard_map/ppermute | solution.py:207
  92.2 0.0 collective-permute-done.6
  92.2 0.1 fusion.2
  92.3 11.5 %all_to_all.20.i_ref = bf16[8,32,256]{2,1,0:T(8,128)(2,1)S(1)} all-to-all(bf16[8,32,256]{2,1,0:T(8,128)(2,1)S(1)} %bitcast.27), channel_id=1, replica_groups=mesh['ctx'=32,'head'=8] {'head'}, dimensions={0} | all-to-all | bytes 262144 | tf_op jit(solution)/shard_map/all_to_all | solution.py:216
  103.8 3.6 %all-to-all-start.2 = ((bf16[8,32,2048]{2,1,0:T(8,128)(2,1)}), bf16[8,32,2048]{2,1,0:T(8,128)(2,1)S(1)}, u32[]{:S(2)}, u32[]{:S(2)}) async-start(bf16[8,32,2048]{2,1,0:T(8,128)(2,1)} %bitcast.7), calls=%async_computation.2 | async-start | bytes 2097152 | tf_op jit(solution)/shard_map/all_to_all | solution.py:216
  107.3 0.7 shard_map.87
  108.0 26.5 %all-to-all-done.2.i_ref = bf16[8,32,2048]{2,1,0:T(8,128)(2,1)S(1)} async-done(((bf16[8,32,2048]{2,1,0:T(8,128)(2,1)}), bf16[8,32,2048]{2,1,0:T(8,128)(2,1)S(1)}, u32[]{:S(2)}, u32[]{:S(2)}) %all-to-all-start.2) | async-done | bytes 1048608 | tf_op jit(solution)/shard_map/all_to_all | solution.py:216
  134.5 1.1 shard_map.86
  (4 shorter events, 0.1 us)
Async XLA Ops:
  0.6 0.8 copy-start.2
  1.5 0.8 copy-start.3
  3.0 17.6 %all-to-all-start.1 = ((bf16[8,32,256]{2,1,0:T(8,128)(2,1)}), bf16[8,32,256]{2,1,0:T(8,128)(2,1)S(1)}, u32[]{:S(2)}, u32[]{:S(2)}) async-start(bf16[8,32,256]{2,1,0:T(8,128)(2,1)} %shard_map.85), calls=%async_computation.1 | async-start | bytes 262144 | tf_op jit(solution)/shard_map/all_to_all | solution.py:216
  11.5 1.0 copy-start
  12.5 1.0 copy-start.1
  14.7 9.4 %copy-start.4 = (s32[256]{0:T(256)S(1)}, s32[256]{0:T(256)}, u32[]{:S(2)}) copy-start(s32[256]{0:T(256)} %param.9) | copy-start | bytes 3076
  20.6 30.9 %all-to-all-start = ((bf16[8,32,2048]{2,1,0:T(8,128)(2,1)}), bf16[8,32,2048]{2,1,0:T(8,128)(2,1)S(1)}, u32[]{:S(2)}, u32[]{:S(2)}) async-start(bf16[8,32,2048]{2,1,0:T(8,128)(2,1)} %shard_map.84), calls=%async_computation | async-start | bytes 2097152 | tf_op jit(solution)/shard_map/all_to_all | solution.py:216
  24.2 11.3 %collective-permute-start.2 = (bf16[272,256]{1,0:T(8,128)(2,1)S(1)}, bf16[272,256]{1,0:T(8,128)(2,1)S(1)}, u32[]{:S(2)}, u32[]{:S(2)}) collective-permute-start(bf16[272,256]{1,0:T(8,128)(2,1)S(1)} %get-tuple-element.24.own), channel_id=1, source_target_pairs={{0,48},{8,56},{16,64},{24,72},{32,80},{40,88},{48,96},{56,104},{64... | collective-permute-start | bytes 417800 | tf_op jit(solution)/shard_map/ppermute | solution.py:207
  29.1 10.4 %collective-permute-start.1 = (bf16[272,256]{1,0:T(8,128)(2,1)S(1)}, bf16[272,256]{1,0:T(8,128)(2,1)S(1)}, u32[]{:S(2)}, u32[]{:S(2)}) collective-permute-start(bf16[272,256]{1,0:T(8,128)(2,1)S(1)} %get-tuple-element.24.own), channel_id=1, source_target_pairs={{0,32},{8,40},{16,48},{24,56},{32,64},{40,72},{48,80},{56,88},{64,... | collective-permute-start | bytes 417800 | tf_op jit(solution)/shard_map/ppermute | solution.py:207
  32.6 9.1 %collective-permute-start = (bf16[272,256]{1,0:T(8,128)(2,1)S(1)}, bf16[272,256]{1,0:T(8,128)(2,1)S(1)}, u32[]{:S(2)}, u32[]{:S(2)}) collective-permute-start(bf16[272,256]{1,0:T(8,128)(2,1)S(1)} %get-tuple-element.24.own), channel_id=1, source_target_pairs={{0,16},{8,24},{16,32},{24,40},{32,48},{40,56},{48,64},{56,72},{64,... | collective-permute-start | bytes 417800 | tf_op jit(solution)/shard_map/ppermute | solution.py:207
  41.7 2.0 %collective-permute-start.3 = (bf16[4,272,256]{2,1,0:T(8,128)(2,1)S(1)}, bf16[4,272,256]{2,1,0:T(8,128)(2,1)S(1)}, u32[]{:S(2)}, u32[]{:S(2)}) collective-permute-start(bf16[4,272,256]{2,1,0:T(8,128)(2,1)S(1)} %pad_maximum_fusion), channel_id=1, source_target_pairs={{0,8},{8,0},{16,24},{24,16},{32,40},{40,32},{48,56},{56,48},{64,72... | collective-permute-start | bytes 1671176 | tf_op jit(solution)/shard_map/ppermute | solution.py:212
  74.0 1.9 %collective-permute-start.4 = (bf16[4,256,256]{2,1,0:T(8,128)(2,1)S(1)}, bf16[4,256,256]{2,1,0:T(8,128)(2,1)S(1)}, u32[]{:S(2)}, u32[]{:S(2)}) collective-permute-start(bf16[4,256,256]{2,1,0:T(8,128)(2,1)S(1)} %get-tuple-element.15), channel_id=1, source_target_pairs={{0,8},{8,0},{16,24},{24,16},{32,40},{40,32},{48,56},{56,48},{64,72... | collective-permute-start | bytes 1572872 | tf_op jit(solution)/shard_map/ppermute | solution.py:212
  76.1 8.8 %collective-permute-start.5 = (bf16[256,256]{1,0:T(8,128)(2,1)S(1)}, bf16[256,256]{1,0:T(8,128)(2,1)S(1)}, u32[]{:S(2)}, u32[]{:S(2)}) collective-permute-start(bf16[256,256]{1,0:T(8,128)(2,1)S(1)} %get-tuple-element.20), channel_id=1, source_target_pairs={{16,0},{24,8},{32,16},{40,24},{48,32},{56,40},{64,48},{72,56},{80,... | collective-permute-start | bytes 393224 | tf_op jit(solution)/shard_map/ppermute | solution.py:207
  81.0 11.2 %collective-permute-start.7 = (bf16[256,256]{1,0:T(8,128)(2,1)S(1)}, bf16[256,256]{1,0:T(8,128)(2,1)S(1)}, u32[]{:S(2)}, u32[]{:S(2)}) collective-permute-start(bf16[256,256]{1,0:T(8,128)(2,1)S(1)} %get-tuple-element.21), channel_id=1, source_target_pairs={{48,0},{56,8},{64,16},{72,24},{80,32},{88,40},{96,48},{104,56},{11... | collective-permute-start | bytes 393224 | tf_op jit(solution)/shard_map/ppermute | solution.py:207
  83.0 9.2 %collective-permute-start.6 = (bf16[256,256]{1,0:T(8,128)(2,1)S(1)}, bf16[256,256]{1,0:T(8,128)(2,1)S(1)}, u32[]{:S(2)}, u32[]{:S(2)}) collective-permute-start(bf16[256,256]{1,0:T(8,128)(2,1)S(1)} %get-tuple-element.22), channel_id=1, source_target_pairs={{32,0},{40,8},{48,16},{56,24},{64,32},{72,40},{80,48},{88,56},{96,... | collective-permute-start | bytes 393224 | tf_op jit(solution)/shard_map/ppermute | solution.py:207
  103.8 30.7 %all-to-all-start.2 = ((bf16[8,32,2048]{2,1,0:T(8,128)(2,1)}), bf16[8,32,2048]{2,1,0:T(8,128)(2,1)S(1)}, u32[]{:S(2)}, u32[]{:S(2)}) async-start(bf16[8,32,2048]{2,1,0:T(8,128)(2,1)} %bitcast.7), calls=%async_computation.2 | async-start | bytes 2097152 | tf_op jit(solution)/shard_map/all_to_all | solution.py:216

commit v2 on v1

--- a/solution.py
+++ b/solution.py
@@ -21,6 +21,8 @@
 MASKED = -1e30
 NT = (((1,), (1,)), ((), ()))
 VMEM = pl.BlockSpec(memory_space=pltpu.VMEM)
+SMEM = pl.BlockSpec(memory_space=pltpu.SMEM)
+SMALL = pltpu.CompilerParams(vmem_limit_bytes=8 * 1024 * 1024)
 
 
 def dot(a, b, dims=(((1,), (0,)), ((), ()))):
@@ -43,9 +45,98 @@
         out_shape=jax.ShapeDtypeStruct((parts, rows, 2 * width // parts), a.dtype),
         in_specs=[VMEM, VMEM],
         out_specs=VMEM,
-        compiler_params=pltpu.CompilerParams(vmem_limit_bytes=8 * 1024 * 1024),
+        compiler_params=SMALL,
         cost_estimate=pl.CostEstimate(flops=rows * width, bytes_accessed=8 * rows * width, transcendentals=0),
     )(a, b)
+
+
+def cut_body(parts, at_ref, a_ref, b_ref, *o_refs):
+    for k in range(parts):
+        source = pl.ds(pl.multiple_of(lax.rem(at_ref[0] + k, parts) * HEAD, HEAD), HEAD)
+        o_refs[k][:, :HEAD] = a_ref[:, source]
+        o_refs[k][:, HEAD:] = b_ref[:, source]
+
+
+def cut(at, a, b, parts):
+    rows = a.shape[0]
+    piece = jax.ShapeDtypeStruct((rows, 2 * HEAD), a.dtype)
+    return pl.pallas_call(
+        functools.partial(cut_body, parts),
+        out_shape=(piece,) * parts,
+        in_specs=[SMEM, VMEM, VMEM],
+        out_specs=(VMEM,) * parts,
+        compiler_params=SMALL,
+        cost_estimate=pl.CostEstimate(flops=a.size, bytes_accessed=8 * a.size, transcendentals=0),
+        name="cut",
+    )(at, a, b)
+
+
+def assemble_body(parts, at_ref, doc_ref, *refs):
+    o_ref = refs[parts]
+    rows = refs[0].shape[0]
+    for k in range(parts):
+        target = pl.multiple_of(lax.rem(at_ref[0] + (parts - k), parts) * rows, rows)
+        o_ref[pl.ds(target, rows), :] = refs[k][...]
+    doc = (doc_ref[...] + 1).astype(jnp.float32)
+    o_ref[parts * rows :, :] = jnp.broadcast_to(doc, (DOC_ROWS, parts * rows)).astype(jnp.bfloat16)
+
+
+def assemble(at, docs, pieces):
+    parts, (rows, columns) = len(pieces), pieces[0].shape
+    return pl.pallas_call(
+        functools.partial(assemble_body, parts),
+        out_shape=jax.ShapeDtypeStruct((parts * rows + DOC_ROWS, columns), pieces[0].dtype),
+        in_specs=[SMEM] + [VMEM] * (parts + 1),
+        out_specs=VMEM,
+        compiler_params=SMALL,
+        cost_estimate=pl.CostEstimate(flops=parts * rows * columns, bytes_accessed=4 * parts * rows * columns, transcendentals=0),
+        name="assemble",
+    )(at, docs[None, :], *pieces)
+
+
+def add_cut_body(parts, at_ref, base_ref, one_ref, two_ref, three_ref, *o_refs):
+    rows = o_refs[0].shape[0]
+    for k in range(parts):
+        source = pl.ds(pl.multiple_of(lax.rem(at_ref[0] + k, parts) * rows, rows), rows)
+        total = base_ref[source, :] + one_ref[source, :].astype(jnp.float32)
+        total = total + two_ref[source, :].astype(jnp.float32) + three_ref[source, :].astype(jnp.float32)
+        o_refs[k][...] = total.astype(jnp.bfloat16)
+
+
+def add_cut(at, base, others, parts):
+    rows, columns = base.shape[0] // parts, base.shape[1]
+    piece = jax.ShapeDtypeStruct((rows, columns), jnp.bfloat16)
+    return pl.pallas_call(
+        functools.partial(add_cut_body, parts),
+        out_shape=(piece,) * parts,
+        in_specs=[SMEM] + [VMEM] * 4,
+        out_specs=(VMEM,) * parts,
+        compiler_params=SMALL,
+        cost_estimate=pl.CostEstimate(flops=4 * base.size, bytes_accessed=12 * base.size, transcendentals=0),
+        name="add_cut",
+    )(at, base, *others)
+
+
+def join_body(parts, at_ref, *refs):
+    a_ref, b_ref = refs[parts:]
+    for k in range(parts):
+        target = pl.ds(pl.multiple_of(lax.rem(at_ref[0] + (parts - k), parts) * HEAD, HEAD), HEAD)
+        a_ref[:, target] = refs[k][:, :HEAD]
+        b_ref[:, target] = refs[k][:, HEAD:]
+
+
+def join(at, pieces):
+    parts, rows = len(pieces), pieces[0].shape[0]
+    out = jax.ShapeDtypeStruct((rows, parts * HEAD), pieces[0].dtype)
+    return pl.pallas_call(
+        functools.partial(join_body, parts),
+        out_shape=(out, out),
+        in_specs=[SMEM] + [VMEM] * parts,
+        out_specs=(VMEM, VMEM),
+        compiler_params=SMALL,
+        cost_estimate=pl.CostEstimate(flops=out.size, bytes_accessed=8 * out.size, transcendentals=0),
+        name="join",
+    )(at, *pieces)
 
 
 def unpack_body(width, parts, i_ref, a_ref, b_ref):
@@ -66,7 +157,7 @@
         out_shape=(out, out),
         in_specs=[VMEM],
         out_specs=(VMEM, VMEM),
-        compiler_params=pltpu.CompilerParams(vmem_limit_bytes=8 * 1024 * 1024),
+        compiler_params=SMALL,
         cost_estimate=pl.CostEstimate(flops=rows * width, bytes_accessed=8 * rows * width, transcendentals=0),
     )(both)
 
@@ -216,15 +307,24 @@
     return lax.all_to_all(value, "head", split_axis=0, concat_axis=0, tiled=True)
 
 
+def around(value, steps):
+    count = lax.axis_size("head")
+    return lax.ppermute(value, "head", [(s, (s + steps) % count) for s in range(count)])
+
+
+def exchange(pieces):
+    return [pieces[0]] + [around(piece, k) for k, piece in enumerate(pieces) if k]
+
+
 def local(queries, key_heads, value_head_array, out_grad, doc_ids):
     parts = lax.axis_size("head")
     core = (lax.axis_index("ctx") % 2).astype(jnp.int32).reshape(1)
-    kv = over_head(pack(key_heads, value_head_array, parts))
-    kv = kv.reshape(BLOCK, 2 * HEAD)
-    docs = jnp.pad((doc_ids + 1).astype(jnp.bfloat16)[None, :], ((0, DOC_ROWS - 1), (0, 0)))
-    own = jnp.concatenate([kv, docs], axis=0)
+    at = lax.axis_index("head").astype(jnp.int32).reshape(1)
+    pieces = cut(at, key_heads, value_head_array, parts)
     packed = pack(queries, out_grad, parts)
     x = over_head(packed).reshape(BLOCK, -1)
+    pieces = exchange(pieces)
+    own = assemble(at, doc_ids, pieces)
     two, four, six = (shift(own, steps) for steps in (2, 4, 6))
     mate = swap(jnp.stack([own, two, four, six]))
     y, mine, sent = attention(core, x, own, two, four, six, mate)
@@ -233,11 +333,10 @@
     sums = mine + sent.astype(jnp.float32)
     rounded = sums.astype(jnp.bfloat16)
     back = [shift(rounded[t], -2 * t) for t in range(1, SLOTS)]
-    grads = sums[0] + sum(b.astype(jnp.float32) for b in back)
-    grads = grads.astype(jnp.bfloat16)
-    grads = over_head(grads.reshape(parts, -1, 2 * HEAD))
+    pieces = add_cut(at, sums[0], back, parts)
+    pieces = exchange(pieces)
     attended, query_grad = unpack(y)
-    key_grad, value_grad = unpack(grads)
+    key_grad, value_grad = join(at, pieces)
     return attended, query_grad, key_grad, value_grad
 
 

time: 136 us -> 132 us (0.971)
  starting transfers between devices: 35.7 us -> 67 us
  waiting for transfers between devices: 57.3 us -> 33.5 us
  blocking collectives: 11.5 us -> 0 us
    all_to_all x3 -> x2, waiting for transfers between devices: 40 us -> 0.01 us  [over_head(): lax.all_to_all(value, 'head', split_axis=0, concat_axis=0, tiled=True)]
    ppermute x0 -> x14, starting transfers between devices: none -> 35.7 us  [around(): lax.ppermute(value, 'head', [(s, (s + steps) % count) for s in range(coun...]
    ppermute x0 -> x14, waiting for transfers between devices: none -> 16.1 us  [around(): lax.ppermute(value, 'head', [(s, (s + steps) % count) for s in range(coun...]
    all_to_all x1 -> x0, blocking collectives: 11.5 us -> none  [over_head(): lax.all_to_all(value, 'head', split_axis=0, concat_axis=0, tiled=True)]
    all_to_all x3 -> x2, starting transfers between devices: 15.6 us -> 13.2 us  [over_head(): lax.all_to_all(value, 'head', split_axis=0, concat_axis=0, tiled=True)]
    ppermute x6, starting transfers between devices: 20 us -> 17.9 us  [shift(): lax.ppermute(value, 'ctx', [(s, s + steps) for s in range(max(0, -steps),...]
    unnamed x10 -> x14, local copies, waits for them, and re-layouts: 3.75 us -> 3.56 us
  transfers between devices with their start and end apart: 11 -> 24, of which waited for: 8 -> 11; matrix products, arithmetic and copies ran while one was open for 0% -> 0% of each run, Pallas kernels for 1% -> 1%
where the time goes in v2:
time: 132 us; the launch traced here: 131 us
  starting transfers between devices  67 us (51%)
  waiting for transfers between devices  33.5 us (25%)
  Pallas kernels  25.7 us (19%)
  local copies, waits for them, and re-layouts  3.6 us (3%)
    ppermute x14, starting transfers between devices, around(): lax.ppermute(value, 'head', [(s, (s + steps) % count) for s in range(coun...  35.7 us
    pallas_call x1, Pallas kernels, attention(): pl.pallas_call(attention_body, out_shape=(jax.ShapeDtypeStruct(x.shape, j...  22.6 us
    ppermute x6, starting transfers between devices, shift(): lax.ppermute(value, 'ctx', [(s, s + steps) for s in range(max(0, -steps),...  17.9 us
    ppermute x14, waiting for transfers between devices, around(): lax.ppermute(value, 'head', [(s, (s + steps) % count) for s in range(coun...  16.1 us
    ppermute x6, waiting for transfers between devices, shift(): lax.ppermute(value, 'ctx', [(s, s + steps) for s in range(max(0, -steps),...  13.6 us
    all_to_all x2, starting transfers between devices, over_head(): lax.all_to_all(value, 'head', split_axis=0, concat_axis=0, tiled=True)  13.2 us
    ppermute x2, waiting for transfers between devices, swap(): return lax.ppermute(value, 'ctx', [(s, s ^ 1) for s in range(count)])  3.83 us
    unnamed x14, local copies, waits for them, and re-layouts  3.56 us
  transfers between devices with their start and end apart: 24, of which 11 were waited for; matrix products, arithmetic and copies ran while one was open for 0% of the time, Pallas kernels for 1%

profile of v2, /device:TPU:2, one launch (start us, length us, event | category | flops | bytes accessed | tf_op | source)
XLA Modules:
  0.0 130.8 jit_solution(5761010313994273649)
XLA Ops:
  0.6 0.0 copy-start
  0.6 1.0 copy-done
  1.7 0.0 copy-start.1
  1.7 1.0 copy-done.1
  2.7 1.2 shard_map.84
  3.9 8.6 %all-to-all-start = ((bf16[8,32,2048]{2,1,0:T(8,128)(2,1)}), bf16[8,32,2048]{2,1,0:T(8,128)(2,1)S(1)}, u32[]{:S(2)}, u32[]{:S(2)}) async-start(bf16[8,32,2048]{2,1,0:T(8,128)(2,1)} %shard_map.84), calls=%async_computation | async-start | bytes 2097152 | tf_op jit(solution)/shard_map/all_to_all | solution.py:307
  12.5 0.0 copy-done.2
  12.5 0.0 copy-done.3
  12.5 2.1 %collective-permute-start = (bf16[32,256]{1,0:T(8,128)(2,1)S(1)}, bf16[32,256]{1,0:T(8,128)(2,1)S(1)}, u32[]{:S(2)}, u32[]{:S(2)}) collective-permute-start(bf16[32,256]{1,0:T(8,128)(2,1)S(1)} %get-tuple-element.28), channel_id=1, source_target_pairs={{0,1},{1,2},{2,3},{3,4},{4,5},{5,6},{6,7},{7,0},{8,9},{9,10},{10,1... | collective-permute-start | bytes 49160 | tf_op jit(solution)/shard_map/ppermute | solution.py:312
  14.6 2.4 %collective-permute-start.1 = (bf16[32,256]{1,0:T(8,128)(2,1)S(1)}, bf16[32,256]{1,0:T(8,128)(2,1)S(1)}, u32[]{:S(2)}, u32[]{:S(2)}) collective-permute-start(bf16[32,256]{1,0:T(8,128)(2,1)S(1)} %get-tuple-element.29), channel_id=1, source_target_pairs={{0,2},{1,3},{2,4},{3,5},{4,6},{5,7},{6,0},{7,1},{8,10},{9,11},{10,... | collective-permute-start | bytes 49160 | tf_op jit(solution)/shard_map/ppermute | solution.py:312
  17.0 2.7 %collective-permute-start.2 = (bf16[32,256]{1,0:T(8,128)(2,1)S(1)}, bf16[32,256]{1,0:T(8,128)(2,1)S(1)}, u32[]{:S(2)}, u32[]{:S(2)}) collective-permute-start(bf16[32,256]{1,0:T(8,128)(2,1)S(1)} %get-tuple-element.30), channel_id=1, source_target_pairs={{0,3},{1,4},{2,5},{3,6},{4,7},{5,0},{6,1},{7,2},{8,11},{9,12},{10,... | collective-permute-start | bytes 49160 | tf_op jit(solution)/shard_map/ppermute | solution.py:312
  19.7 2.4 %collective-permute-start.3 = (bf16[32,256]{1,0:T(8,128)(2,1)S(1)}, bf16[32,256]{1,0:T(8,128)(2,1)S(1)}, u32[]{:S(2)}, u32[]{:S(2)}) collective-permute-start(bf16[32,256]{1,0:T(8,128)(2,1)S(1)} %get-tuple-element.31), channel_id=1, source_target_pairs={{0,4},{1,5},{2,6},{3,7},{4,0},{5,1},{6,2},{7,3},{8,12},{9,13},{10,... | collective-permute-start | bytes 49160 | tf_op jit(solution)/shard_map/ppermute | solution.py:312
  22.0 2.7 %collective-permute-start.4 = (bf16[32,256]{1,0:T(8,128)(2,1)S(1)}, bf16[32,256]{1,0:T(8,128)(2,1)S(1)}, u32[]{:S(2)}, u32[]{:S(2)}) collective-permute-start(bf16[32,256]{1,0:T(8,128)(2,1)S(1)} %get-tuple-element.32), channel_id=1, source_target_pairs={{0,5},{1,6},{2,7},{3,0},{4,1},{5,2},{6,3},{7,4},{8,13},{9,14},{10,... | collective-permute-start | bytes 49160 | tf_op jit(solution)/shard_map/ppermute | solution.py:312
  24.7 10.5 %collective-permute-done.refs_1_ = bf16[32,256]{1,0:T(8,128)(2,1)S(1)} collective-permute-done((bf16[32,256]{1,0:T(8,128)(2,1)S(1)}, bf16[32,256]{1,0:T(8,128)(2,1)S(1)}, u32[]{:S(2)}, u32[]{:S(2)}) %collective-permute-start) | collective-permute-done | bytes 16416 | tf_op jit(solution)/shard_map/ppermute | solution.py:312
  35.2 4.7 %collective-permute-start.5 = (bf16[32,256]{1,0:T(8,128)(2,1)S(1)}, bf16[32,256]{1,0:T(8,128)(2,1)S(1)}, u32[]{:S(2)}, u32[]{:S(2)}) collective-permute-start(bf16[32,256]{1,0:T(8,128)(2,1)S(1)} %get-tuple-element.33), channel_id=1, source_target_pairs={{0,6},{1,7},{2,0},{3,1},{4,2},{5,3},{6,4},{7,5},{8,14},{9,15},{10,... | collective-permute-start | bytes 49160 | tf_op jit(solution)/shard_map/ppermute | solution.py:312
  40.0 1.3 collective-permute-done.1.refs_2_
  41.2 1.7 %collective-permute-start.6 = (bf16[32,256]{1,0:T(8,128)(2,1)S(1)}, bf16[32,256]{1,0:T(8,128)(2,1)S(1)}, u32[]{:S(2)}, u32[]{:S(2)}) collective-permute-start(bf16[32,256]{1,0:T(8,128)(2,1)S(1)} %get-tuple-element.34), channel_id=1, source_target_pairs={{0,7},{1,0},{2,1},{3,2},{4,3},{5,4},{6,5},{7,6},{8,15},{9,8},{10,9... | collective-permute-start | bytes 49160 | tf_op jit(solution)/shard_map/ppermute | solution.py:312
  42.9 0.0 collective-permute-done.2.refs_3_
  42.9 0.2 collective-permute-done.3.refs_4_
  43.1 0.0 collective-permute-done.4.refs_5_
  43.1 0.0 collective-permute-done.5.refs_6_
  43.1 1.8 %collective-permute-done.6.refs_7_ = bf16[32,256]{1,0:T(8,128)(2,1)S(1)} collective-permute-done((bf16[32,256]{1,0:T(8,128)(2,1)S(1)}, bf16[32,256]{1,0:T(8,128)(2,1)S(1)}, u32[]{:S(2)}, u32[]{:S(2)}) %collective-permute-start.6) | collective-permute-done | bytes 16416 | tf_op jit(solution)/shard_map/ppermute | solution.py:312
  45.0 0.7 copy-done.4
  45.7 4.9 %collective-permute-start.9 = (bf16[272,256]{1,0:T(8,128)(2,1)S(1)}, bf16[272,256]{1,0:T(8,128)(2,1)S(1)}, u32[]{:S(2)}, u32[]{:S(2)}) collective-permute-start(bf16[272,256]{1,0:T(8,128)(2,1)S(1)} %assemble.1.own), channel_id=1, source_target_pairs={{0,48},{8,56},{16,64},{24,72},{32,80},{40,88},{48,96},{56,104},{64... | collective-permute-start | bytes 417800 | tf_op jit(solution)/shard_map/ppermute | solution.py:298
  50.6 3.5 %collective-permute-start.8 = (bf16[272,256]{1,0:T(8,128)(2,1)S(1)}, bf16[272,256]{1,0:T(8,128)(2,1)S(1)}, u32[]{:S(2)}, u32[]{:S(2)}) collective-permute-start(bf16[272,256]{1,0:T(8,128)(2,1)S(1)} %assemble.1.own), channel_id=1, source_target_pairs={{0,32},{8,40},{16,48},{24,56},{32,64},{40,72},{48,80},{56,88},{64,... | collective-permute-start | bytes 417800 | tf_op jit(solution)/shard_map/ppermute | solution.py:298
  54.1 2.9 %collective-permute-start.7 = (bf16[272,256]{1,0:T(8,128)(2,1)S(1)}, bf16[272,256]{1,0:T(8,128)(2,1)S(1)}, u32[]{:S(2)}, u32[]{:S(2)}) collective-permute-start(bf16[272,256]{1,0:T(8,128)(2,1)S(1)} %assemble.1.own), channel_id=1, source_target_pairs={{0,16},{8,24},{16,32},{24,40},{32,48},{40,56},{48,64},{56,72},{64,... | collective-permute-start | bytes 417800 | tf_op jit(solution)/shard_map/ppermute | solution.py:298
  56.9 0.0 collective-permute-done.9.six
  57.0 4.0 %collective-permute-done.8.four = bf16[272,256]{1,0:T(8,128)(2,1)S(1)} collective-permute-done((bf16[272,256]{1,0:T(8,128)(2,1)S(1)}, bf16[272,256]{1,0:T(8,128)(2,1)S(1)}, u32[]{:S(2)}, u32[]{:S(2)}) %collective-permute-start.8) | collective-permute-done | bytes 139296 | tf_op jit(solution)/shard_map/ppermute | solution.py:298
  61.0 2.1 %collective-permute-done.7.two = bf16[272,256]{1,0:T(8,128)(2,1)S(1)} collective-permute-done((bf16[272,256]{1,0:T(8,128)(2,1)S(1)}, bf16[272,256]{1,0:T(8,128)(2,1)S(1)}, u32[]{:S(2)}, u32[]{:S(2)}) %collective-permute-start.7) | collective-permute-done | bytes 139296 | tf_op jit(solution)/shard_map/ppermute | solution.py:298
  63.1 0.1 pad_maximum_fusion
  63.2 0.1 collective-permute-start.10
  63.3 1.9 %collective-permute-done.10.mate = bf16[4,272,256]{2,1,0:T(8,128)(2,1)S(1)} collective-permute-done((bf16[4,272,256]{2,1,0:T(8,128)(2,1)S(1)}, bf16[4,272,256]{2,1,0:T(8,128)(2,1)S(1)}, u32[]{:S(2)}, u32[]{:S(2)}) %collective-permute-start.10) | collective-permute-done | bytes 557088 | tf_op jit(solution)/shard_map/ppermute | solution.py:303
  65.2 0.0 all-to-all-done
  65.2 22.6 %attention.1 = (bf16[256,2048]{1,0:T(8,128)(2,1)}, f32[4,256,256]{2,1,0:T(8,128)S(1)}, bf16[4,256,256]{2,1,0:T(8,128)(2,1)S(1)}) custom-call(s32[1]{0:T(128)} %bitcast.core_ref, bf16[256,2048]{1,0:T(8,128)(2,1)S(1)} %bitcast.17, bf16[272,256]{1,0:T(8,128)(2,1)S(1)} %assemble.1.own, bf16[272,256]{1,0:T(8,128)(2,1)S(1)} %collective-permute-done.7.two, ...), custom_call_target="tpu_custom_call" | custom-call | flops 5637144576 | bytes 5242880 | tf_op jit(solution)/shard_map/attention/pallas_call | solution.py:256
  87.8 0.8 copy-done.5
  88.6 4.6 %all-to-all-start.1 = ((bf16[8,32,2048]{2,1,0:T(8,128)(2,1)}), bf16[8,32,2048]{2,1,0:T(8,128)(2,1)S(1)}, u32[]{:S(2)}, u32[]{:S(2)}) async-start(bf16[8,32,2048]{2,1,0:T(8,128)(2,1)} %bitcast.8), calls=%async_computation.1 | async-start | bytes 2097152 | tf_op jit(solution)/shard_map/all_to_all | solution.py:307
  93.2 0.0 copy-done.6
  93.2 0.1 collective-permute-start.11
  93.3 1.9 %collective-permute-done.11 = bf16[4,256,256]{2,1,0:T(8,128)(2,1)S(1)} collective-permute-done((bf16[4,256,256]{2,1,0:T(8,128)(2,1)S(1)}, bf16[4,256,256]{2,1,0:T(8,128)(2,1)S(1)}, u32[]{:S(2)}, u32[]{:S(2)}) %collective-permute-start.11) | collective-permute-done | bytes 524320 | tf_op jit(solution)/shard_map/ppermute | solution.py:303
  95.2 0.1 fusion
  95.4 1.9 %collective-permute-start.14 = (bf16[256,256]{1,0:T(8,128)(2,1)S(1)}, bf16[256,256]{1,0:T(8,128)(2,1)S(1)}, u32[]{:S(2)}, u32[]{:S(2)}) collective-permute-start(bf16[256,256]{1,0:T(8,128)(2,1)S(1)} %get-tuple-element.52), channel_id=1, source_target_pairs={{48,0},{56,8},{64,16},{72,24},{80,32},{88,40},{96,48},{104,56},{11... | collective-permute-start | bytes 393224 | tf_op jit(solution)/shard_map/ppermute | solution.py:298
  97.4 2.0 %collective-permute-start.13 = (bf16[256,256]{1,0:T(8,128)(2,1)S(1)}, bf16[256,256]{1,0:T(8,128)(2,1)S(1)}, u32[]{:S(2)}, u32[]{:S(2)}) collective-permute-start(bf16[256,256]{1,0:T(8,128)(2,1)S(1)} %get-tuple-element.53), channel_id=1, source_target_pairs={{32,0},{40,8},{48,16},{56,24},{64,32},{72,40},{80,48},{88,56},{96,... | collective-permute-start | bytes 393224 | tf_op jit(solution)/shard_map/ppermute | solution.py:298
  99.4 2.7 %collective-permute-start.12 = (bf16[256,256]{1,0:T(8,128)(2,1)S(1)}, bf16[256,256]{1,0:T(8,128)(2,1)S(1)}, u32[]{:S(2)}, u32[]{:S(2)}) collective-permute-start(bf16[256,256]{1,0:T(8,128)(2,1)S(1)} %get-tuple-element.54), channel_id=1, source_target_pairs={{16,0},{24,8},{32,16},{40,24},{48,32},{56,40},{64,48},{72,56},{80,... | collective-permute-start | bytes 393224 | tf_op jit(solution)/shard_map/ppermute | solution.py:298
  102.1 4.8 %collective-permute-done.14.three_ref = bf16[256,256]{1,0:T(8,128)(2,1)S(1)} collective-permute-done((bf16[256,256]{1,0:T(8,128)(2,1)S(1)}, bf16[256,256]{1,0:T(8,128)(2,1)S(1)}, u32[]{:S(2)}, u32[]{:S(2)}) %collective-permute-start.14) | collective-permute-done | bytes 131104 | tf_op jit(solution)/shard_map/ppermute | solution.py:298
  106.9 0.0 collective-permute-done.13.two_ref
  106.9 2.6 %collective-permute-done.12.one_ref = bf16[256,256]{1,0:T(8,128)(2,1)S(1)} collective-permute-done((bf16[256,256]{1,0:T(8,128)(2,1)S(1)}, bf16[256,256]{1,0:T(8,128)(2,1)S(1)}, u32[]{:S(2)}, u32[]{:S(2)}) %collective-permute-start.12) | collective-permute-done | bytes 131104 | tf_op jit(solution)/shard_map/ppermute | solution.py:298
  109.5 0.1 add_cut.1
  109.6 2.0 %collective-permute-start.15 = (bf16[32,256]{1,0:T(8,128)(2,1)S(1)}, bf16[32,256]{1,0:T(8,128)(2,1)S(1)}, u32[]{:S(2)}, u32[]{:S(2)}) collective-permute-start(bf16[32,256]{1,0:T(8,128)(2,1)S(1)} %get-tuple-element.41), channel_id=1, source_target_pairs={{0,1},{1,2},{2,3},{3,4},{4,5},{5,6},{6,7},{7,0},{8,9},{9,10},{10,1... | collective-permute-start | bytes 49160 | tf_op jit(solution)/shard_map/ppermute | solution.py:312
  111.6 2.4 %collective-permute-start.16 = (bf16[32,256]{1,0:T(8,128)(2,1)S(1)}, bf16[32,256]{1,0:T(8,128)(2,1)S(1)}, u32[]{:S(2)}, u32[]{:S(2)}) collective-permute-start(bf16[32,256]{1,0:T(8,128)(2,1)S(1)} %get-tuple-element.42), channel_id=1, source_target_pairs={{0,2},{1,3},{2,4},{3,5},{4,6},{5,7},{6,0},{7,1},{8,10},{9,11},{10,... | collective-permute-start | bytes 49160 | tf_op jit(solution)/shard_map/ppermute | solution.py:312
  114.0 2.7 %collective-permute-start.17 = (bf16[32,256]{1,0:T(8,128)(2,1)S(1)}, bf16[32,256]{1,0:T(8,128)(2,1)S(1)}, u32[]{:S(2)}, u32[]{:S(2)}) collective-permute-start(bf16[32,256]{1,0:T(8,128)(2,1)S(1)} %get-tuple-element.43), channel_id=1, source_target_pairs={{0,3},{1,4},{2,5},{3,6},{4,7},{5,0},{6,1},{7,2},{8,11},{9,12},{10,... | collective-permute-start | bytes 49160 | tf_op jit(solution)/shard_map/ppermute | solution.py:312
  116.6 2.4 %collective-permute-start.18 = (bf16[32,256]{1,0:T(8,128)(2,1)S(1)}, bf16[32,256]{1,0:T(8,128)(2,1)S(1)}, u32[]{:S(2)}, u32[]{:S(2)}) collective-permute-start(bf16[32,256]{1,0:T(8,128)(2,1)S(1)} %get-tuple-element.44), channel_id=1, source_target_pairs={{0,4},{1,5},{2,6},{3,7},{4,0},{5,1},{6,2},{7,3},{8,12},{9,13},{10,... | collective-permute-start | bytes 49160 | tf_op jit(solution)/shard_map/ppermute | solution.py:312
  119.0 2.7 %collective-permute-start.19 = (bf16[32,256]{1,0:T(8,128)(2,1)S(1)}, bf16[32,256]{1,0:T(8,128)(2,1)S(1)}, u32[]{:S(2)}, u32[]{:S(2)}) collective-permute-start(bf16[32,256]{1,0:T(8,128)(2,1)S(1)} %get-tuple-element.45), channel_id=1, source_target_pairs={{0,5},{1,6},{2,7},{3,0},{4,1},{5,2},{6,3},{7,4},{8,13},{9,14},{10,... | collective-permute-start | bytes 49160 | tf_op jit(solution)/shard_map/ppermute | solution.py:312
  121.7 0.0 collective-permute-done.15.refs_1_
  121.7 3.6 %collective-permute-start.20 = (bf16[32,256]{1,0:T(8,128)(2,1)S(1)}, bf16[32,256]{1,0:T(8,128)(2,1)S(1)}, u32[]{:S(2)}, u32[]{:S(2)}) collective-permute-start(bf16[32,256]{1,0:T(8,128)(2,1)S(1)} %get-tuple-element.46), channel_id=1, source_target_pairs={{0,6},{1,7},{2,0},{3,1},{4,2},{5,3},{6,4},{7,5},{8,14},{9,15},{10,... | collective-permute-start | bytes 49160 | tf_op jit(solution)/shard_map/ppermute | solution.py:312
  125.3 0.0 collective-permute-done.16.refs_2_
  125.3 1.5 %collective-permute-start.21 = (bf16[32,256]{1,0:T(8,128)(2,1)S(1)}, bf16[32,256]{1,0:T(8,128)(2,1)S(1)}, u32[]{:S(2)}, u32[]{:S(2)}) collective-permute-start(bf16[32,256]{1,0:T(8,128)(2,1)S(1)} %get-tuple-element.47), channel_id=1, source_target_pairs={{0,7},{1,0},{2,1},{3,2},{4,3},{5,4},{6,5},{7,6},{8,15},{9,8},{10,9... | collective-permute-start | bytes 49160 | tf_op jit(solution)/shard_map/ppermute | solution.py:312
  126.7 0.0 collective-permute-done.17.refs_3_
  126.7 0.0 collective-permute-done.18.refs_4_
  126.7 0.0 collective-permute-done.19.refs_5_
  126.7 0.0 collective-permute-done.20.refs_6_
  126.7 2.3 %collective-permute-done.21.refs_7_ = bf16[32,256]{1,0:T(8,128)(2,1)S(1)} collective-permute-done((bf16[32,256]{1,0:T(8,128)(2,1)S(1)}, bf16[32,256]{1,0:T(8,128)(2,1)S(1)}, u32[]{:S(2)}, u32[]{:S(2)}) %collective-permute-start.21) | collective-permute-done | bytes 16416 | tf_op jit(solution)/shard_map/ppermute | solution.py:312
  129.0 0.7 join.1
  129.7 0.0 all-to-all-done.1.i_ref
  129.7 1.1 shard_map.85
  (9 shorter events, 0.1 us)
Async XLA Ops:
  0.6 1.0 copy-start
  1.7 1.0 copy-start.1
  3.9 8.6 %copy-start.2 = (bf16[32,1024]{1,0:T(8,128)(2,1)S(1)}, bf16[32,1024]{1,0:T(8,128)(2,1)}, u32[]{:S(2)}) copy-start(bf16[32,1024]{1,0:T(8,128)(2,1)} %a_ref.3) | copy-start | bytes 196612
  3.9 8.6 %copy-start.3 = (bf16[32,1024]{1,0:T(8,128)(2,1)S(1)}, bf16[32,1024]{1,0:T(8,128)(2,1)}, u32[]{:S(2)}) copy-start(bf16[32,1024]{1,0:T(8,128)(2,1)} %b_ref.3) | copy-start | bytes 196612
  3.9 61.4 %all-to-all-start = ((bf16[8,32,2048]{2,1,0:T(8,128)(2,1)}), bf16[8,32,2048]{2,1,0:T(8,128)(2,1)S(1)}, u32[]{:S(2)}, u32[]{:S(2)}) async-start(bf16[8,32,2048]{2,1,0:T(8,128)(2,1)} %shard_map.84), calls=%async_computation | async-start | bytes 2097152 | tf_op jit(solution)/shard_map/all_to_all | solution.py:307
  12.5 22.7 %collective-permute-start = (bf16[32,256]{1,0:T(8,128)(2,1)S(1)}, bf16[32,256]{1,0:T(8,128)(2,1)S(1)}, u32[]{:S(2)}, u32[]{:S(2)}) collective-permute-start(bf16[32,256]{1,0:T(8,128)(2,1)S(1)} %get-tuple-element.28), channel_id=1, source_target_pairs={{0,1},{1,2},{2,3},{3,4},{4,5},{5,6},{6,7},{7,0},{8,9},{9,10},{10,1... | collective-permute-start | bytes 49160 | tf_op jit(solution)/shard_map/ppermute | solution.py:312
  14.6 26.6 %collective-permute-start.1 = (bf16[32,256]{1,0:T(8,128)(2,1)S(1)}, bf16[32,256]{1,0:T(8,128)(2,1)S(1)}, u32[]{:S(2)}, u32[]{:S(2)}) collective-permute-start(bf16[32,256]{1,0:T(8,128)(2,1)S(1)} %get-tuple-element.29), channel_id=1, source_target_pairs={{0,2},{1,3},{2,4},{3,5},{4,6},{5,7},{6,0},{7,1},{8,10},{9,11},{10,... | collective-permute-start | bytes 49160 | tf_op jit(solution)/shard_map/ppermute | solution.py:312
  17.0 25.9 %collective-permute-start.2 = (bf16[32,256]{1,0:T(8,128)(2,1)S(1)}, bf16[32,256]{1,0:T(8,128)(2,1)S(1)}, u32[]{:S(2)}, u32[]{:S(2)}) collective-permute-start(bf16[32,256]{1,0:T(8,128)(2,1)S(1)} %get-tuple-element.30), channel_id=1, source_target_pairs={{0,3},{1,4},{2,5},{3,6},{4,7},{5,0},{6,1},{7,2},{8,11},{9,12},{10,... | collective-permute-start | bytes 49160 | tf_op jit(solution)/shard_map/ppermute | solution.py:312
  19.7 23.5 %collective-permute-start.3 = (bf16[32,256]{1,0:T(8,128)(2,1)S(1)}, bf16[32,256]{1,0:T(8,128)(2,1)S(1)}, u32[]{:S(2)}, u32[]{:S(2)}) collective-permute-start(bf16[32,256]{1,0:T(8,128)(2,1)S(1)} %get-tuple-element.31), channel_id=1, source_target_pairs={{0,4},{1,5},{2,6},{3,7},{4,0},{5,1},{6,2},{7,3},{8,12},{9,13},{10,... | collective-permute-start | bytes 49160 | tf_op jit(solution)/shard_map/ppermute | solution.py:312
  22.0 21.1 %collective-permute-start.4 = (bf16[32,256]{1,0:T(8,128)(2,1)S(1)}, bf16[32,256]{1,0:T(8,128)(2,1)S(1)}, u32[]{:S(2)}, u32[]{:S(2)}) collective-permute-start(bf16[32,256]{1,0:T(8,128)(2,1)S(1)} %get-tuple-element.32), channel_id=1, source_target_pairs={{0,5},{1,6},{2,7},{3,0},{4,1},{5,2},{6,3},{7,4},{8,13},{9,14},{10,... | collective-permute-start | bytes 49160 | tf_op jit(solution)/shard_map/ppermute | solution.py:312
  35.2 7.9 %collective-permute-start.5 = (bf16[32,256]{1,0:T(8,128)(2,1)S(1)}, bf16[32,256]{1,0:T(8,128)(2,1)S(1)}, u32[]{:S(2)}, u32[]{:S(2)}) collective-permute-start(bf16[32,256]{1,0:T(8,128)(2,1)S(1)} %get-tuple-element.33), channel_id=1, source_target_pairs={{0,6},{1,7},{2,0},{3,1},{4,2},{5,3},{6,4},{7,5},{8,14},{9,15},{10,... | collective-permute-start | bytes 49160 | tf_op jit(solution)/shard_map/ppermute | solution.py:312
  41.2 3.7 %collective-permute-start.6 = (bf16[32,256]{1,0:T(8,128)(2,1)S(1)}, bf16[32,256]{1,0:T(8,128)(2,1)S(1)}, u32[]{:S(2)}, u32[]{:S(2)}) collective-permute-start(bf16[32,256]{1,0:T(8,128)(2,1)S(1)} %get-tuple-element.34), channel_id=1, source_target_pairs={{0,7},{1,0},{2,1},{3,2},{4,3},{5,4},{6,5},{7,6},{8,15},{9,8},{10,9... | collective-permute-start | bytes 49160 | tf_op jit(solution)/shard_map/ppermute | solution.py:312
  45.0 0.7 copy-start.4
  45.7 11.3 %collective-permute-start.9 = (bf16[272,256]{1,0:T(8,128)(2,1)S(1)}, bf16[272,256]{1,0:T(8,128)(2,1)S(1)}, u32[]{:S(2)}, u32[]{:S(2)}) collective-permute-start(bf16[272,256]{1,0:T(8,128)(2,1)S(1)} %assemble.1.own), channel_id=1, source_target_pairs={{0,48},{8,56},{16,64},{24,72},{32,80},{40,88},{48,96},{56,104},{64... | collective-permute-start | bytes 417800 | tf_op jit(solution)/shard_map/ppermute | solution.py:298
  50.6 10.4 %collective-permute-start.8 = (bf16[272,256]{1,0:T(8,128)(2,1)S(1)}, bf16[272,256]{1,0:T(8,128)(2,1)S(1)}, u32[]{:S(2)}, u32[]{:S(2)}) collective-permute-start(bf16[272,256]{1,0:T(8,128)(2,1)S(1)} %assemble.1.own), channel_id=1, source_target_pairs={{0,32},{8,40},{16,48},{24,56},{32,64},{40,72},{48,80},{56,88},{64,... | collective-permute-start | bytes 417800 | tf_op jit(solution)/shard_map/ppermute | solution.py:298
  54.1 9.1 %collective-permute-start.7 = (bf16[272,256]{1,0:T(8,128)(2,1)S(1)}, bf16[272,256]{1,0:T(8,128)(2,1)S(1)}, u32[]{:S(2)}, u32[]{:S(2)}) collective-permute-start(bf16[272,256]{1,0:T(8,128)(2,1)S(1)} %assemble.1.own), channel_id=1, source_target_pairs={{0,16},{8,24},{16,32},{24,40},{32,48},{40,56},{48,64},{56,72},{64,... | collective-permute-start | bytes 417800 | tf_op jit(solution)/shard_map/ppermute | solution.py:298
  63.2 2.0 %collective-permute-start.10 = (bf16[4,272,256]{2,1,0:T(8,128)(2,1)S(1)}, bf16[4,272,256]{2,1,0:T(8,128)(2,1)S(1)}, u32[]{:S(2)}, u32[]{:S(2)}) collective-permute-start(bf16[4,272,256]{2,1,0:T(8,128)(2,1)S(1)} %pad_maximum_fusion), channel_id=1, source_target_pairs={{0,8},{8,0},{16,24},{24,16},{32,40},{40,32},{48,56},{56,48},{64,72... | collective-permute-start | bytes 1671176 | tf_op jit(solution)/shard_map/ppermute | solution.py:303
  87.8 0.8 copy-start.5
  88.6 4.6 %copy-start.6 = (bf16[4,256,256]{2,1,0:T(8,128)(2,1)S(1)}, bf16[4,256,256]{2,1,0:T(8,128)(2,1)}, u32[]{:S(2)}) copy-start(bf16[4,256,256]{2,1,0:T(8,128)(2,1)} %copy-done.5) | copy-start | bytes 1572868
  88.6 41.0 %all-to-all-start.1 = ((bf16[8,32,2048]{2,1,0:T(8,128)(2,1)}), bf16[8,32,2048]{2,1,0:T(8,128)(2,1)S(1)}, u32[]{:S(2)}, u32[]{:S(2)}) async-start(bf16[8,32,2048]{2,1,0:T(8,128)(2,1)} %bitcast.8), calls=%async_computation.1 | async-start | bytes 2097152 | tf_op jit(solution)/shard_map/all_to_all | solution.py:307
  93.2 2.0 %collective-permute-start.11 = (bf16[4,256,256]{2,1,0:T(8,128)(2,1)S(1)}, bf16[4,256,256]{2,1,0:T(8,128)(2,1)S(1)}, u32[]{:S(2)}, u32[]{:S(2)}) collective-permute-start(bf16[4,256,256]{2,1,0:T(8,128)(2,1)S(1)} %copy-done.6), channel_id=1, source_target_pairs={{0,8},{8,0},{16,24},{24,16},{32,40},{40,32},{48,56},{56,48},{64,72... | collective-permute-start | bytes 1572872 | tf_op jit(solution)/shard_map/ppermute | solution.py:303
  95.4 11.5 %collective-permute-start.14 = (bf16[256,256]{1,0:T(8,128)(2,1)S(1)}, bf16[256,256]{1,0:T(8,128)(2,1)S(1)}, u32[]{:S(2)}, u32[]{:S(2)}) collective-permute-start(bf16[256,256]{1,0:T(8,128)(2,1)S(1)} %get-tuple-element.52), channel_id=1, source_target_pairs={{48,0},{56,8},{64,16},{72,24},{80,32},{88,40},{96,48},{104,56},{11... | collective-permute-start | bytes 393224 | tf_op jit(solution)/shard_map/ppermute | solution.py:298
  97.4 9.5 %collective-permute-start.13 = (bf16[256,256]{1,0:T(8,128)(2,1)S(1)}, bf16[256,256]{1,0:T(8,128)(2,1)S(1)}, u32[]{:S(2)}, u32[]{:S(2)}) collective-permute-start(bf16[256,256]{1,0:T(8,128)(2,1)S(1)} %get-tuple-element.53), channel_id=1, source_target_pairs={{32,0},{40,8},{48,16},{56,24},{64,32},{72,40},{80,48},{88,56},{96,... | collective-permute-start | bytes 393224 | tf_op jit(solution)/shard_map/ppermute | solution.py:298
  99.4 10.1 %collective-permute-start.12 = (bf16[256,256]{1,0:T(8,128)(2,1)S(1)}, bf16[256,256]{1,0:T(8,128)(2,1)S(1)}, u32[]{:S(2)}, u32[]{:S(2)}) collective-permute-start(bf16[256,256]{1,0:T(8,128)(2,1)S(1)} %get-tuple-element.54), channel_id=1, source_target_pairs={{16,0},{24,8},{32,16},{40,24},{48,32},{56,40},{64,48},{72,56},{80,... | collective-permute-start | bytes 393224 | tf_op jit(solution)/shard_map/ppermute | solution.py:298
  109.6 12.1 %collective-permute-start.15 = (bf16[32,256]{1,0:T(8,128)(2,1)S(1)}, bf16[32,256]{1,0:T(8,128)(2,1)S(1)}, u32[]{:S(2)}, u32[]{:S(2)}) collective-permute-start(bf16[32,256]{1,0:T(8,128)(2,1)S(1)} %get-tuple-element.41), channel_id=1, source_target_pairs={{0,1},{1,2},{2,3},{3,4},{4,5},{5,6},{6,7},{7,0},{8,9},{9,10},{10,1... | collective-permute-start | bytes 49160 | tf_op jit(solution)/shard_map/ppermute | solution.py:312
  111.6 13.7 %collective-permute-start.16 = (bf16[32,256]{1,0:T(8,128)(2,1)S(1)}, bf16[32,256]{1,0:T(8,128)(2,1)S(1)}, u32[]{:S(2)}, u32[]{:S(2)}) collective-permute-start(bf16[32,256]{1,0:T(8,128)(2,1)S(1)} %get-tuple-element.42), channel_id=1, source_target_pairs={{0,2},{1,3},{2,4},{3,5},{4,6},{5,7},{6,0},{7,1},{8,10},{9,11},{10,... | collective-permute-start | bytes 49160 | tf_op jit(solution)/shard_map/ppermute | solution.py:312
  114.0 12.8 %collective-permute-start.17 = (bf16[32,256]{1,0:T(8,128)(2,1)S(1)}, bf16[32,256]{1,0:T(8,128)(2,1)S(1)}, u32[]{:S(2)}, u32[]{:S(2)}) collective-permute-start(bf16[32,256]{1,0:T(8,128)(2,1)S(1)} %get-tuple-element.43), channel_id=1, source_target_pairs={{0,3},{1,4},{2,5},{3,6},{4,7},{5,0},{6,1},{7,2},{8,11},{9,12},{10,... | collective-permute-start | bytes 49160 | tf_op jit(solution)/shard_map/ppermute | solution.py:312
  116.6 10.1 %collective-permute-start.18 = (bf16[32,256]{1,0:T(8,128)(2,1)S(1)}, bf16[32,256]{1,0:T(8,128)(2,1)S(1)}, u32[]{:S(2)}, u32[]{:S(2)}) collective-permute-start(bf16[32,256]{1,0:T(8,128)(2,1)S(1)} %get-tuple-element.44), channel_id=1, source_target_pairs={{0,4},{1,5},{2,6},{3,7},{4,0},{5,1},{6,2},{7,3},{8,12},{9,13},{10,... | collective-permute-start | bytes 49160 | tf_op jit(solution)/shard_map/ppermute | solution.py:312
  119.0 7.7 %collective-permute-start.19 = (bf16[32,256]{1,0:T(8,128)(2,1)S(1)}, bf16[32,256]{1,0:T(8,128)(2,1)S(1)}, u32[]{:S(2)}, u32[]{:S(2)}) collective-permute-start(bf16[32,256]{1,0:T(8,128)(2,1)S(1)} %get-tuple-element.45), channel_id=1, source_target_pairs={{0,5},{1,6},{2,7},{3,0},{4,1},{5,2},{6,3},{7,4},{8,13},{9,14},{10,... | collective-permute-start | bytes 49160 | tf_op jit(solution)/shard_map/ppermute | solution.py:312
  121.7 5.1 %collective-permute-start.20 = (bf16[32,256]{1,0:T(8,128)(2,1)S(1)}, bf16[32,256]{1,0:T(8,128)(2,1)S(1)}, u32[]{:S(2)}, u32[]{:S(2)}) collective-permute-start(bf16[32,256]{1,0:T(8,128)(2,1)S(1)} %get-tuple-element.46), channel_id=1, source_target_pairs={{0,6},{1,7},{2,0},{3,1},{4,2},{5,3},{6,4},{7,5},{8,14},{9,15},{10,... | collective-permute-start | bytes 49160 | tf_op jit(solution)/shard_map/ppermute | solution.py:312
  125.3 3.7 %collective-permute-start.21 = (bf16[32,256]{1,0:T(8,128)(2,1)S(1)}, bf16[32,256]{1,0:T(8,128)(2,1)S(1)}, u32[]{:S(2)}, u32[]{:S(2)}) collective-permute-start(bf16[32,256]{1,0:T(8,128)(2,1)S(1)} %get-tuple-element.47), channel_id=1, source_target_pairs={{0,7},{1,0},{2,1},{3,2},{4,3},{5,4},{6,5},{7,6},{8,15},{9,8},{10,9... | collective-permute-start | bytes 49160 | tf_op jit(solution)/shard_map/ppermute | solution.py:312

commit v3 on v1

v3 whole, which is shorter than its diff:
```python
import functools
import math

import jax
import jax.numpy as jnp
from jax import lax
from jax.experimental import pallas as pl
from jax.experimental.pallas import tpu as pltpu
from jax.sharding import PartitionSpec as P


HEAD = 128
WINDOW = 1536
BLOCK = 256
SLOTS = 4
OFFSETS = (0, 2, 4, 6, 1, 3, 5)
CHUNKS = len(OFFSETS)
DOC_ROWS = 16
PIECE = 64
SCALE = HEAD ** (-0.5)
EXP2_SCALE = SCALE * math.log2(math.e)
MASKED = -1e30
NT = (((1,), (1,)), ((), ()))
VMEM = pl.BlockSpec(memory_space=pltpu.VMEM)
SMALL = pltpu.CompilerParams(vmem_limit_bytes=8 * 1024 * 1024)


def dot(a, b, dims=(((1,), (0,)), ((), ()))):
    return lax.dot_general(a, b, dims, preferred_element_type=jnp.float32)


def run(copies):
    for copy in copies:
        copy.start()
    for copy in copies:
        copy.wait()


def pack_body(parts, *refs):
    ins, o_ref, sems = refs[:-2], refs[-2], refs[-1]
    copies = []
    for part in range(parts):
        start = 0
        for ref in ins:
            width = ref.shape[1] // parts
            source, target = ref.at[:, pl.ds(part * width, width)], o_ref.at[part, :, pl.ds(start, width)]
            copies.append(pltpu.make_async_copy(source, target, sems.at[len(copies)]))
            start += width
    run(copies)


def pack(arrays, parts):
    rows, width = arrays[0].shape[0], sum(a.shape[1] for a in arrays)
    return pl.pallas_call(
        functools.partial(pack_body, parts),
        out_shape=jax.ShapeDtypeStruct((parts, rows, width // parts), arrays[0].dtype),
        in_specs=[pl.BlockSpec(memory_space=pl.ANY)] * len(arrays),
        out_specs=VMEM,
        scratch_shapes=[pltpu.SemaphoreType.DMA((parts * len(arrays),))],
        cost_estimate=pl.CostEstimate(flops=rows * width, bytes_accessed=4 * rows * width, transcendentals=0),
    )(*arrays)


def unpack_body(parts, i_ref, *refs):
    outs, sems = refs[:-1], refs[-1]
    copies = []
    for part in range(parts):
        start = 0
        for ref in outs:
            width = ref.shape[1] // parts
            source, target = i_ref.at[part, :, pl.ds(start, width)], ref.at[:, pl.ds(part * width, width)]
            copies.append(pltpu.make_async_copy(source, target, sems.at[len(copies)]))
            start += width
    run(copies)


def unpack(value, widths):
    parts, rows, _ = value.shape
    return pl.pallas_call(
        functools.partial(unpack_body, parts),
        out_shape=tuple(jax.ShapeDtypeStruct((rows, parts * width), value.dtype) for width in widths),
        in_specs=[VMEM],
        out_specs=(pl.BlockSpec(memory_space=pl.ANY),) * len(widths),
        scratch_shapes=[pltpu.SemaphoreType.DMA((parts * len(widths),))],
        compiler_params=SMALL,
        cost_estimate=pl.CostEstimate(flops=value.size, bytes_accessed=4 * value.size, transcendentals=0),
    )(value)


def add_body(dq_ref, base_ref, one_ref, two_ref, three_ref, o_ref):
    width = dq_ref.shape[1]
    o_ref[:, :width] = dq_ref[...]
    total = base_ref[...] + one_ref[...].astype(jnp.float32)
    total = total + two_ref[...].astype(jnp.float32) + three_ref[...].astype(jnp.float32)
    o_ref[:, width:] = total.astype(jnp.bfloat16)


def add(dq, base, others):
    rows, width = dq.shape[0], dq.shape[1] + base.shape[1]
    return pl.pallas_call(
        add_body,
        out_shape=jax.ShapeDtypeStruct((rows, width), jnp.bfloat16),
        in_specs=[VMEM] * 5,
        out_specs=VMEM,
        compiler_params=SMALL,
        cost_estimate=pl.CostEstimate(flops=4 * base.size, bytes_accessed=4 * rows * width, transcendentals=0),
        name="add",
    )(dq, base, *others)


def prepare(core, own, two, four, six, mate, k_s, v_s, kt_s, vt_s, bias_s, dk_s, dv_s):
    first = 1 - core
    docs = []
    for c in range(CHUNKS):
        if c < SLOTS:
            ref = (own, two, four, six)[c]
            rows, doc = ref[:BLOCK, :], ref[BLOCK:, :]
        else:
            slot = first + (c - SLOTS)
            rows, doc = mate[slot, :BLOCK, :], mate[slot, BLOCK:, :]
        docs.append(doc[0:1, :].astype(jnp.float32))
        key, value = rows[:, :HEAD], rows[:, HEAD:]
        k_s[c] = key
        v_s[c] = value
        kt_s[c] = key.astype(jnp.float32).T.astype(jnp.bfloat16)
        vt_s[c] = value.astype(jnp.float32).T.astype(jnp.bfloat16)
    mine = docs[0]
    by_key = jnp.broadcast_to(mine, (BLOCK, BLOCK)).T
    row = lax.broadcasted_iota(jnp.int32, (BLOCK, BLOCK), 0)
    lane = lax.broadcasted_iota(jnp.int32, (BLOCK, BLOCK), 1)
    before = jnp.sum(jnp.where((by_key == mine) & (row < lane), 1.0, 0.0), axis=0, keepdims=True)
    opening = mine[:, 0:1]
    carried = jnp.zeros((1, 1), jnp.float32)
    for c in range(1, CHUNKS):
        carried = carried + jnp.sum(jnp.where(docs[c] == opening, 1.0, 0.0), axis=1, keepdims=True)
    before = before + jnp.where(mine == opening, carried, 0.0)
    before = jnp.minimum(before, WINDOW - 1.0).astype(jnp.int32)
    for c in range(CHUNKS):
        back = lane - row + OFFSETS[c] * BLOCK
        bias_s[c] = jnp.where((back >= 0) & (back <= before), 0.0, MASKED)
    dk_s[...] = jnp.zeros_like(dk_s)
    dv_s[...] = jnp.zeros_like(dv_s)


def scores(query, s_ref, k_s, bias_s):
    top = None
    for c in range(CHUNKS):
        s = dot(k_s[c], query, NT) * EXP2_SCALE + bias_s[c]
        s_ref[c] = s
        most = jnp.max(s, axis=0, keepdims=True)
        top = most if top is None else jnp.maximum(top, most)
    return top


def weigh(c, s_ref, top, total):
    for r in range(0, BLOCK, PIECE):
        p = jnp.exp2(s_ref[c, r : r + PIECE, :] - top)
        s_ref[c, r : r + PIECE, :] = p
        part = jnp.sum(p, axis=0, keepdims=True)
        total = part if total is None else total + part
    return total


def collect(grad, s_ref, total, att_ref, columns, stat_ref, vt_s, dv_s):
    inverse = 1.0 / total
    out = None
    for c in range(CHUNKS):
        p16 = (s_ref[c] * inverse).astype(jnp.bfloat16)
        term = dot(vt_s[c], p16)
        out = term if out is None else out + term
        dv_s[c] += dot(p16, grad)
    out16 = out.astype(jnp.bfloat16).astype(jnp.float32)
    att_ref[:, columns] = out16.T.astype(jnp.bfloat16)
    delta = jnp.sum(grad.astype(jnp.float32).T * out16, axis=0, keepdims=True)
    stat_ref[0:1, :] = inverse
    stat_ref[1:2, :] = delta


def step(ahead, behind, q_ref, g_ref, att_ref, dq_ref, k_s, v_s, kt_s, vt_s, bias_s, dk_s, dv_s):
    columns = lambda head: pl.ds(pl.multiple_of(head * HEAD, HEAD), HEAD)
    total = dq = None
    if ahead:
        head, s_ref, stat_ref = ahead
        grad = g_ref[:, columns(head)]
        top = scores(q_ref[:, columns(head)], s_ref, k_s, bias_s)
    if behind:
        last, p_ref, last_ref = behind
        last_query, last_grad = q_ref[:, columns(last)], g_ref[:, columns(last)]
        inverse, delta = last_ref[0:1, :], last_ref[1:2, :]
        coming = dot(v_s[0], last_grad, NT)
    for c in range(CHUNKS):
        if behind:
            dp = coming
            if c + 1 < CHUNKS:
                coming = dot(v_s[c + 1], last_grad, NT)
        if ahead:
            total = weigh(c, s_ref, top, total)
        if behind:
            ds = (p_ref[c] * ((dp - delta) * inverse)).astype(jnp.bfloat16)
            term = dot(kt_s[c], ds)
            dq = term if dq is None else dq + term
            dk_s[c] += dot(ds, last_query)
    if behind:
        dq_ref[:, columns(last)] = (dq * SCALE).T.astype(jnp.bfloat16)
    if ahead:
        collect(grad, s_ref, total, att_ref, columns(head), stat_ref, vt_s, dv_s)


def attention_body(core_ref, q_ref, g_ref, own, two, four, six, mate, att_ref, dq_ref, mine_ref, mate_ref, k_s, v_s, kt_s, vt_s, bias_s, dk_s, dv_s, even_s, odd_s, even_t, odd_t):
    core = core_ref[0]
    heads = dq_ref.shape[1] // HEAD
    prepare(core, own, two, four, six, mate, k_s, v_s, kt_s, vt_s, bias_s, dk_s, dv_s)
    refs = (q_ref, g_ref, att_ref, dq_ref, k_s, v_s, kt_s, vt_s, bias_s, dk_s, dv_s)
    step((0, even_s, even_t), None, *refs)

    def pair(i, _):
        head = 2 * i
        step((head + 1, odd_s, odd_t), (head, even_s, even_t), *refs)
        step((head + 2, even_s, even_t), (head + 1, odd_s, odd_t), *refs)
        return 0

    lax.fori_loop(0, heads // 2 - 1, pair, 0)
    step((heads - 1, odd_s, odd_t), (heads - 2, even_s, even_t), *refs)
    step(None, (heads - 1, odd_s, odd_t), *refs)
    for t in range(SLOTS):
        mine_ref[t, :, :HEAD] = dk_s[t] * SCALE
        mine_ref[t, :, HEAD:] = dv_s[t]
    first = 1 - core
    mate_ref[3 - 3 * first] = jnp.zeros((BLOCK, 2 * HEAD), jnp.bfloat16)
    for t in range(SLOTS - 1):
        mate_ref[first + t, :, :HEAD] = (dk_s[SLOTS + t] * SCALE).astype(jnp.bfloat16)
        mate_ref[first + t, :, HEAD:] = dv_s[SLOTS + t].astype(jnp.bfloat16)


def attention(core, q, g, own, two, four, six, mate):
    heads = g.shape[1] // HEAD
    work = heads * CHUNKS * BLOCK * BLOCK
    scratch = lambda dims, kind: pltpu.VMEM(dims, kind)
    return pl.pallas_call(
        attention_body,
        out_shape=(
            jax.ShapeDtypeStruct(g.shape, jnp.bfloat16),
            jax.ShapeDtypeStruct(g.shape, jnp.bfloat16),
            jax.ShapeDtypeStruct((SLOTS, BLOCK, 2 * HEAD), jnp.float32),
            jax.ShapeDtypeStruct((SLOTS, BLOCK, 2 * HEAD), jnp.bfloat16),
        ),
        in_specs=[pl.BlockSpec(memory_space=pltpu.SMEM)] + [VMEM] * 7,
        out_specs=(VMEM,) * 4,
        scratch_shapes=[
            scratch((CHUNKS, BLOCK, HEAD), jnp.bfloat16),
            scratch((CHUNKS, BLOCK, HEAD), jnp.bfloat16),
            scratch((CHUNKS, HEAD, BLOCK), jnp.bfloat16),
            scratch((CHUNKS, HEAD, BLOCK), jnp.bfloat16),
            scratch((CHUNKS, BLOCK, BLOCK), jnp.float32),
            scratch((CHUNKS, BLOCK, HEAD), jnp.float32),
            scratch((CHUNKS, BLOCK, HEAD), jnp.float32),
            scratch((CHUNKS, BLOCK, BLOCK), jnp.float32),
            scratch((CHUNKS, BLOCK, BLOCK), jnp.float32),
            scratch((8, BLOCK), jnp.float32),
            scratch((8, BLOCK), jnp.float32),
        ],
        compiler_params=pltpu.CompilerParams(vmem_limit_bytes=16 * 1024 * 1024),
        cost_estimate=pl.CostEstimate(flops=12 * work * HEAD, bytes_accessed=5 * 1024 * 1024, transcendentals=work),
        name="attention",
    )(core, q, g, own, two, four, six, mate)


def shift(value, steps):
    count = lax.axis_size("ctx")
    return lax.ppermute(value, "ctx", [(s, s + steps) for s in range(max(0, -steps), min(count, count - steps))])


def swap(value):
    count = lax.axis_size("ctx")
    return lax.ppermute(value, "ctx", [(s, s ^ 1) for s in range(count)])


def over_head(value):
    return lax.all_to_all(value, "head", split_axis=0, concat_axis=0, tiled=True)


def local(queries, key_heads, value_head_array, out_grad, doc_ids):
    parts = lax.axis_size("head")
    core = (lax.axis_index("ctx") % 2).astype(jnp.int32).reshape(1)
    q = over_head(pack((queries, key_heads, value_head_array), parts)).reshape(BLOCK, -1)
    packed = pack((out_grad,), parts)
    g = over_head(packed).reshape(BLOCK, -1)
    docs = jnp.pad((doc_ids + 1).astype(jnp.bfloat16)[None, :], ((0, DOC_ROWS - 1), (0, 0)))
    own = jnp.concatenate([q[:, -2 * HEAD :], docs], axis=0)
    two, four, six = (shift(own, steps) for steps in (2, 4, 6))
    mate = swap(jnp.stack([own, two, four, six]))
    attended, dq, mine, sent = attention(core, q, g, own, two, four, six, mate)
    attended = over_head(attended.reshape(parts, -1, attended.shape[1]))
    sent = swap(sent)
    sums = mine + sent.astype(jnp.float32)
    rounded = sums.astype(jnp.bfloat16)
    back = [shift(rounded[t], -2 * t) for t in range(1, SLOTS)]
    grads = add(dq, sums[0], back)
    grads = over_head(grads.reshape(parts, -1, grads.shape[1]))
    (attended,) = unpack(attended, (attended.shape[2],))
    query_grad, key_grad, value_grad = unpack(grads, (dq.shape[1], HEAD, HEAD))
    return attended, query_grad, key_grad, value_grad


def solution(mesh):
    rows = P(("ctx", "head"), None)

    return jax.shard_map(
        local,
        mesh=mesh,
        in_specs=(rows, rows, rows, rows, P("ctx")),
        out_specs=(rows, rows, rows, rows),
        check_vma=False,
    )
```

time: 136 us -> 125 us (0.919)
  blocking collectives: 11.5 us -> 0 us
  starting transfers between devices: 35.7 us -> 41.3 us
  Pallas kernels: 26.3 us -> 23.4 us
  local copies, waits for them, and re-layouts: 3.79 us -> 1.93 us
    all_to_all x1 -> x0, blocking collectives: 11.5 us -> none  [over_head(): lax.all_to_all(value, 'head', split_axis=0, concat_axis=0, tiled=True)]
    all_to_all x3 -> x4, starting transfers between devices: 15.6 us -> 23 us  [over_head(): lax.all_to_all(value, 'head', split_axis=0, concat_axis=0, tiled=True)]
    pallas_call x5 -> x6, Pallas kernels: 26.3 us -> 23.4 us  [the longest x1 16.3 us: attention(): pl.pallas_call(attention_body, out_shape=(jax.ShapeDtypeStruct(g.shape, j...]
    ppermute x6, starting transfers between devices: 20 us -> 18 us  [shift(): lax.ppermute(value, 'ctx', [(s, s + steps) for s in range(max(0, -steps),...]
    ppermute x2, waiting for transfers between devices: 3.84 us -> 1.92 us  [swap(): return lax.ppermute(value, 'ctx', [(s, s ^ 1) for s in range(count)])]
    unnamed x10 -> x6, local copies, waits for them, and re-layouts: 3.75 us -> 1.87 us
    all_to_all x3 -> x4, waiting for transfers between devices: 40 us -> 40.4 us  [over_head(): lax.all_to_all(value, 'head', split_axis=0, concat_axis=0, tiled=True)]
  transfers between devices with their start and end apart: 11 -> 12, of which waited for: 8 -> 8; matrix products, arithmetic and copies ran while one was open for 0% -> 0% of each run, Pallas kernels for 1% -> 3%
where the time goes in v3:
time: 125 us; the launch traced here: 124 us
  waiting for transfers between devices  56 us (45%)
  starting transfers between devices  41.3 us (33%)
  Pallas kernels  23.4 us (19%)
  local copies, waits for them, and re-layouts  1.93 us (2%)
    all_to_all x4, waiting for transfers between devices, over_head(): lax.all_to_all(value, 'head', split_axis=0, concat_axis=0, tiled=True)  40.4 us
    all_to_all x4, starting transfers between devices, over_head(): lax.all_to_all(value, 'head', split_axis=0, concat_axis=0, tiled=True)  23 us
    ppermute x6, starting transfers between devices, shift(): lax.ppermute(value, 'ctx', [(s, s + steps) for s in range(max(0, -steps),...  18 us
    pallas_call x1, Pallas kernels, attention(): pl.pallas_call(attention_body, out_shape=(jax.ShapeDtypeStruct(g.shape, j...  16.3 us
    ppermute x6, waiting for transfers between devices, shift(): lax.ppermute(value, 'ctx', [(s, s + steps) for s in range(max(0, -steps),...  13.6 us
    pallas_call x2, Pallas kernels, pack(): pl.pallas_call(functools.partial(pack_body, parts), out_shape=jax.ShapeDt...  4.2 us
  transfers between devices with their start and end apart: 12, of which 8 were waited for; matrix products, arithmetic and copies ran while one was open for 0% of the time, Pallas kernels for 3%

profile of v3, /device:TPU:2, one launch (start us, length us, event | category | flops | bytes accessed | tf_op | source)
XLA Modules:
  0.0 123.6 jit_solution(17744743349459875496)
XLA Ops:
  0.6 2.3 %shard_map.84 = bf16[8,32,1280]{2,1,0:T(8,128)(2,1)} custom-call(bf16[32,8192]{1,0:T(8,128)(2,1)} %refs_0_.2, bf16[32,1024]{1,0:T(8,128)(2,1)} %refs_1_.1, bf16[32,1024]{1,0:T(8,128)(2,1)} %refs_2_.1), custom_call_target="tpu_custom_call" | custom-call | flops 327680 | bytes 1310720 | tf_op jit(solution)/shard_map/pallas_call | solution.py:54
  2.9 8.5 %all-to-all-start = ((bf16[8,32,1280]{2,1,0:T(8,128)(2,1)}), bf16[8,32,1280]{2,1,0:T(8,128)(2,1)S(1)}, u32[]{:S(2)}, u32[]{:S(2)}) async-start(bf16[8,32,1280]{2,1,0:T(8,128)(2,1)} %shard_map.84), calls=%async_computation | async-start | bytes 1310720 | tf_op jit(solution)/shard_map/all_to_all | solution.py:279
  11.4 0.0 copy-start.2
  11.4 1.9 %shard_map.85 = bf16[8,32,1024]{2,1,0:T(8,128)(2,1)} custom-call(bf16[32,8192]{1,0:T(8,128)(2,1)} %refs_0_.3), custom_call_target="tpu_custom_call" | custom-call | flops 262144 | bytes 1048576 | tf_op jit(solution)/shard_map/pallas_call | solution.py:54
  13.3 0.0 copy-done.2
  13.4 18.3 %all-to-all-done = bf16[8,32,1280]{2,1,0:T(8,128)(2,1)S(1)} async-done(((bf16[8,32,1280]{2,1,0:T(8,128)(2,1)}), bf16[8,32,1280]{2,1,0:T(8,128)(2,1)S(1)}, u32[]{:S(2)}, u32[]{:S(2)}) %all-to-all-start) | async-done | bytes 655392 | tf_op jit(solution)/shard_map/all_to_all | solution.py:279
  31.7 3.5 %all-to-all-start.1 = ((bf16[8,32,1024]{2,1,0:T(8,128)(2,1)}), bf16[8,32,1024]{2,1,0:T(8,128)(2,1)S(1)}, u32[]{:S(2)}, u32[]{:S(2)}) async-start(bf16[8,32,1024]{2,1,0:T(8,128)(2,1)} %shard_map.85), calls=%async_computation.1 | async-start | bytes 1048576 | tf_op jit(solution)/shard_map/all_to_all | solution.py:279
  35.2 4.9 %collective-permute-start.2 = (bf16[272,256]{1,0:T(8,128)(2,1)S(1)}, bf16[272,256]{1,0:T(8,128)(2,1)S(1)}, u32[]{:S(2)}, u32[]{:S(2)}) collective-permute-start(bf16[272,256]{1,0:T(8,128)(2,1)S(1)} %get-tuple-element.24.own), channel_id=1, source_target_pairs={{0,48},{8,56},{16,64},{24,72},{32,80},{40,88},{48,96},{56,104},{64... | collective-permute-start | bytes 417800 | tf_op jit(solution)/shard_map/ppermute | solution.py:270
  40.2 3.5 %collective-permute-start.1 = (bf16[272,256]{1,0:T(8,128)(2,1)S(1)}, bf16[272,256]{1,0:T(8,128)(2,1)S(1)}, u32[]{:S(2)}, u32[]{:S(2)}) collective-permute-start(bf16[272,256]{1,0:T(8,128)(2,1)S(1)} %get-tuple-element.24.own), channel_id=1, source_target_pairs={{0,32},{8,40},{16,48},{24,56},{32,64},{40,72},{48,80},{56,88},{64,... | collective-permute-start | bytes 417800 | tf_op jit(solution)/shard_map/ppermute | solution.py:270
  43.6 2.9 %collective-permute-start = (bf16[272,256]{1,0:T(8,128)(2,1)S(1)}, bf16[272,256]{1,0:T(8,128)(2,1)S(1)}, u32[]{:S(2)}, u32[]{:S(2)}) collective-permute-start(bf16[272,256]{1,0:T(8,128)(2,1)S(1)} %get-tuple-element.24.own), channel_id=1, source_target_pairs={{0,16},{8,24},{16,32},{24,40},{32,48},{40,56},{48,64},{56,72},{64,... | collective-permute-start | bytes 417800 | tf_op jit(solution)/shard_map/ppermute | solution.py:270
  46.5 0.0 collective-permute-done.2.six
  46.5 3.5 %collective-permute-done.1.four = bf16[272,256]{1,0:T(8,128)(2,1)S(1)} collective-permute-done((bf16[272,256]{1,0:T(8,128)(2,1)S(1)}, bf16[272,256]{1,0:T(8,128)(2,1)S(1)}, u32[]{:S(2)}, u32[]{:S(2)}) %collective-permute-start.1) | collective-permute-done | bytes 139296 | tf_op jit(solution)/shard_map/ppermute | solution.py:270
  50.0 2.9 %collective-permute-done.two = bf16[272,256]{1,0:T(8,128)(2,1)S(1)} collective-permute-done((bf16[272,256]{1,0:T(8,128)(2,1)S(1)}, bf16[272,256]{1,0:T(8,128)(2,1)S(1)}, u32[]{:S(2)}, u32[]{:S(2)}) %collective-permute-start) | collective-permute-done | bytes 139296 | tf_op jit(solution)/shard_map/ppermute | solution.py:270
  52.9 0.1 pad_maximum_fusion
  52.9 0.1 collective-permute-start.3
  53.0 0.0 all-to-all-done.1
  53.1 1.9 %collective-permute-done.3.mate = bf16[4,272,256]{2,1,0:T(8,128)(2,1)S(1)} collective-permute-done((bf16[4,272,256]{2,1,0:T(8,128)(2,1)S(1)}, bf16[4,272,256]{2,1,0:T(8,128)(2,1)S(1)}, u32[]{:S(2)}, u32[]{:S(2)}) %collective-permute-start.3) | collective-permute-done | bytes 557088 | tf_op jit(solution)/shard_map/ppermute | solution.py:275
  55.0 0.0 copy-start
  55.0 0.8 copy-done
  55.8 0.0 copy-start.1
  55.8 1.1 copy-done.1
  56.8 16.3 %attention.1 = (bf16[256,1024]{1,0:T(8,128)(2,1)}, bf16[256,1024]{1,0:T(8,128)(2,1)S(1)}, f32[4,256,256]{2,1,0:T(8,128)S(1)}, bf16[4,256,256]{2,1,0:T(8,128)(2,1)}) custom-call(s32[1]{0:T(128)} %bitcast.core_ref, bf16[256,1280]{1,0:T(8,128)(2,1)S(1)} %bitcast.19, bf16[256,1024]{1,0:T(8,128)(2,1)S(1)} %bitcast.20, ...), custom_call_target="tpu_custom_call" | custom-call | flops 5637144576 | bytes 5242880 | tf_op jit(solution)/shard_map/attention/pallas_call | solution.py:239
  73.2 0.1 collective-permute-start.4
  73.3 7.0 %all-to-all-start.2 = ((bf16[8,32,1024]{2,1,0:T(8,128)(2,1)}), bf16[8,32,1024]{2,1,0:T(8,128)(2,1)S(1)}, u32[]{:S(2)}, u32[]{:S(2)}) async-start(bf16[8,32,1024]{2,1,0:T(8,128)(2,1)} %bitcast.7), calls=%async_computation.2 | async-start | bytes 1048576 | tf_op jit(solution)/shard_map/all_to_all | solution.py:279
  80.2 0.0 collective-permute-done.4
  80.3 0.1 fusion.3
  80.4 1.9 %collective-permute-start.7 = (bf16[256,256]{1,0:T(8,128)(2,1)S(1)}, bf16[256,256]{1,0:T(8,128)(2,1)S(1)}, u32[]{:S(2)}, u32[]{:S(2)}) collective-permute-start(bf16[256,256]{1,0:T(8,128)(2,1)S(1)} %get-tuple-element.20), channel_id=1, source_target_pairs={{48,0},{56,8},{64,16},{72,24},{80,32},{88,40},{96,48},{104,56},{11... | collective-permute-start | bytes 393224 | tf_op jit(solution)/shard_map/ppermute | solution.py:270
  82.4 2.0 %collective-permute-start.6 = (bf16[256,256]{1,0:T(8,128)(2,1)S(1)}, bf16[256,256]{1,0:T(8,128)(2,1)S(1)}, u32[]{:S(2)}, u32[]{:S(2)}) collective-permute-start(bf16[256,256]{1,0:T(8,128)(2,1)S(1)} %get-tuple-element.21), channel_id=1, source_target_pairs={{32,0},{40,8},{48,16},{56,24},{64,32},{72,40},{80,48},{88,56},{96,... | collective-permute-start | bytes 393224 | tf_op jit(solution)/shard_map/ppermute | solution.py:270
  84.4 2.8 %collective-permute-start.5 = (bf16[256,256]{1,0:T(8,128)(2,1)S(1)}, bf16[256,256]{1,0:T(8,128)(2,1)S(1)}, u32[]{:S(2)}, u32[]{:S(2)}) collective-permute-start(bf16[256,256]{1,0:T(8,128)(2,1)S(1)} %get-tuple-element.22), channel_id=1, source_target_pairs={{16,0},{24,8},{32,16},{40,24},{48,32},{56,40},{64,48},{72,56},{80,... | collective-permute-start | bytes 393224 | tf_op jit(solution)/shard_map/ppermute | solution.py:270
  87.2 4.6 %collective-permute-done.7.three_ref = bf16[256,256]{1,0:T(8,128)(2,1)S(1)} collective-permute-done((bf16[256,256]{1,0:T(8,128)(2,1)S(1)}, bf16[256,256]{1,0:T(8,128)(2,1)S(1)}, u32[]{:S(2)}, u32[]{:S(2)}) %collective-permute-start.7) | collective-permute-done | bytes 131104 | tf_op jit(solution)/shard_map/ppermute | solution.py:270
  91.9 0.0 collective-permute-done.6.two_ref
  91.9 2.6 %collective-permute-done.5.one_ref = bf16[256,256]{1,0:T(8,128)(2,1)S(1)} collective-permute-done((bf16[256,256]{1,0:T(8,128)(2,1)S(1)}, bf16[256,256]{1,0:T(8,128)(2,1)S(1)}, u32[]{:S(2)}, u32[]{:S(2)}) %collective-permute-start.5) | collective-permute-done | bytes 131104 | tf_op jit(solution)/shard_map/ppermute | solution.py:270
  94.5 1.0 add.24
  95.5 2.8 %all-to-all-done.2.i_ref = bf16[8,32,1024]{2,1,0:T(8,128)(2,1)S(1)} async-done(((bf16[8,32,1024]{2,1,0:T(8,128)(2,1)}), bf16[8,32,1024]{2,1,0:T(8,128)(2,1)S(1)}, u32[]{:S(2)}, u32[]{:S(2)}) %all-to-all-start.2) | async-done | bytes 524320 | tf_op jit(solution)/shard_map/all_to_all | solution.py:279
  98.3 4.1 %all-to-all-start.3 = ((bf16[8,32,1280]{2,1,0:T(8,128)(2,1)}), bf16[8,32,1280]{2,1,0:T(8,128)(2,1)S(1)}, u32[]{:S(2)}, u32[]{:S(2)}) async-start(bf16[8,32,1280]{2,1,0:T(8,128)(2,1)} %bitcast.12), calls=%async_computation.3 | async-start | bytes 1310720 | tf_op jit(solution)/shard_map/all_to_all | solution.py:279
  102.4 0.8 shard_map.86
  103.3 19.3 %all-to-all-done.3.i_ref = bf16[8,32,1280]{2,1,0:T(8,128)(2,1)S(1)} async-done(((bf16[8,32,1280]{2,1,0:T(8,128)(2,1)}), bf16[8,32,1280]{2,1,0:T(8,128)(2,1)S(1)}, u32[]{:S(2)}, u32[]{:S(2)}) %all-to-all-start.3) | async-done | bytes 655392 | tf_op jit(solution)/shard_map/all_to_all | solution.py:279
  122.5 1.0 shard_map.87
  (6 shorter events, 0.1 us)
Async XLA Ops:
  2.9 28.8 %all-to-all-start = ((bf16[8,32,1280]{2,1,0:T(8,128)(2,1)}), bf16[8,32,1280]{2,1,0:T(8,128)(2,1)S(1)}, u32[]{:S(2)}, u32[]{:S(2)}) async-start(bf16[8,32,1280]{2,1,0:T(8,128)(2,1)} %shard_map.84), calls=%async_computation | async-start | bytes 1310720 | tf_op jit(solution)/shard_map/all_to_all | solution.py:279
  11.4 1.9 %copy-start.2 = (s32[256]{0:T(256)S(1)}, s32[256]{0:T(256)}, u32[]{:S(2)}) copy-start(s32[256]{0:T(256)} %param.9) | copy-start | bytes 3076
  31.7 21.4 %all-to-all-start.1 = ((bf16[8,32,1024]{2,1,0:T(8,128)(2,1)}), bf16[8,32,1024]{2,1,0:T(8,128)(2,1)S(1)}, u32[]{:S(2)}, u32[]{:S(2)}) async-start(bf16[8,32,1024]{2,1,0:T(8,128)(2,1)} %shard_map.85), calls=%async_computation.1 | async-start | bytes 1048576 | tf_op jit(solution)/shard_map/all_to_all | solution.py:279
  35.2 11.3 %collective-permute-start.2 = (bf16[272,256]{1,0:T(8,128)(2,1)S(1)}, bf16[272,256]{1,0:T(8,128)(2,1)S(1)}, u32[]{:S(2)}, u32[]{:S(2)}) collective-permute-start(bf16[272,256]{1,0:T(8,128)(2,1)S(1)} %get-tuple-element.24.own), channel_id=1, source_target_pairs={{0,48},{8,56},{16,64},{24,72},{32,80},{40,88},{48,96},{56,104},{64... | collective-permute-start | bytes 417800 | tf_op jit(solution)/shard_map/ppermute | solution.py:270
  40.2 9.8 %collective-permute-start.1 = (bf16[272,256]{1,0:T(8,128)(2,1)S(1)}, bf16[272,256]{1,0:T(8,128)(2,1)S(1)}, u32[]{:S(2)}, u32[]{:S(2)}) collective-permute-start(bf16[272,256]{1,0:T(8,128)(2,1)S(1)} %get-tuple-element.24.own), channel_id=1, source_target_pairs={{0,32},{8,40},{16,48},{24,56},{32,64},{40,72},{48,80},{56,88},{64,... | collective-permute-start | bytes 417800 | tf_op jit(solution)/shard_map/ppermute | solution.py:270
  43.6 9.2 %collective-permute-start = (bf16[272,256]{1,0:T(8,128)(2,1)S(1)}, bf16[272,256]{1,0:T(8,128)(2,1)S(1)}, u32[]{:S(2)}, u32[]{:S(2)}) collective-permute-start(bf16[272,256]{1,0:T(8,128)(2,1)S(1)} %get-tuple-element.24.own), channel_id=1, source_target_pairs={{0,16},{8,24},{16,32},{24,40},{32,48},{40,56},{48,64},{56,72},{64,... | collective-permute-start | bytes 417800 | tf_op jit(solution)/shard_map/ppermute | solution.py:270
  52.9 2.0 %collective-permute-start.3 = (bf16[4,272,256]{2,1,0:T(8,128)(2,1)S(1)}, bf16[4,272,256]{2,1,0:T(8,128)(2,1)S(1)}, u32[]{:S(2)}, u32[]{:S(2)}) collective-permute-start(bf16[4,272,256]{2,1,0:T(8,128)(2,1)S(1)} %pad_maximum_fusion), channel_id=1, source_target_pairs={{0,8},{8,0},{16,24},{24,16},{32,40},{40,32},{48,56},{56,48},{64,72... | collective-permute-start | bytes 1671176 | tf_op jit(solution)/shard_map/ppermute | solution.py:275
  55.0 0.8 copy-start
  55.8 1.1 copy-start.1
  73.2 7.1 %collective-permute-start.4 = (bf16[4,256,256]{2,1,0:T(8,128)(2,1)}, bf16[4,256,256]{2,1,0:T(8,128)(2,1)S(1)}, u32[]{:S(2)}, u32[]{:S(2)}) collective-permute-start(bf16[4,256,256]{2,1,0:T(8,128)(2,1)} %get-tuple-element.14), channel_id=1, source_target_pairs={{0,8},{8,0},{16,24},{24,16},{32,40},{40,32},{48,56},{56,48},{64,72... | collective-permute-start | bytes 1572872 | tf_op jit(solution)/shard_map/ppermute | solution.py:275
  73.3 25.0 %all-to-all-start.2 = ((bf16[8,32,1024]{2,1,0:T(8,128)(2,1)}), bf16[8,32,1024]{2,1,0:T(8,128)(2,1)S(1)}, u32[]{:S(2)}, u32[]{:S(2)}) async-start(bf16[8,32,1024]{2,1,0:T(8,128)(2,1)} %bitcast.7), calls=%async_computation.2 | async-start | bytes 1048576 | tf_op jit(solution)/shard_map/all_to_all | solution.py:279
  80.4 11.4 %collective-permute-start.7 = (bf16[256,256]{1,0:T(8,128)(2,1)S(1)}, bf16[256,256]{1,0:T(8,128)(2,1)S(1)}, u32[]{:S(2)}, u32[]{:S(2)}) collective-permute-start(bf16[256,256]{1,0:T(8,128)(2,1)S(1)} %get-tuple-element.20), channel_id=1, source_target_pairs={{48,0},{56,8},{64,16},{72,24},{80,32},{88,40},{96,48},{104,56},{11... | collective-permute-start | bytes 393224 | tf_op jit(solution)/shard_map/ppermute | solution.py:270
  82.4 9.5 %collective-permute-start.6 = (bf16[256,256]{1,0:T(8,128)(2,1)S(1)}, bf16[256,256]{1,0:T(8,128)(2,1)S(1)}, u32[]{:S(2)}, u32[]{:S(2)}) collective-permute-start(bf16[256,256]{1,0:T(8,128)(2,1)S(1)} %get-tuple-element.21), channel_id=1, source_target_pairs={{32,0},{40,8},{48,16},{56,24},{64,32},{72,40},{80,48},{88,56},{96,... | collective-permute-start | bytes 393224 | tf_op jit(solution)/shard_map/ppermute | solution.py:270
  84.4 10.1 %collective-permute-start.5 = (bf16[256,256]{1,0:T(8,128)(2,1)S(1)}, bf16[256,256]{1,0:T(8,128)(2,1)S(1)}, u32[]{:S(2)}, u32[]{:S(2)}) collective-permute-start(bf16[256,256]{1,0:T(8,128)(2,1)S(1)} %get-tuple-element.22), channel_id=1, source_target_pairs={{16,0},{24,8},{32,16},{40,24},{48,32},{56,40},{64,48},{72,56},{80,... | collective-permute-start | bytes 393224 | tf_op jit(solution)/shard_map/ppermute | solution.py:270
  98.3 24.2 %all-to-all-start.3 = ((bf16[8,32,1280]{2,1,0:T(8,128)(2,1)}), bf16[8,32,1280]{2,1,0:T(8,128)(2,1)S(1)}, u32[]{:S(2)}, u32[]{:S(2)}) async-start(bf16[8,32,1280]{2,1,0:T(8,128)(2,1)} %bitcast.12), calls=%async_computation.3 | async-start | bytes 1310720 | tf_op jit(solution)/shard_map/all_to_all | solution.py:279

commit v4 on v3

--- a/solution.py
+++ b/solution.py
@@ -22,6 +22,7 @@
 MASKED = -1e30
 NT = (((1,), (1,)), ((), ()))
 VMEM = pl.BlockSpec(memory_space=pltpu.VMEM)
+SMEM = pl.BlockSpec(memory_space=pltpu.SMEM)
 SMALL = pltpu.CompilerParams(vmem_limit_bytes=8 * 1024 * 1024)
 
 
@@ -87,25 +88,49 @@
     )(value)
 
 
-def add_body(dq_ref, base_ref, one_ref, two_ref, three_ref, o_ref):
-    width = dq_ref.shape[1]
-    o_ref[:, :width] = dq_ref[...]
-    total = base_ref[...] + one_ref[...].astype(jnp.float32)
-    total = total + two_ref[...].astype(jnp.float32) + three_ref[...].astype(jnp.float32)
-    o_ref[:, width:] = total.astype(jnp.bfloat16)
-
-
-def add(dq, base, others):
-    rows, width = dq.shape[0], dq.shape[1] + base.shape[1]
-    return pl.pallas_call(
-        add_body,
-        out_shape=jax.ShapeDtypeStruct((rows, width), jnp.bfloat16),
-        in_specs=[VMEM] * 5,
-        out_specs=VMEM,
+def add_cut_body(parts, at_ref, base_ref, one_ref, two_ref, three_ref, *o_refs):
+    rows = o_refs[0].shape[0]
+    for k in range(parts):
+        source = pl.ds(pl.multiple_of(lax.rem(at_ref[0] + k, parts) * rows, rows), rows)
+        total = base_ref[source, :] + one_ref[source, :].astype(jnp.float32)
+        total = total + two_ref[source, :].astype(jnp.float32) + three_ref[source, :].astype(jnp.float32)
+        o_refs[k][...] = total.astype(jnp.bfloat16)
+
+
+def add_cut(at, base, others, parts):
+    rows, columns = base.shape[0] // parts, base.shape[1]
+    piece = jax.ShapeDtypeStruct((rows, columns), jnp.bfloat16)
+    return pl.pallas_call(
+        functools.partial(add_cut_body, parts),
+        out_shape=(piece,) * parts,
+        in_specs=[SMEM] + [VMEM] * 4,
+        out_specs=(VMEM,) * parts,
         compiler_params=SMALL,
-        cost_estimate=pl.CostEstimate(flops=4 * base.size, bytes_accessed=4 * rows * width, transcendentals=0),
-        name="add",
-    )(dq, base, *others)
+        cost_estimate=pl.CostEstimate(flops=4 * base.size, bytes_accessed=12 * base.size, transcendentals=0),
+        name="add_cut",
+    )(at, base, *others)
+
+
+def join_body(parts, at_ref, *refs):
+    a_ref, b_ref = refs[parts:]
+    for k in range(parts):
+        target = pl.ds(pl.multiple_of(lax.rem(at_ref[0] + (parts - k), parts) * HEAD, HEAD), HEAD)
+        a_ref[:, target] = refs[k][:, :HEAD]
+        b_ref[:, target] = refs[k][:, HEAD:]
+
+
+def join(at, pieces):
+    parts, rows = len(pieces), pieces[0].shape[0]
+    out = jax.ShapeDtypeStruct((rows, parts * HEAD), pieces[0].dtype)
+    return pl.pallas_call(
+        functools.partial(join_body, parts),
+        out_shape=(out, out),
+        in_specs=[SMEM] + [VMEM] * parts,
+        out_specs=(VMEM, VMEM),
+        compiler_params=SMALL,
+        cost_estimate=pl.CostEstimate(flops=out.size, bytes_accessed=8 * out.size, transcendentals=0),
+        name="join",
+    )(at, *pieces)
 
 
 def prepare(core, own, two, four, six, mate, k_s, v_s, kt_s, vt_s, bias_s, dk_s, dv_s):
@@ -161,7 +186,7 @@
     return total
 
 
-def collect(grad, s_ref, total, att_ref, columns, stat_ref, vt_s, dv_s):
+def collect(grad, s_ref, total, y_ref, columns, stat_ref, vt_s, dv_s):
     inverse = 1.0 / total
     out = None
     for c in range(CHUNKS):
@@ -170,22 +195,24 @@
         out = term if out is None else out + term
         dv_s[c] += dot(p16, grad)
     out16 = out.astype(jnp.bfloat16).astype(jnp.float32)
-    att_ref[:, columns] = out16.T.astype(jnp.bfloat16)
+    y_ref[:, columns] = out16.T.astype(jnp.bfloat16)
     delta = jnp.sum(grad.astype(jnp.float32).T * out16, axis=0, keepdims=True)
     stat_ref[0:1, :] = inverse
     stat_ref[1:2, :] = delta
 
 
-def step(ahead, behind, q_ref, g_ref, att_ref, dq_ref, k_s, v_s, kt_s, vt_s, bias_s, dk_s, dv_s):
-    columns = lambda head: pl.ds(pl.multiple_of(head * HEAD, HEAD), HEAD)
+def step(ahead, behind, x_ref, y_ref, k_s, v_s, kt_s, vt_s, bias_s, dk_s, dv_s):
+    heads = x_ref.shape[1] // (2 * HEAD)
+    first = lambda head: pl.ds(pl.multiple_of(head * HEAD, HEAD), HEAD)
+    second = lambda head: pl.ds(pl.multiple_of((heads + head) * HEAD, HEAD), HEAD)
     total = dq = None
     if ahead:
         head, s_ref, stat_ref = ahead
-        grad = g_ref[:, columns(head)]
-        top = scores(q_ref[:, columns(head)], s_ref, k_s, bias_s)
+        grad = x_ref[:, second(head)]
+        top = scores(x_ref[:, first(head)], s_ref, k_s, bias_s)
     if behind:
         last, p_ref, last_ref = behind
-        last_query, last_grad = q_ref[:, columns(last)], g_ref[:, columns(last)]
+        last_query, last_grad = x_ref[:, first(last)], x_ref[:, second(last)]
         inverse, delta = last_ref[0:1, :], last_ref[1:2, :]
         coming = dot(v_s[0], last_grad, NT)
     for c in range(CHUNKS):
@@ -201,16 +228,16 @@
             dq = term if dq is None else dq + term
             dk_s[c] += dot(ds, last_query)
     if behind:
-        dq_ref[:, columns(last)] = (dq * SCALE).T.astype(jnp.bfloat16)
+        y_ref[:, second(last)] = (dq * SCALE).T.astype(jnp.bfloat16)
     if ahead:
-        collect(grad, s_ref, total, att_ref, columns(head), stat_ref, vt_s, dv_s)
-
-
-def attention_body(core_ref, q_ref, g_ref, own, two, four, six, mate, att_ref, dq_ref, mine_ref, mate_ref, k_s, v_s, kt_s, vt_s, bias_s, dk_s, dv_s, even_s, odd_s, even_t, odd_t):
+        collect(grad, s_ref, total, y_ref, first(head), stat_ref, vt_s, dv_s)
+
+
+def attention_body(core_ref, x_ref, own, two, four, six, mate, y_ref, mine_ref, mate_ref, k_s, v_s, kt_s, vt_s, bias_s, dk_s, dv_s, even_s, odd_s, even_t, odd_t):
     core = core_ref[0]
-    heads = dq_ref.shape[1] // HEAD
+    heads = x_ref.shape[1] // (2 * HEAD)
     prepare(core, own, two, four, six, mate, k_s, v_s, kt_s, vt_s, bias_s, dk_s, dv_s)
-    refs = (q_ref, g_ref, att_ref, dq_ref, k_s, v_s, kt_s, vt_s, bias_s, dk_s, dv_s)
+    refs = (x_ref, y_ref, k_s, v_s, kt_s, vt_s, bias_s, dk_s, dv_s)
     step((0, even_s, even_t), None, *refs)
 
     def pair(i, _):
@@ -232,37 +259,35 @@
         mate_ref[first + t, :, HEAD:] = dv_s[SLOTS + t].astype(jnp.bfloat16)
 
 
-def attention(core, q, g, own, two, four, six, mate):
-    heads = g.shape[1] // HEAD
+def attention(core, x, own, two, four, six, mate):
+    heads = x.shape[1] // (2 * HEAD)
     work = heads * CHUNKS * BLOCK * BLOCK
-    scratch = lambda dims, kind: pltpu.VMEM(dims, kind)
     return pl.pallas_call(
         attention_body,
         out_shape=(
-            jax.ShapeDtypeStruct(g.shape, jnp.bfloat16),
-            jax.ShapeDtypeStruct(g.shape, jnp.bfloat16),
+            jax.ShapeDtypeStruct(x.shape, jnp.bfloat16),
             jax.ShapeDtypeStruct((SLOTS, BLOCK, 2 * HEAD), jnp.float32),
             jax.ShapeDtypeStruct((SLOTS, BLOCK, 2 * HEAD), jnp.bfloat16),
         ),
-        in_specs=[pl.BlockSpec(memory_space=pltpu.SMEM)] + [VMEM] * 7,
-        out_specs=(VMEM,) * 4,
+        in_specs=[SMEM] + [VMEM] * 6,
+        out_specs=(VMEM,) * 3,
         scratch_shapes=[
-            scratch((CHUNKS, BLOCK, HEAD), jnp.bfloat16),
-            scratch((CHUNKS, BLOCK, HEAD), jnp.bfloat16),
-            scratch((CHUNKS, HEAD, BLOCK), jnp.bfloat16),
-            scratch((CHUNKS, HEAD, BLOCK), jnp.bfloat16),
-            scratch((CHUNKS, BLOCK, BLOCK), jnp.float32),
-            scratch((CHUNKS, BLOCK, HEAD), jnp.float32),
-            scratch((CHUNKS, BLOCK, HEAD), jnp.float32),
-            scratch((CHUNKS, BLOCK, BLOCK), jnp.float32),
-            scratch((CHUNKS, BLOCK, BLOCK), jnp.float32),
-            scratch((8, BLOCK), jnp.float32),
-            scratch((8, BLOCK), jnp.float32),
+            pltpu.VMEM((CHUNKS, BLOCK, HEAD), jnp.bfloat16),
+            pltpu.VMEM((CHUNKS, BLOCK, HEAD), jnp.bfloat16),
+            pltpu.VMEM((CHUNKS, HEAD, BLOCK), jnp.bfloat16),
+            pltpu.VMEM((CHUNKS, HEAD, BLOCK), jnp.bfloat16),
+            pltpu.VMEM((CHUNKS, BLOCK, BLOCK), jnp.float32),
+            pltpu.VMEM((CHUNKS, BLOCK, HEAD), jnp.float32),
+            pltpu.VMEM((CHUNKS, BLOCK, HEAD), jnp.float32),
+            pltpu.VMEM((CHUNKS, BLOCK, BLOCK), jnp.float32),
+            pltpu.VMEM((CHUNKS, BLOCK, BLOCK), jnp.float32),
+            pltpu.VMEM((8, BLOCK), jnp.float32),
+            pltpu.VMEM((8, BLOCK), jnp.float32),
         ],
         compiler_params=pltpu.CompilerParams(vmem_limit_bytes=16 * 1024 * 1024),
         cost_estimate=pl.CostEstimate(flops=12 * work * HEAD, bytes_accessed=5 * 1024 * 1024, transcendentals=work),
         name="attention",
-    )(core, q, g, own, two, four, six, mate)
+    )(core, x, own, two, four, six, mate)
 
 
 def shift(value, steps):
@@ -279,26 +304,32 @@
     return lax.all_to_all(value, "head", split_axis=0, concat_axis=0, tiled=True)
 
 
+def around(value, steps):
+    count = lax.axis_size("head")
+    return lax.ppermute(value, "head", [(s, (s + steps) % count) for s in range(count)])
+
+
 def local(queries, key_heads, value_head_array, out_grad, doc_ids):
     parts = lax.axis_size("head")
     core = (lax.axis_index("ctx") % 2).astype(jnp.int32).reshape(1)
-    q = over_head(pack((queries, key_heads, value_head_array), parts)).reshape(BLOCK, -1)
-    packed = pack((out_grad,), parts)
-    g = over_head(packed).reshape(BLOCK, -1)
+    at = lax.axis_index("head").astype(jnp.int32).reshape(1)
+    kv = over_head(pack((key_heads, value_head_array), parts)).reshape(BLOCK, -1)
     docs = jnp.pad((doc_ids + 1).astype(jnp.bfloat16)[None, :], ((0, DOC_ROWS - 1), (0, 0)))
-    own = jnp.concatenate([q[:, -2 * HEAD :], docs], axis=0)
+    own = jnp.concatenate([kv, docs], axis=0)
+    packed = pack((queries, out_grad), parts)
+    x = over_head(packed).reshape(BLOCK, -1)
     two, four, six = (shift(own, steps) for steps in (2, 4, 6))
     mate = swap(jnp.stack([own, two, four, six]))
-    attended, dq, mine, sent = attention(core, q, g, own, two, four, six, mate)
-    attended = over_head(attended.reshape(parts, -1, attended.shape[1]))
+    y, mine, sent = attention(core, x, own, two, four, six, mate)
     sent = swap(sent)
+    y = over_head(y.reshape(parts, -1, y.shape[1]))
     sums = mine + sent.astype(jnp.float32)
     rounded = sums.astype(jnp.bfloat16)
     back = [shift(rounded[t], -2 * t) for t in range(1, SLOTS)]
-    grads = add(dq, sums[0], back)
-    grads = over_head(grads.reshape(parts, -1, grads.shape[1]))
-    (attended,) = unpack(attended, (attended.shape[2],))
-    query_grad, key_grad, value_grad = unpack(grads, (dq.shape[1], HEAD, HEAD))
+    pieces = add_cut(at, sums[0], back, parts)
+    pieces = [pieces[0]] + [around(piece, k) for k, piece in enumerate(pieces) if k]
+    attended, query_grad = unpack(y, (y.shape[2] // 2,) * 2)
+    key_grad, value_grad = join(at, pieces)
     return attended, query_grad, key_grad, value_grad
 
 

time: 125 us -> 113 us (0.904)
  waiting for transfers between devices: 56 us -> 32.3 us
  starting transfers between devices: 41.3 us -> 53.5 us
    all_to_all x4 -> x3, waiting for transfers between devices: 40.4 us -> 14.4 us  [over_head(): lax.all_to_all(value, 'head', split_axis=0, concat_axis=0, tiled=True)]
    ppermute x0 -> x7, starting transfers between devices: none -> 17 us  [around(): lax.ppermute(value, 'head', [(s, (s + steps) % count) for s in range(coun...]
    all_to_all x4 -> x3, starting transfers between devices: 23 us -> 15.7 us  [over_head(): lax.all_to_all(value, 'head', split_axis=0, concat_axis=0, tiled=True)]
    ppermute x6, starting transfers between devices: 18 us -> 20.6 us  [shift(): lax.ppermute(value, 'ctx', [(s, s + steps) for s in range(max(0, -steps),...]
    ppermute x0 -> x7, waiting for transfers between devices: none -> 2.28 us  [around(): lax.ppermute(value, 'head', [(s, (s + steps) % count) for s in range(coun...]
    ppermute x2, waiting for transfers between devices: 1.92 us -> 3.83 us  [swap(): return lax.ppermute(value, 'ctx', [(s, s ^ 1) for s in range(count)])]
    ppermute x6, waiting for transfers between devices: 13.6 us -> 11.8 us  [shift(): lax.ppermute(value, 'ctx', [(s, s + steps) for s in range(max(0, -steps),...]
    pallas_call x2 -> x3, Pallas kernels: 17.3 us -> 17.2 us  [the longest x1 16.4 us: attention(): pl.pallas_call(attention_body, out_shape=(jax.ShapeDtypeStruct(x.shape, j...]
  transfers between devices with their start and end apart: 12 -> 18, of which waited for: 8 -> 9; matrix products, arithmetic and copies ran while one was open for 0% -> 1% of each run, Pallas kernels for 3% -> 3%
where the time goes in v4:
time: 113 us; the launch traced here: 112 us
  starting transfers between devices  53.5 us (47%)
  waiting for transfers between devices  32.3 us (29%)
  Pallas kernels  22.3 us (20%)
  local copies, waits for them, and re-layouts  1.65 us (1%)
  other arithmetic  1.29 us (1%)
    ppermute x6, starting transfers between devices, shift(): lax.ppermute(value, 'ctx', [(s, s + steps) for s in range(max(0, -steps),...  20.6 us
    ppermute x7, starting transfers between devices, around(): lax.ppermute(value, 'head', [(s, (s + steps) % count) for s in range(coun...  17 us
    pallas_call x1, Pallas kernels, attention(): pl.pallas_call(attention_body, out_shape=(jax.ShapeDtypeStruct(x.shape, j...  16.4 us
    all_to_all x3, starting transfers between devices, over_head(): lax.all_to_all(value, 'head', split_axis=0, concat_axis=0, tiled=True)  15.7 us
    all_to_all x3, waiting for transfers between devices, over_head(): lax.all_to_all(value, 'head', split_axis=0, concat_axis=0, tiled=True)  14.4 us
    ppermute x6, waiting for transfers between devices, shift(): lax.ppermute(value, 'ctx', [(s, s + steps) for s in range(max(0, -steps),...  11.8 us
    pallas_call x2, Pallas kernels, pack(): pl.pallas_call(functools.partial(pack_body, parts), out_shape=jax.ShapeDt...  4.02 us
    ppermute x2, waiting for transfers between devices, swap(): return lax.ppermute(value, 'ctx', [(s, s ^ 1) for s in range(count)])  3.83 us
  transfers between devices with their start and end apart: 18, of which 9 were waited for; matrix products, arithmetic and copies ran while one was open for 1% of the time, Pallas kernels for 3%

profile of v4, /device:TPU:2, one launch (start us, length us, event | category | flops | bytes accessed | tf_op | source)
XLA Modules:
  0.0 112.1 jit_solution(3897790245186435962)
XLA Ops:
  0.6 1.7 %shard_map.85 = bf16[8,32,256]{2,1,0:T(8,128)(2,1)} custom-call(bf16[32,1024]{1,0:T(8,128)(2,1)} %refs_0_.3, bf16[32,1024]{1,0:T(8,128)(2,1)} %refs_1_.3), custom_call_target="tpu_custom_call" | custom-call | flops 65536 | bytes 262144 | tf_op jit(solution)/shard_map/pallas_call | solution.py:55
  2.3 8.5 %all-to-all-start.1 = ((bf16[8,32,256]{2,1,0:T(8,128)(2,1)}), bf16[8,32,256]{2,1,0:T(8,128)(2,1)S(1)}, u32[]{:S(2)}, u32[]{:S(2)}) async-start(bf16[8,32,256]{2,1,0:T(8,128)(2,1)} %shard_map.85), calls=%async_computation.1 | async-start | bytes 262144 | tf_op jit(solution)/shard_map/all_to_all | solution.py:304
  10.8 2.4 %shard_map.84 = bf16[8,32,2048]{2,1,0:T(8,128)(2,1)} custom-call(bf16[32,8192]{1,0:T(8,128)(2,1)} %refs_0_.2, bf16[32,8192]{1,0:T(8,128)(2,1)} %refs_1_.2), custom_call_target="tpu_custom_call" | custom-call | flops 524288 | bytes 2097152 | tf_op jit(solution)/shard_map/pallas_call | solution.py:55
  13.1 0.0 copy-start.3
  13.2 6.7 %all-to-all-done.1 = bf16[8,32,256]{2,1,0:T(8,128)(2,1)S(1)} async-done(((bf16[8,32,256]{2,1,0:T(8,128)(2,1)}), bf16[8,32,256]{2,1,0:T(8,128)(2,1)S(1)}, u32[]{:S(2)}, u32[]{:S(2)}) %all-to-all-start.1) | async-done | bytes 131104 | tf_op jit(solution)/shard_map/all_to_all | solution.py:304
  19.9 3.6 %all-to-all-start = ((bf16[8,32,2048]{2,1,0:T(8,128)(2,1)}), bf16[8,32,2048]{2,1,0:T(8,128)(2,1)S(1)}, u32[]{:S(2)}, u32[]{:S(2)}) async-start(bf16[8,32,2048]{2,1,0:T(8,128)(2,1)} %shard_map.84), calls=%async_computation | async-start | bytes 2097152 | tf_op jit(solution)/shard_map/all_to_all | solution.py:304
  23.4 0.0 copy-done.3
  23.5 4.9 %collective-permute-start.2 = (bf16[272,256]{1,0:T(8,128)(2,1)S(1)}, bf16[272,256]{1,0:T(8,128)(2,1)S(1)}, u32[]{:S(2)}, u32[]{:S(2)}) collective-permute-start(bf16[272,256]{1,0:T(8,128)(2,1)S(1)} %get-tuple-element.40.own), channel_id=1, source_target_pairs={{0,48},{8,56},{16,64},{24,72},{32,80},{40,88},{48,96},{56,104},{64... | collective-permute-start | bytes 417800 | tf_op jit(solution)/shard_map/ppermute | solution.py:295
  28.4 3.5 %collective-permute-start.1 = (bf16[272,256]{1,0:T(8,128)(2,1)S(1)}, bf16[272,256]{1,0:T(8,128)(2,1)S(1)}, u32[]{:S(2)}, u32[]{:S(2)}) collective-permute-start(bf16[272,256]{1,0:T(8,128)(2,1)S(1)} %get-tuple-element.40.own), channel_id=1, source_target_pairs={{0,32},{8,40},{16,48},{24,56},{32,64},{40,72},{48,80},{56,88},{64,... | collective-permute-start | bytes 417800 | tf_op jit(solution)/shard_map/ppermute | solution.py:295
  31.9 2.9 %collective-permute-start = (bf16[272,256]{1,0:T(8,128)(2,1)S(1)}, bf16[272,256]{1,0:T(8,128)(2,1)S(1)}, u32[]{:S(2)}, u32[]{:S(2)}) collective-permute-start(bf16[272,256]{1,0:T(8,128)(2,1)S(1)} %get-tuple-element.40.own), channel_id=1, source_target_pairs={{0,16},{8,24},{16,32},{24,40},{32,48},{40,56},{48,64},{56,72},{64,... | collective-permute-start | bytes 417800 | tf_op jit(solution)/shard_map/ppermute | solution.py:295
  34.8 0.0 collective-permute-done.2.six
  34.8 4.0 %collective-permute-done.1.four = bf16[272,256]{1,0:T(8,128)(2,1)S(1)} collective-permute-done((bf16[272,256]{1,0:T(8,128)(2,1)S(1)}, bf16[272,256]{1,0:T(8,128)(2,1)S(1)}, u32[]{:S(2)}, u32[]{:S(2)}) %collective-permute-start.1) | collective-permute-done | bytes 139296 | tf_op jit(solution)/shard_map/ppermute | solution.py:295
  38.8 2.1 %collective-permute-done.two = bf16[272,256]{1,0:T(8,128)(2,1)S(1)} collective-permute-done((bf16[272,256]{1,0:T(8,128)(2,1)S(1)}, bf16[272,256]{1,0:T(8,128)(2,1)S(1)}, u32[]{:S(2)}, u32[]{:S(2)}) %collective-permute-start) | collective-permute-done | bytes 139296 | tf_op jit(solution)/shard_map/ppermute | solution.py:295
  41.0 0.1 pad_maximum_fusion
  41.0 0.1 collective-permute-start.3
  41.1 1.9 %collective-permute-done.3.mate = bf16[4,272,256]{2,1,0:T(8,128)(2,1)S(1)} collective-permute-done((bf16[4,272,256]{2,1,0:T(8,128)(2,1)S(1)}, bf16[4,272,256]{2,1,0:T(8,128)(2,1)S(1)}, u32[]{:S(2)}, u32[]{:S(2)}) %collective-permute-start.3) | collective-permute-done | bytes 557088 | tf_op jit(solution)/shard_map/ppermute | solution.py:300
  43.1 7.7 %all-to-all-done = bf16[8,32,2048]{2,1,0:T(8,128)(2,1)S(1)} async-done(((bf16[8,32,2048]{2,1,0:T(8,128)(2,1)}), bf16[8,32,2048]{2,1,0:T(8,128)(2,1)S(1)}, u32[]{:S(2)}, u32[]{:S(2)}) %all-to-all-start) | async-done | bytes 1048608 | tf_op jit(solution)/shard_map/all_to_all | solution.py:304
  50.7 16.4 %attention.1 = (bf16[256,2048]{1,0:T(8,128)(2,1)}, f32[4,256,256]{2,1,0:T(8,128)S(1)}, bf16[4,256,256]{2,1,0:T(8,128)(2,1)S(1)}) custom-call(s32[1]{0:T(128)} %bitcast.core_ref, bf16[256,2048]{1,0:T(8,128)(2,1)S(1)} %bitcast.18, bf16[272,256]{1,0:T(8,128)(2,1)S(1)} %get-tuple-element.40.own, bf16[272,256]{1,0:T(8,128)(2,1)S(1)} %collective-permute-done.two, ...), custom_call_target="tpu_custom_call" | custom-call | flops 5637144576 | bytes 5242880 | tf_op jit(solution)/shard_map/attention/pallas_call | solution.py:265
  67.2 0.0 copy-start
  67.2 0.8 copy-done
  68.0 0.0 copy-start.1
  68.0 3.7 %all-to-all-start.2 = ((bf16[8,32,2048]{2,1,0:T(8,128)(2,1)}), bf16[8,32,2048]{2,1,0:T(8,128)(2,1)S(1)}, u32[]{:S(2)}, u32[]{:S(2)}) async-start(bf16[8,32,2048]{2,1,0:T(8,128)(2,1)} %bitcast.7), calls=%async_computation.2 | async-start | bytes 2097152 | tf_op jit(solution)/shard_map/all_to_all | solution.py:304
  71.7 0.0 copy-done.1
  71.7 0.1 collective-permute-start.4
  71.8 1.9 %collective-permute-done.4 = bf16[4,256,256]{2,1,0:T(8,128)(2,1)S(1)} collective-permute-done((bf16[4,256,256]{2,1,0:T(8,128)(2,1)S(1)}, bf16[4,256,256]{2,1,0:T(8,128)(2,1)S(1)}, u32[]{:S(2)}, u32[]{:S(2)}) %collective-permute-start.4) | collective-permute-done | bytes 524320 | tf_op jit(solution)/shard_map/ppermute | solution.py:300
  73.7 0.0 copy-start.2
  73.7 0.8 copy-done.2
  74.5 1.2 %fusion.3 = (bf16[4,256,256]{2,1,0:T(8,128)(2,1)S(1)}, f32[4,256,256]{2,1,0:T(8,128)S(1)}) fusion(f32[4,256,256]{2,1,0:T(8,128)S(1)} %get-tuple-element.22, bf16[4,256,256]{2,1,0:T(8,128)(2,1)} %copy-done.2), kind=kLoop, calls=%fused_computation.11 | loop fusion | flops 786432 | bytes 3145728 | tf_op jit(solution)/shard_map/convert_element_type | solution.py:327
  75.7 3.5 %collective-permute-start.7 = (bf16[256,256]{1,0:T(8,128)(2,1)S(1)}, bf16[256,256]{1,0:T(8,128)(2,1)S(1)}, u32[]{:S(2)}, u32[]{:S(2)}) collective-permute-start(bf16[256,256]{1,0:T(8,128)(2,1)S(1)} %get-tuple-element.36), channel_id=1, source_target_pairs={{48,0},{56,8},{64,16},{72,24},{80,32},{88,40},{96,48},{104,56},{11... | collective-permute-start | bytes 393224 | tf_op jit(solution)/shard_map/ppermute | solution.py:295
  79.2 2.9 %collective-permute-start.6 = (bf16[256,256]{1,0:T(8,128)(2,1)S(1)}, bf16[256,256]{1,0:T(8,128)(2,1)S(1)}, u32[]{:S(2)}, u32[]{:S(2)}) collective-permute-start(bf16[256,256]{1,0:T(8,128)(2,1)S(1)} %get-tuple-element.37), channel_id=1, source_target_pairs={{32,0},{40,8},{48,16},{56,24},{64,32},{72,40},{80,48},{88,56},{96,... | collective-permute-start | bytes 393224 | tf_op jit(solution)/shard_map/ppermute | solution.py:295
  82.1 3.0 %collective-permute-start.5 = (bf16[256,256]{1,0:T(8,128)(2,1)S(1)}, bf16[256,256]{1,0:T(8,128)(2,1)S(1)}, u32[]{:S(2)}, u32[]{:S(2)}) collective-permute-start(bf16[256,256]{1,0:T(8,128)(2,1)S(1)} %get-tuple-element.38), channel_id=1, source_target_pairs={{16,0},{24,8},{32,16},{40,24},{48,32},{56,40},{64,48},{72,56},{80,... | collective-permute-start | bytes 393224 | tf_op jit(solution)/shard_map/ppermute | solution.py:295
  85.1 0.0 collective-permute-done.7.three_ref
  85.1 4.2 %collective-permute-done.6.two_ref = bf16[256,256]{1,0:T(8,128)(2,1)S(1)} collective-permute-done((bf16[256,256]{1,0:T(8,128)(2,1)S(1)}, bf16[256,256]{1,0:T(8,128)(2,1)S(1)}, u32[]{:S(2)}, u32[]{:S(2)}) %collective-permute-start.6) | collective-permute-done | bytes 131104 | tf_op jit(solution)/shard_map/ppermute | solution.py:295
  89.3 1.5 %collective-permute-done.5.one_ref = bf16[256,256]{1,0:T(8,128)(2,1)S(1)} collective-permute-done((bf16[256,256]{1,0:T(8,128)(2,1)S(1)}, bf16[256,256]{1,0:T(8,128)(2,1)S(1)}, u32[]{:S(2)}, u32[]{:S(2)}) %collective-permute-start.5) | collective-permute-done | bytes 131104 | tf_op jit(solution)/shard_map/ppermute | solution.py:295
  90.8 0.1 add_cut.1
  90.8 1.9 %collective-permute-start.8 = (bf16[32,256]{1,0:T(8,128)(2,1)S(1)}, bf16[32,256]{1,0:T(8,128)(2,1)S(1)}, u32[]{:S(2)}, u32[]{:S(2)}) collective-permute-start(bf16[32,256]{1,0:T(8,128)(2,1)S(1)} %get-tuple-element.25), channel_id=1, source_target_pairs={{0,1},{1,2},{2,3},{3,4},{4,5},{5,6},{6,7},{7,0},{8,9},{9,10},{10,1... | collective-permute-start | bytes 49160 | tf_op jit(solution)/shard_map/ppermute | solution.py:309
  92.7 2.4 %collective-permute-start.9 = (bf16[32,256]{1,0:T(8,128)(2,1)S(1)}, bf16[32,256]{1,0:T(8,128)(2,1)S(1)}, u32[]{:S(2)}, u32[]{:S(2)}) collective-permute-start(bf16[32,256]{1,0:T(8,128)(2,1)S(1)} %get-tuple-element.26), channel_id=1, source_target_pairs={{0,2},{1,3},{2,4},{3,5},{4,6},{5,7},{6,0},{7,1},{8,10},{9,11},{10,... | collective-permute-start | bytes 49160 | tf_op jit(solution)/shard_map/ppermute | solution.py:309
  95.1 2.7 %collective-permute-start.10 = (bf16[32,256]{1,0:T(8,128)(2,1)S(1)}, bf16[32,256]{1,0:T(8,128)(2,1)S(1)}, u32[]{:S(2)}, u32[]{:S(2)}) collective-permute-start(bf16[32,256]{1,0:T(8,128)(2,1)S(1)} %get-tuple-element.27), channel_id=1, source_target_pairs={{0,3},{1,4},{2,5},{3,6},{4,7},{5,0},{6,1},{7,2},{8,11},{9,12},{10,... | collective-permute-start | bytes 49160 | tf_op jit(solution)/shard_map/ppermute | solution.py:309
  97.8 2.3 %collective-permute-start.11 = (bf16[32,256]{1,0:T(8,128)(2,1)S(1)}, bf16[32,256]{1,0:T(8,128)(2,1)S(1)}, u32[]{:S(2)}, u32[]{:S(2)}) collective-permute-start(bf16[32,256]{1,0:T(8,128)(2,1)S(1)} %get-tuple-element.28), channel_id=1, source_target_pairs={{0,4},{1,5},{2,6},{3,7},{4,0},{5,1},{6,2},{7,3},{8,12},{9,13},{10,... | collective-permute-start | bytes 49160 | tf_op jit(solution)/shard_map/ppermute | solution.py:309
  100.1 2.7 %collective-permute-start.12 = (bf16[32,256]{1,0:T(8,128)(2,1)S(1)}, bf16[32,256]{1,0:T(8,128)(2,1)S(1)}, u32[]{:S(2)}, u32[]{:S(2)}) collective-permute-start(bf16[32,256]{1,0:T(8,128)(2,1)S(1)} %get-tuple-element.29), channel_id=1, source_target_pairs={{0,5},{1,6},{2,7},{3,0},{4,1},{5,2},{6,3},{7,4},{8,13},{9,14},{10,... | collective-permute-start | bytes 49160 | tf_op jit(solution)/shard_map/ppermute | solution.py:309
  102.8 0.0 collective-permute-done.8.refs_1_
  102.8 3.6 %collective-permute-start.13 = (bf16[32,256]{1,0:T(8,128)(2,1)S(1)}, bf16[32,256]{1,0:T(8,128)(2,1)S(1)}, u32[]{:S(2)}, u32[]{:S(2)}) collective-permute-start(bf16[32,256]{1,0:T(8,128)(2,1)S(1)} %get-tuple-element.30), channel_id=1, source_target_pairs={{0,6},{1,7},{2,0},{3,1},{4,2},{5,3},{6,4},{7,5},{8,14},{9,15},{10,... | collective-permute-start | bytes 49160 | tf_op jit(solution)/shard_map/ppermute | solution.py:309
  106.4 0.0 collective-permute-done.9.refs_2_
  106.4 1.5 %collective-permute-start.14 = (bf16[32,256]{1,0:T(8,128)(2,1)S(1)}, bf16[32,256]{1,0:T(8,128)(2,1)S(1)}, u32[]{:S(2)}, u32[]{:S(2)}) collective-permute-start(bf16[32,256]{1,0:T(8,128)(2,1)S(1)} %get-tuple-element.31), channel_id=1, source_target_pairs={{0,7},{1,0},{2,1},{3,2},{4,3},{5,4},{6,5},{7,6},{8,15},{9,8},{10,9... | collective-permute-start | bytes 49160 | tf_op jit(solution)/shard_map/ppermute | solution.py:309
  107.9 0.0 collective-permute-done.10.refs_3_
  107.9 0.0 collective-permute-done.11.refs_4_
  107.9 0.0 collective-permute-done.12.refs_5_
  107.9 0.0 collective-permute-done.13.refs_6_
  107.9 2.3 %collective-permute-done.14.refs_7_ = bf16[32,256]{1,0:T(8,128)(2,1)S(1)} collective-permute-done((bf16[32,256]{1,0:T(8,128)(2,1)S(1)}, bf16[32,256]{1,0:T(8,128)(2,1)S(1)}, u32[]{:S(2)}, u32[]{:S(2)}) %collective-permute-start.14) | collective-permute-done | bytes 16416 | tf_op jit(solution)/shard_map/ppermute | solution.py:309
  110.2 0.7 join.1
  110.8 0.0 all-to-all-done.2.i_ref
  110.8 1.1 shard_map.86
  (5 shorter events, 0.1 us)
Async XLA Ops:
  2.3 17.6 %all-to-all-start.1 = ((bf16[8,32,256]{2,1,0:T(8,128)(2,1)}), bf16[8,32,256]{2,1,0:T(8,128)(2,1)S(1)}, u32[]{:S(2)}, u32[]{:S(2)}) async-start(bf16[8,32,256]{2,1,0:T(8,128)(2,1)} %shard_map.85), calls=%async_computation.1 | async-start | bytes 262144 | tf_op jit(solution)/shard_map/all_to_all | solution.py:304
  13.1 10.3 %copy-start.3 = (s32[256]{0:T(256)S(1)}, s32[256]{0:T(256)}, u32[]{:S(2)}) copy-start(s32[256]{0:T(256)} %param.9) | copy-start | bytes 3076
  19.9 30.9 %all-to-all-start = ((bf16[8,32,2048]{2,1,0:T(8,128)(2,1)}), bf16[8,32,2048]{2,1,0:T(8,128)(2,1)S(1)}, u32[]{:S(2)}, u32[]{:S(2)}) async-start(bf16[8,32,2048]{2,1,0:T(8,128)(2,1)} %shard_map.84), calls=%async_computation | async-start | bytes 2097152 | tf_op jit(solution)/shard_map/all_to_all | solution.py:304
  23.5 11.3 %collective-permute-start.2 = (bf16[272,256]{1,0:T(8,128)(2,1)S(1)}, bf16[272,256]{1,0:T(8,128)(2,1)S(1)}, u32[]{:S(2)}, u32[]{:S(2)}) collective-permute-start(bf16[272,256]{1,0:T(8,128)(2,1)S(1)} %get-tuple-element.40.own), channel_id=1, source_target_pairs={{0,48},{8,56},{16,64},{24,72},{32,80},{40,88},{48,96},{56,104},{64... | collective-permute-start | bytes 417800 | tf_op jit(solution)/shard_map/ppermute | solution.py:295
  28.4 10.4 %collective-permute-start.1 = (bf16[272,256]{1,0:T(8,128)(2,1)S(1)}, bf16[272,256]{1,0:T(8,128)(2,1)S(1)}, u32[]{:S(2)}, u32[]{:S(2)}) collective-permute-start(bf16[272,256]{1,0:T(8,128)(2,1)S(1)} %get-tuple-element.40.own), channel_id=1, source_target_pairs={{0,32},{8,40},{16,48},{24,56},{32,64},{40,72},{48,80},{56,88},{64,... | collective-permute-start | bytes 417800 | tf_op jit(solution)/shard_map/ppermute | solution.py:295
  31.9 9.1 %collective-permute-start = (bf16[272,256]{1,0:T(8,128)(2,1)S(1)}, bf16[272,256]{1,0:T(8,128)(2,1)S(1)}, u32[]{:S(2)}, u32[]{:S(2)}) collective-permute-start(bf16[272,256]{1,0:T(8,128)(2,1)S(1)} %get-tuple-element.40.own), channel_id=1, source_target_pairs={{0,16},{8,24},{16,32},{24,40},{32,48},{40,56},{48,64},{56,72},{64,... | collective-permute-start | bytes 417800 | tf_op jit(solution)/shard_map/ppermute | solution.py:295
  41.0 2.0 %collective-permute-start.3 = (bf16[4,272,256]{2,1,0:T(8,128)(2,1)S(1)}, bf16[4,272,256]{2,1,0:T(8,128)(2,1)S(1)}, u32[]{:S(2)}, u32[]{:S(2)}) collective-permute-start(bf16[4,272,256]{2,1,0:T(8,128)(2,1)S(1)} %pad_maximum_fusion), channel_id=1, source_target_pairs={{0,8},{8,0},{16,24},{24,16},{32,40},{40,32},{48,56},{56,48},{64,72... | collective-permute-start | bytes 1671176 | tf_op jit(solution)/shard_map/ppermute | solution.py:300
  67.2 0.8 copy-start
  68.0 3.7 %copy-start.1 = (bf16[4,256,256]{2,1,0:T(8,128)(2,1)S(1)}, bf16[4,256,256]{2,1,0:T(8,128)(2,1)}, u32[]{:S(2)}) copy-start(bf16[4,256,256]{2,1,0:T(8,128)(2,1)} %copy-done) | copy-start | bytes 1572868
  68.0 42.9 %all-to-all-start.2 = ((bf16[8,32,2048]{2,1,0:T(8,128)(2,1)}), bf16[8,32,2048]{2,1,0:T(8,128)(2,1)S(1)}, u32[]{:S(2)}, u32[]{:S(2)}) async-start(bf16[8,32,2048]{2,1,0:T(8,128)(2,1)} %bitcast.7), calls=%async_computation.2 | async-start | bytes 2097152 | tf_op jit(solution)/shard_map/all_to_all | solution.py:304
  71.7 2.0 %collective-permute-start.4 = (bf16[4,256,256]{2,1,0:T(8,128)(2,1)S(1)}, bf16[4,256,256]{2,1,0:T(8,128)(2,1)S(1)}, u32[]{:S(2)}, u32[]{:S(2)}) collective-permute-start(bf16[4,256,256]{2,1,0:T(8,128)(2,1)S(1)} %copy-done.1), channel_id=1, source_target_pairs={{0,8},{8,0},{16,24},{24,16},{32,40},{40,32},{48,56},{56,48},{64,72... | collective-permute-start | bytes 1572872 | tf_op jit(solution)/shard_map/ppermute | solution.py:300
  73.7 0.8 copy-start.2
  75.7 9.4 %collective-permute-start.7 = (bf16[256,256]{1,0:T(8,128)(2,1)S(1)}, bf16[256,256]{1,0:T(8,128)(2,1)S(1)}, u32[]{:S(2)}, u32[]{:S(2)}) collective-permute-start(bf16[256,256]{1,0:T(8,128)(2,1)S(1)} %get-tuple-element.36), channel_id=1, source_target_pairs={{48,0},{56,8},{64,16},{72,24},{80,32},{88,40},{96,48},{104,56},{11... | collective-permute-start | bytes 393224 | tf_op jit(solution)/shard_map/ppermute | solution.py:295
  79.2 10.1 %collective-permute-start.6 = (bf16[256,256]{1,0:T(8,128)(2,1)S(1)}, bf16[256,256]{1,0:T(8,128)(2,1)S(1)}, u32[]{:S(2)}, u32[]{:S(2)}) collective-permute-start(bf16[256,256]{1,0:T(8,128)(2,1)S(1)} %get-tuple-element.37), channel_id=1, source_target_pairs={{32,0},{40,8},{48,16},{56,24},{64,32},{72,40},{80,48},{88,56},{96,... | collective-permute-start | bytes 393224 | tf_op jit(solution)/shard_map/ppermute | solution.py:295
  82.1 8.7 %collective-permute-start.5 = (bf16[256,256]{1,0:T(8,128)(2,1)S(1)}, bf16[256,256]{1,0:T(8,128)(2,1)S(1)}, u32[]{:S(2)}, u32[]{:S(2)}) collective-permute-start(bf16[256,256]{1,0:T(8,128)(2,1)S(1)} %get-tuple-element.38), channel_id=1, source_target_pairs={{16,0},{24,8},{32,16},{40,24},{48,32},{56,40},{64,48},{72,56},{80,... | collective-permute-start | bytes 393224 | tf_op jit(solution)/shard_map/ppermute | solution.py:295
  90.8 12.0 %collective-permute-start.8 = (bf16[32,256]{1,0:T(8,128)(2,1)S(1)}, bf16[32,256]{1,0:T(8,128)(2,1)S(1)}, u32[]{:S(2)}, u32[]{:S(2)}) collective-permute-start(bf16[32,256]{1,0:T(8,128)(2,1)S(1)} %get-tuple-element.25), channel_id=1, source_target_pairs={{0,1},{1,2},{2,3},{3,4},{4,5},{5,6},{6,7},{7,0},{8,9},{9,10},{10,1... | collective-permute-start | bytes 49160 | tf_op jit(solution)/shard_map/ppermute | solution.py:309
  92.7 13.7 %collective-permute-start.9 = (bf16[32,256]{1,0:T(8,128)(2,1)S(1)}, bf16[32,256]{1,0:T(8,128)(2,1)S(1)}, u32[]{:S(2)}, u32[]{:S(2)}) collective-permute-start(bf16[32,256]{1,0:T(8,128)(2,1)S(1)} %get-tuple-element.26), channel_id=1, source_target_pairs={{0,2},{1,3},{2,4},{3,5},{4,6},{5,7},{6,0},{7,1},{8,10},{9,11},{10,... | collective-permute-start | bytes 49160 | tf_op jit(solution)/shard_map/ppermute | solution.py:309
  95.1 12.8 %collective-permute-start.10 = (bf16[32,256]{1,0:T(8,128)(2,1)S(1)}, bf16[32,256]{1,0:T(8,128)(2,1)S(1)}, u32[]{:S(2)}, u32[]{:S(2)}) collective-permute-start(bf16[32,256]{1,0:T(8,128)(2,1)S(1)} %get-tuple-element.27), channel_id=1, source_target_pairs={{0,3},{1,4},{2,5},{3,6},{4,7},{5,0},{6,1},{7,2},{8,11},{9,12},{10,... | collective-permute-start | bytes 49160 | tf_op jit(solution)/shard_map/ppermute | solution.py:309
  97.8 10.1 %collective-permute-start.11 = (bf16[32,256]{1,0:T(8,128)(2,1)S(1)}, bf16[32,256]{1,0:T(8,128)(2,1)S(1)}, u32[]{:S(2)}, u32[]{:S(2)}) collective-permute-start(bf16[32,256]{1,0:T(8,128)(2,1)S(1)} %get-tuple-element.28), channel_id=1, source_target_pairs={{0,4},{1,5},{2,6},{3,7},{4,0},{5,1},{6,2},{7,3},{8,12},{9,13},{10,... | collective-permute-start | bytes 49160 | tf_op jit(solution)/shard_map/ppermute | solution.py:309
  100.1 7.7 %collective-permute-start.12 = (bf16[32,256]{1,0:T(8,128)(2,1)S(1)}, bf16[32,256]{1,0:T(8,128)(2,1)S(1)}, u32[]{:S(2)}, u32[]{:S(2)}) collective-permute-start(bf16[32,256]{1,0:T(8,128)(2,1)S(1)} %get-tuple-element.29), channel_id=1, source_target_pairs={{0,5},{1,6},{2,7},{3,0},{4,1},{5,2},{6,3},{7,4},{8,13},{9,14},{10,... | collective-permute-start | bytes 49160 | tf_op jit(solution)/shard_map/ppermute | solution.py:309
  102.8 5.0 %collective-permute-start.13 = (bf16[32,256]{1,0:T(8,128)(2,1)S(1)}, bf16[32,256]{1,0:T(8,128)(2,1)S(1)}, u32[]{:S(2)}, u32[]{:S(2)}) collective-permute-start(bf16[32,256]{1,0:T(8,128)(2,1)S(1)} %get-tuple-element.30), channel_id=1, source_target_pairs={{0,6},{1,7},{2,0},{3,1},{4,2},{5,3},{6,4},{7,5},{8,14},{9,15},{10,... | collective-permute-start | bytes 49160 | tf_op jit(solution)/shard_map/ppermute | solution.py:309
  106.4 3.7 %collective-permute-start.14 = (bf16[32,256]{1,0:T(8,128)(2,1)S(1)}, bf16[32,256]{1,0:T(8,128)(2,1)S(1)}, u32[]{:S(2)}, u32[]{:S(2)}) collective-permute-start(bf16[32,256]{1,0:T(8,128)(2,1)S(1)} %get-tuple-element.31), channel_id=1, source_target_pairs={{0,7},{1,0},{2,1},{3,2},{4,3},{5,4},{6,5},{7,6},{8,15},{9,8},{10,9... | collective-permute-start | bytes 49160 | tf_op jit(solution)/shard_map/ppermute | solution.py:309

commit v5 on v4

--- a/solution.py
+++ b/solution.py
@@ -178,77 +178,72 @@
 
 
 def weigh(c, s_ref, top, total):
+    whole = []
     for r in range(0, BLOCK, PIECE):
         p = jnp.exp2(s_ref[c, r : r + PIECE, :] - top)
         s_ref[c, r : r + PIECE, :] = p
         part = jnp.sum(p, axis=0, keepdims=True)
         total = part if total is None else total + part
-    return total
-
-
-def collect(grad, s_ref, total, y_ref, columns, stat_ref, vt_s, dv_s):
-    inverse = 1.0 / total
-    out = None
-    for c in range(CHUNKS):
-        p16 = (s_ref[c] * inverse).astype(jnp.bfloat16)
-        term = dot(vt_s[c], p16)
-        out = term if out is None else out + term
-        dv_s[c] += dot(p16, grad)
-    out16 = out.astype(jnp.bfloat16).astype(jnp.float32)
-    y_ref[:, columns] = out16.T.astype(jnp.bfloat16)
-    delta = jnp.sum(grad.astype(jnp.float32).T * out16, axis=0, keepdims=True)
-    stat_ref[0:1, :] = inverse
-    stat_ref[1:2, :] = delta
+        whole.append(p.astype(jnp.bfloat16))
+    return total, jnp.concatenate(whole, axis=0)
 
 
 def step(ahead, behind, x_ref, y_ref, k_s, v_s, kt_s, vt_s, bias_s, dk_s, dv_s):
     heads = x_ref.shape[1] // (2 * HEAD)
     first = lambda head: pl.ds(pl.multiple_of(head * HEAD, HEAD), HEAD)
     second = lambda head: pl.ds(pl.multiple_of((heads + head) * HEAD, HEAD), HEAD)
-    total = dq = None
+    total = out = dq = None
     if ahead:
-        head, s_ref, stat_ref = ahead
-        grad = x_ref[:, second(head)]
+        head, s_ref, g_ref, sum_ref = ahead
         top = scores(x_ref[:, first(head)], s_ref, k_s, bias_s)
     if behind:
-        last, p_ref, last_ref = behind
-        last_query, last_grad = x_ref[:, first(last)], x_ref[:, second(last)]
-        inverse, delta = last_ref[0:1, :], last_ref[1:2, :]
-        coming = dot(v_s[0], last_grad, NT)
+        last, p_ref, last_ref, delta_ref = behind
+        query, grad = x_ref[:, first(last)], last_ref[...]
+        delta = delta_ref[0:1, :]
+        coming = dot(v_s[0], grad, NT)
     for c in range(CHUNKS):
         if behind:
             dp = coming
             if c + 1 < CHUNKS:
-                coming = dot(v_s[c + 1], last_grad, NT)
+                coming = dot(v_s[c + 1], grad, NT)
         if ahead:
-            total = weigh(c, s_ref, top, total)
+            total, p16 = weigh(c, s_ref, top, total)
+            term = dot(vt_s[c], p16)
+            out = term if out is None else out + term
         if behind:
-            ds = (p_ref[c] * ((dp - delta) * inverse)).astype(jnp.bfloat16)
+            p = p_ref[c]
+            ds = (p * (dp - delta)).astype(jnp.bfloat16)
             term = dot(kt_s[c], ds)
             dq = term if dq is None else dq + term
-            dk_s[c] += dot(ds, last_query)
+            dk_s[c] += dot(ds, query)
+            dv_s[c] += dot(p.astype(jnp.bfloat16), grad)
     if behind:
         y_ref[:, second(last)] = (dq * SCALE).T.astype(jnp.bfloat16)
     if ahead:
-        collect(grad, s_ref, total, y_ref, first(head), stat_ref, vt_s, dv_s)
-
-
-def attention_body(core_ref, x_ref, own, two, four, six, mate, y_ref, mine_ref, mate_ref, k_s, v_s, kt_s, vt_s, bias_s, dk_s, dv_s, even_s, odd_s, even_t, odd_t):
+        inverse = 1.0 / total
+        out16 = (out * inverse).astype(jnp.bfloat16).astype(jnp.float32)
+        y_ref[:, first(head)] = out16.T.astype(jnp.bfloat16)
+        full = x_ref[:, second(head)].astype(jnp.float32)
+        sum_ref[0:1, :] = jnp.sum(full.T * out16, axis=0, keepdims=True) * inverse
+        g_ref[...] = (full * jnp.broadcast_to(inverse, (HEAD, BLOCK)).T).astype(jnp.bfloat16)
+
+
+def attention_body(core_ref, x_ref, own, two, four, six, mate, y_ref, mine_ref, mate_ref, k_s, v_s, kt_s, vt_s, bias_s, dk_s, dv_s, even_s, odd_s, even_g, odd_g, even_t, odd_t):
     core = core_ref[0]
     heads = x_ref.shape[1] // (2 * HEAD)
     prepare(core, own, two, four, six, mate, k_s, v_s, kt_s, vt_s, bias_s, dk_s, dv_s)
     refs = (x_ref, y_ref, k_s, v_s, kt_s, vt_s, bias_s, dk_s, dv_s)
-    step((0, even_s, even_t), None, *refs)
+    step((0, even_s, even_g, even_t), None, *refs)
 
     def pair(i, _):
         head = 2 * i
-        step((head + 1, odd_s, odd_t), (head, even_s, even_t), *refs)
-        step((head + 2, even_s, even_t), (head + 1, odd_s, odd_t), *refs)
+        step((head + 1, odd_s, odd_g, odd_t), (head, even_s, even_g, even_t), *refs)
+        step((head + 2, even_s, even_g, even_t), (head + 1, odd_s, odd_g, odd_t), *refs)
         return 0
 
     lax.fori_loop(0, heads // 2 - 1, pair, 0)
-    step((heads - 1, odd_s, odd_t), (heads - 2, even_s, even_t), *refs)
-    step(None, (heads - 1, odd_s, odd_t), *refs)
+    step((heads - 1, odd_s, odd_g, odd_t), (heads - 2, even_s, even_g, even_t), *refs)
+    step(None, (heads - 1, odd_s, odd_g, odd_t), *refs)
     for t in range(SLOTS):
         mine_ref[t, :, :HEAD] = dk_s[t] * SCALE
         mine_ref[t, :, HEAD:] = dv_s[t]
@@ -281,6 +276,8 @@
             pltpu.VMEM((CHUNKS, BLOCK, HEAD), jnp.float32),
             pltpu.VMEM((CHUNKS, BLOCK, BLOCK), jnp.float32),
             pltpu.VMEM((CHUNKS, BLOCK, BLOCK), jnp.float32),
+            pltpu.VMEM((BLOCK, HEAD), jnp.bfloat16),
+            pltpu.VMEM((BLOCK, HEAD), jnp.bfloat16),
             pltpu.VMEM((8, BLOCK), jnp.float32),
             pltpu.VMEM((8, BLOCK), jnp.float32),
         ],
@@ -325,7 +322,9 @@
     y = over_head(y.reshape(parts, -1, y.shape[1]))
     sums = mine + sent.astype(jnp.float32)
     rounded = sums.astype(jnp.bfloat16)
-    back = [shift(rounded[t], -2 * t) for t in range(1, SLOTS)]
+    back = []
+    for t in range(1, SLOTS):
+        back.append(shift(rounded[t], -2 * t))
     pieces = add_cut(at, sums[0], back, parts)
     pieces = [pieces[0]] + [around(piece, k) for k, piece in enumerate(pieces) if k]
     attended, query_grad = unpack(y, (y.shape[2] // 2,) * 2)

time: 113 us -> 112 us (level)
  no operation moved by 1% of the time
where the time goes in v5:
time: 112 us; the launch traced here: 111 us
  starting transfers between devices  53.5 us (48%)
  waiting for transfers between devices  32.3 us (29%)
  Pallas kernels  21.3 us (19%)
  local copies, waits for them, and re-layouts  1.65 us (1%)
  other arithmetic  1.29 us (1%)
    ppermute x6, starting transfers between devices, shift(): lax.ppermute(value, 'ctx', [(s, s + steps) for s in range(max(0, -steps),...  20.6 us
    ppermute x7, starting transfers between devices, around(): lax.ppermute(value, 'head', [(s, (s + steps) % count) for s in range(coun...  17 us
    all_to_all x3, starting transfers between devices, over_head(): lax.all_to_all(value, 'head', split_axis=0, concat_axis=0, tiled=True)  15.7 us
    pallas_call x1, Pallas kernels, attention(): pl.pallas_call(attention_body, out_shape=(jax.ShapeDtypeStruct(x.shape, j...  15.5 us
    all_to_all x3, waiting for transfers between devices, over_head(): lax.all_to_all(value, 'head', split_axis=0, concat_axis=0, tiled=True)  14.4 us
    ppermute x6, waiting for transfers between devices, shift(): lax.ppermute(value, 'ctx', [(s, s + steps) for s in range(max(0, -steps),...  11.8 us
    pallas_call x2, Pallas kernels, pack(): pl.pallas_call(functools.partial(pack_body, parts), out_shape=jax.ShapeDt...  4.02 us
    ppermute x2, waiting for transfers between devices, swap(): return lax.ppermute(value, 'ctx', [(s, s ^ 1) for s in range(count)])  3.83 us
  transfers between devices with their start and end apart: 18, of which 9 were waited for; matrix products, arithmetic and copies ran while one was open for 1% of the time, Pallas kernels for 3%

profile of v5, /device:TPU:2, one launch (start us, length us, event | category | flops | bytes accessed | tf_op | source)
XLA Modules:
  0.0 111.1 jit_solution(17488432697828082362)
XLA Ops:
  0.6 1.7 %shard_map.85 = bf16[8,32,256]{2,1,0:T(8,128)(2,1)} custom-call(bf16[32,1024]{1,0:T(8,128)(2,1)} %refs_0_.3, bf16[32,1024]{1,0:T(8,128)(2,1)} %refs_1_.3), custom_call_target="tpu_custom_call" | custom-call | flops 65536 | bytes 262144 | tf_op jit(solution)/shard_map/pallas_call | solution.py:55
  2.3 8.5 %all-to-all-start.1 = ((bf16[8,32,256]{2,1,0:T(8,128)(2,1)}), bf16[8,32,256]{2,1,0:T(8,128)(2,1)S(1)}, u32[]{:S(2)}, u32[]{:S(2)}) async-start(bf16[8,32,256]{2,1,0:T(8,128)(2,1)} %shard_map.85), calls=%async_computation.1 | async-start | bytes 262144 | tf_op jit(solution)/shard_map/all_to_all | solution.py:301
  10.8 2.4 %shard_map.84 = bf16[8,32,2048]{2,1,0:T(8,128)(2,1)} custom-call(bf16[32,8192]{1,0:T(8,128)(2,1)} %refs_0_.2, bf16[32,8192]{1,0:T(8,128)(2,1)} %refs_1_.2), custom_call_target="tpu_custom_call" | custom-call | flops 524288 | bytes 2097152 | tf_op jit(solution)/shard_map/pallas_call | solution.py:55
  13.1 0.0 copy-start.3
  13.2 6.7 %all-to-all-done.1 = bf16[8,32,256]{2,1,0:T(8,128)(2,1)S(1)} async-done(((bf16[8,32,256]{2,1,0:T(8,128)(2,1)}), bf16[8,32,256]{2,1,0:T(8,128)(2,1)S(1)}, u32[]{:S(2)}, u32[]{:S(2)}) %all-to-all-start.1) | async-done | bytes 131104 | tf_op jit(solution)/shard_map/all_to_all | solution.py:301
  19.9 3.6 %all-to-all-start = ((bf16[8,32,2048]{2,1,0:T(8,128)(2,1)}), bf16[8,32,2048]{2,1,0:T(8,128)(2,1)S(1)}, u32[]{:S(2)}, u32[]{:S(2)}) async-start(bf16[8,32,2048]{2,1,0:T(8,128)(2,1)} %shard_map.84), calls=%async_computation | async-start | bytes 2097152 | tf_op jit(solution)/shard_map/all_to_all | solution.py:301
  23.4 0.0 copy-done.3
  23.5 4.9 %collective-permute-start.2 = (bf16[272,256]{1,0:T(8,128)(2,1)S(1)}, bf16[272,256]{1,0:T(8,128)(2,1)S(1)}, u32[]{:S(2)}, u32[]{:S(2)}) collective-permute-start(bf16[272,256]{1,0:T(8,128)(2,1)S(1)} %get-tuple-element.40.own), channel_id=1, source_target_pairs={{0,48},{8,56},{16,64},{24,72},{32,80},{40,88},{48,96},{56,104},{64... | collective-permute-start | bytes 417800 | tf_op jit(solution)/shard_map/ppermute | solution.py:292
  28.4 3.5 %collective-permute-start.1 = (bf16[272,256]{1,0:T(8,128)(2,1)S(1)}, bf16[272,256]{1,0:T(8,128)(2,1)S(1)}, u32[]{:S(2)}, u32[]{:S(2)}) collective-permute-start(bf16[272,256]{1,0:T(8,128)(2,1)S(1)} %get-tuple-element.40.own), channel_id=1, source_target_pairs={{0,32},{8,40},{16,48},{24,56},{32,64},{40,72},{48,80},{56,88},{64,... | collective-permute-start | bytes 417800 | tf_op jit(solution)/shard_map/ppermute | solution.py:292
  31.9 2.9 %collective-permute-start = (bf16[272,256]{1,0:T(8,128)(2,1)S(1)}, bf16[272,256]{1,0:T(8,128)(2,1)S(1)}, u32[]{:S(2)}, u32[]{:S(2)}) collective-permute-start(bf16[272,256]{1,0:T(8,128)(2,1)S(1)} %get-tuple-element.40.own), channel_id=1, source_target_pairs={{0,16},{8,24},{16,32},{24,40},{32,48},{40,56},{48,64},{56,72},{64,... | collective-permute-start | bytes 417800 | tf_op jit(solution)/shard_map/ppermute | solution.py:292
  34.8 0.0 collective-permute-done.2.six
  34.8 4.0 %collective-permute-done.1.four = bf16[272,256]{1,0:T(8,128)(2,1)S(1)} collective-permute-done((bf16[272,256]{1,0:T(8,128)(2,1)S(1)}, bf16[272,256]{1,0:T(8,128)(2,1)S(1)}, u32[]{:S(2)}, u32[]{:S(2)}) %collective-permute-start.1) | collective-permute-done | bytes 139296 | tf_op jit(solution)/shard_map/ppermute | solution.py:292
  38.8 2.1 %collective-permute-done.two = bf16[272,256]{1,0:T(8,128)(2,1)S(1)} collective-permute-done((bf16[272,256]{1,0:T(8,128)(2,1)S(1)}, bf16[272,256]{1,0:T(8,128)(2,1)S(1)}, u32[]{:S(2)}, u32[]{:S(2)}) %collective-permute-start) | collective-permute-done | bytes 139296 | tf_op jit(solution)/shard_map/ppermute | solution.py:292
  41.0 0.1 pad_maximum_fusion
  41.0 0.1 collective-permute-start.3
  41.1 1.9 %collective-permute-done.3.mate = bf16[4,272,256]{2,1,0:T(8,128)(2,1)S(1)} collective-permute-done((bf16[4,272,256]{2,1,0:T(8,128)(2,1)S(1)}, bf16[4,272,256]{2,1,0:T(8,128)(2,1)S(1)}, u32[]{:S(2)}, u32[]{:S(2)}) %collective-permute-start.3) | collective-permute-done | bytes 557088 | tf_op jit(solution)/shard_map/ppermute | solution.py:297
  43.1 7.7 %all-to-all-done = bf16[8,32,2048]{2,1,0:T(8,128)(2,1)S(1)} async-done(((bf16[8,32,2048]{2,1,0:T(8,128)(2,1)}), bf16[8,32,2048]{2,1,0:T(8,128)(2,1)S(1)}, u32[]{:S(2)}, u32[]{:S(2)}) %all-to-all-start) | async-done | bytes 1048608 | tf_op jit(solution)/shard_map/all_to_all | solution.py:301
  50.7 15.5 %attention.1 = (bf16[256,2048]{1,0:T(8,128)(2,1)}, f32[4,256,256]{2,1,0:T(8,128)S(1)}, bf16[4,256,256]{2,1,0:T(8,128)(2,1)S(1)}) custom-call(s32[1]{0:T(128)} %bitcast.core_ref, bf16[256,2048]{1,0:T(8,128)(2,1)S(1)} %bitcast.18, bf16[272,256]{1,0:T(8,128)(2,1)S(1)} %get-tuple-element.40.own, bf16[272,256]{1,0:T(8,128)(2,1)S(1)} %collective-permute-done.two, ...), custom_call_target="tpu_custom_call" | custom-call | flops 5637144576 | bytes 5242880 | tf_op jit(solution)/shard_map/attention/pallas_call | solution.py:260
  66.2 0.0 copy-start
  66.2 0.8 copy-done
  67.0 0.0 copy-start.1
  67.0 3.7 %all-to-all-start.2 = ((bf16[8,32,2048]{2,1,0:T(8,128)(2,1)}), bf16[8,32,2048]{2,1,0:T(8,128)(2,1)S(1)}, u32[]{:S(2)}, u32[]{:S(2)}) async-start(bf16[8,32,2048]{2,1,0:T(8,128)(2,1)} %bitcast.7), calls=%async_computation.2 | async-start | bytes 2097152 | tf_op jit(solution)/shard_map/all_to_all | solution.py:301
  70.7 0.0 copy-done.1
  70.7 0.1 collective-permute-start.4
  70.8 1.9 %collective-permute-done.4 = bf16[4,256,256]{2,1,0:T(8,128)(2,1)S(1)} collective-permute-done((bf16[4,256,256]{2,1,0:T(8,128)(2,1)S(1)}, bf16[4,256,256]{2,1,0:T(8,128)(2,1)S(1)}, u32[]{:S(2)}, u32[]{:S(2)}) %collective-permute-start.4) | collective-permute-done | bytes 524320 | tf_op jit(solution)/shard_map/ppermute | solution.py:297
  72.7 0.0 copy-start.2
  72.7 0.8 copy-done.2
  73.5 1.2 %fusion.3 = (bf16[4,256,256]{2,1,0:T(8,128)(2,1)S(1)}, f32[4,256,256]{2,1,0:T(8,128)S(1)}) fusion(f32[4,256,256]{2,1,0:T(8,128)S(1)} %get-tuple-element.22, bf16[4,256,256]{2,1,0:T(8,128)(2,1)} %copy-done.2), kind=kLoop, calls=%fused_computation.11 | loop fusion | flops 786432 | bytes 3145728 | tf_op jit(solution)/shard_map/convert_element_type | solution.py:324
  74.7 3.5 %collective-permute-start.7 = (bf16[256,256]{1,0:T(8,128)(2,1)S(1)}, bf16[256,256]{1,0:T(8,128)(2,1)S(1)}, u32[]{:S(2)}, u32[]{:S(2)}) collective-permute-start(bf16[256,256]{1,0:T(8,128)(2,1)S(1)} %get-tuple-element.36), channel_id=1, source_target_pairs={{48,0},{56,8},{64,16},{72,24},{80,32},{88,40},{96,48},{104,56},{11... | collective-permute-start | bytes 393224 | tf_op jit(solution)/shard_map/ppermute | solution.py:292
  78.2 2.9 %collective-permute-start.6 = (bf16[256,256]{1,0:T(8,128)(2,1)S(1)}, bf16[256,256]{1,0:T(8,128)(2,1)S(1)}, u32[]{:S(2)}, u32[]{:S(2)}) collective-permute-start(bf16[256,256]{1,0:T(8,128)(2,1)S(1)} %get-tuple-element.37), channel_id=1, source_target_pairs={{32,0},{40,8},{48,16},{56,24},{64,32},{72,40},{80,48},{88,56},{96,... | collective-permute-start | bytes 393224 | tf_op jit(solution)/shard_map/ppermute | solution.py:292
  81.1 3.0 %collective-permute-start.5 = (bf16[256,256]{1,0:T(8,128)(2,1)S(1)}, bf16[256,256]{1,0:T(8,128)(2,1)S(1)}, u32[]{:S(2)}, u32[]{:S(2)}) collective-permute-start(bf16[256,256]{1,0:T(8,128)(2,1)S(1)} %get-tuple-element.38), channel_id=1, source_target_pairs={{16,0},{24,8},{32,16},{40,24},{48,32},{56,40},{64,48},{72,56},{80,... | collective-permute-start | bytes 393224 | tf_op jit(solution)/shard_map/ppermute | solution.py:292
  84.1 0.0 collective-permute-done.7.three_ref
  84.1 4.2 %collective-permute-done.6.two_ref = bf16[256,256]{1,0:T(8,128)(2,1)S(1)} collective-permute-done((bf16[256,256]{1,0:T(8,128)(2,1)S(1)}, bf16[256,256]{1,0:T(8,128)(2,1)S(1)}, u32[]{:S(2)}, u32[]{:S(2)}) %collective-permute-start.6) | collective-permute-done | bytes 131104 | tf_op jit(solution)/shard_map/ppermute | solution.py:292
  88.3 1.5 %collective-permute-done.5.one_ref = bf16[256,256]{1,0:T(8,128)(2,1)S(1)} collective-permute-done((bf16[256,256]{1,0:T(8,128)(2,1)S(1)}, bf16[256,256]{1,0:T(8,128)(2,1)S(1)}, u32[]{:S(2)}, u32[]{:S(2)}) %collective-permute-start.5) | collective-permute-done | bytes 131104 | tf_op jit(solution)/shard_map/ppermute | solution.py:292
  89.8 0.1 add_cut.1
  89.9 1.9 %collective-permute-start.8 = (bf16[32,256]{1,0:T(8,128)(2,1)S(1)}, bf16[32,256]{1,0:T(8,128)(2,1)S(1)}, u32[]{:S(2)}, u32[]{:S(2)}) collective-permute-start(bf16[32,256]{1,0:T(8,128)(2,1)S(1)} %get-tuple-element.25), channel_id=1, source_target_pairs={{0,1},{1,2},{2,3},{3,4},{4,5},{5,6},{6,7},{7,0},{8,9},{9,10},{10,1... | collective-permute-start | bytes 49160 | tf_op jit(solution)/shard_map/ppermute | solution.py:306
  91.8 2.4 %collective-permute-start.9 = (bf16[32,256]{1,0:T(8,128)(2,1)S(1)}, bf16[32,256]{1,0:T(8,128)(2,1)S(1)}, u32[]{:S(2)}, u32[]{:S(2)}) collective-permute-start(bf16[32,256]{1,0:T(8,128)(2,1)S(1)} %get-tuple-element.26), channel_id=1, source_target_pairs={{0,2},{1,3},{2,4},{3,5},{4,6},{5,7},{6,0},{7,1},{8,10},{9,11},{10,... | collective-permute-start | bytes 49160 | tf_op jit(solution)/shard_map/ppermute | solution.py:306
  94.1 2.7 %collective-permute-start.10 = (bf16[32,256]{1,0:T(8,128)(2,1)S(1)}, bf16[32,256]{1,0:T(8,128)(2,1)S(1)}, u32[]{:S(2)}, u32[]{:S(2)}) collective-permute-start(bf16[32,256]{1,0:T(8,128)(2,1)S(1)} %get-tuple-element.27), channel_id=1, source_target_pairs={{0,3},{1,4},{2,5},{3,6},{4,7},{5,0},{6,1},{7,2},{8,11},{9,12},{10,... | collective-permute-start | bytes 49160 | tf_op jit(solution)/shard_map/ppermute | solution.py:306
  96.8 2.3 %collective-permute-start.11 = (bf16[32,256]{1,0:T(8,128)(2,1)S(1)}, bf16[32,256]{1,0:T(8,128)(2,1)S(1)}, u32[]{:S(2)}, u32[]{:S(2)}) collective-permute-start(bf16[32,256]{1,0:T(8,128)(2,1)S(1)} %get-tuple-element.28), channel_id=1, source_target_pairs={{0,4},{1,5},{2,6},{3,7},{4,0},{5,1},{6,2},{7,3},{8,12},{9,13},{10,... | collective-permute-start | bytes 49160 | tf_op jit(solution)/shard_map/ppermute | solution.py:306
  99.2 2.7 %collective-permute-start.12 = (bf16[32,256]{1,0:T(8,128)(2,1)S(1)}, bf16[32,256]{1,0:T(8,128)(2,1)S(1)}, u32[]{:S(2)}, u32[]{:S(2)}) collective-permute-start(bf16[32,256]{1,0:T(8,128)(2,1)S(1)} %get-tuple-element.29), channel_id=1, source_target_pairs={{0,5},{1,6},{2,7},{3,0},{4,1},{5,2},{6,3},{7,4},{8,13},{9,14},{10,... | collective-permute-start | bytes 49160 | tf_op jit(solution)/shard_map/ppermute | solution.py:306
  101.9 0.0 collective-permute-done.8.refs_1_
  101.9 3.6 %collective-permute-start.13 = (bf16[32,256]{1,0:T(8,128)(2,1)S(1)}, bf16[32,256]{1,0:T(8,128)(2,1)S(1)}, u32[]{:S(2)}, u32[]{:S(2)}) collective-permute-start(bf16[32,256]{1,0:T(8,128)(2,1)S(1)} %get-tuple-element.30), channel_id=1, source_target_pairs={{0,6},{1,7},{2,0},{3,1},{4,2},{5,3},{6,4},{7,5},{8,14},{9,15},{10,... | collective-permute-start | bytes 49160 | tf_op jit(solution)/shard_map/ppermute | solution.py:306
  105.4 0.0 collective-permute-done.9.refs_2_
  105.4 1.5 %collective-permute-start.14 = (bf16[32,256]{1,0:T(8,128)(2,1)S(1)}, bf16[32,256]{1,0:T(8,128)(2,1)S(1)}, u32[]{:S(2)}, u32[]{:S(2)}) collective-permute-start(bf16[32,256]{1,0:T(8,128)(2,1)S(1)} %get-tuple-element.31), channel_id=1, source_target_pairs={{0,7},{1,0},{2,1},{3,2},{4,3},{5,4},{6,5},{7,6},{8,15},{9,8},{10,9... | collective-permute-start | bytes 49160 | tf_op jit(solution)/shard_map/ppermute | solution.py:306
  106.9 0.0 collective-permute-done.10.refs_3_
  106.9 0.0 collective-permute-done.11.refs_4_
  106.9 0.0 collective-permute-done.12.refs_5_
  106.9 0.0 collective-permute-done.13.refs_6_
  106.9 2.3 %collective-permute-done.14.refs_7_ = bf16[32,256]{1,0:T(8,128)(2,1)S(1)} collective-permute-done((bf16[32,256]{1,0:T(8,128)(2,1)S(1)}, bf16[32,256]{1,0:T(8,128)(2,1)S(1)}, u32[]{:S(2)}, u32[]{:S(2)}) %collective-permute-start.14) | collective-permute-done | bytes 16416 | tf_op jit(solution)/shard_map/ppermute | solution.py:306
  109.2 0.7 join.1
  109.9 0.0 all-to-all-done.2.i_ref
  109.9 1.1 shard_map.86
  (5 shorter events, 0.1 us)
Async XLA Ops:
  2.3 17.6 %all-to-all-start.1 = ((bf16[8,32,256]{2,1,0:T(8,128)(2,1)}), bf16[8,32,256]{2,1,0:T(8,128)(2,1)S(1)}, u32[]{:S(2)}, u32[]{:S(2)}) async-start(bf16[8,32,256]{2,1,0:T(8,128)(2,1)} %shard_map.85), calls=%async_computation.1 | async-start | bytes 262144 | tf_op jit(solution)/shard_map/all_to_all | solution.py:301
  13.1 10.3 %copy-start.3 = (s32[256]{0:T(256)S(1)}, s32[256]{0:T(256)}, u32[]{:S(2)}) copy-start(s32[256]{0:T(256)} %param.9) | copy-start | bytes 3076
  19.9 30.9 %all-to-all-start = ((bf16[8,32,2048]{2,1,0:T(8,128)(2,1)}), bf16[8,32,2048]{2,1,0:T(8,128)(2,1)S(1)}, u32[]{:S(2)}, u32[]{:S(2)}) async-start(bf16[8,32,2048]{2,1,0:T(8,128)(2,1)} %shard_map.84), calls=%async_computation | async-start | bytes 2097152 | tf_op jit(solution)/shard_map/all_to_all | solution.py:301
  23.5 11.3 %collective-permute-start.2 = (bf16[272,256]{1,0:T(8,128)(2,1)S(1)}, bf16[272,256]{1,0:T(8,128)(2,1)S(1)}, u32[]{:S(2)}, u32[]{:S(2)}) collective-permute-start(bf16[272,256]{1,0:T(8,128)(2,1)S(1)} %get-tuple-element.40.own), channel_id=1, source_target_pairs={{0,48},{8,56},{16,64},{24,72},{32,80},{40,88},{48,96},{56,104},{64... | collective-permute-start | bytes 417800 | tf_op jit(solution)/shard_map/ppermute | solution.py:292
  28.4 10.4 %collective-permute-start.1 = (bf16[272,256]{1,0:T(8,128)(2,1)S(1)}, bf16[272,256]{1,0:T(8,128)(2,1)S(1)}, u32[]{:S(2)}, u32[]{:S(2)}) collective-permute-start(bf16[272,256]{1,0:T(8,128)(2,1)S(1)} %get-tuple-element.40.own), channel_id=1, source_target_pairs={{0,32},{8,40},{16,48},{24,56},{32,64},{40,72},{48,80},{56,88},{64,... | collective-permute-start | bytes 417800 | tf_op jit(solution)/shard_map/ppermute | solution.py:292
  31.9 9.1 %collective-permute-start = (bf16[272,256]{1,0:T(8,128)(2,1)S(1)}, bf16[272,256]{1,0:T(8,128)(2,1)S(1)}, u32[]{:S(2)}, u32[]{:S(2)}) collective-permute-start(bf16[272,256]{1,0:T(8,128)(2,1)S(1)} %get-tuple-element.40.own), channel_id=1, source_target_pairs={{0,16},{8,24},{16,32},{24,40},{32,48},{40,56},{48,64},{56,72},{64,... | collective-permute-start | bytes 417800 | tf_op jit(solution)/shard_map/ppermute | solution.py:292
  41.0 2.0 %collective-permute-start.3 = (bf16[4,272,256]{2,1,0:T(8,128)(2,1)S(1)}, bf16[4,272,256]{2,1,0:T(8,128)(2,1)S(1)}, u32[]{:S(2)}, u32[]{:S(2)}) collective-permute-start(bf16[4,272,256]{2,1,0:T(8,128)(2,1)S(1)} %pad_maximum_fusion), channel_id=1, source_target_pairs={{0,8},{8,0},{16,24},{24,16},{32,40},{40,32},{48,56},{56,48},{64,72... | collective-permute-start | bytes 1671176 | tf_op jit(solution)/shard_map/ppermute | solution.py:297
  66.2 0.8 copy-start
  67.0 3.7 %copy-start.1 = (bf16[4,256,256]{2,1,0:T(8,128)(2,1)S(1)}, bf16[4,256,256]{2,1,0:T(8,128)(2,1)}, u32[]{:S(2)}) copy-start(bf16[4,256,256]{2,1,0:T(8,128)(2,1)} %copy-done) | copy-start | bytes 1572868
  67.0 42.9 %all-to-all-start.2 = ((bf16[8,32,2048]{2,1,0:T(8,128)(2,1)}), bf16[8,32,2048]{2,1,0:T(8,128)(2,1)S(1)}, u32[]{:S(2)}, u32[]{:S(2)}) async-start(bf16[8,32,2048]{2,1,0:T(8,128)(2,1)} %bitcast.7), calls=%async_computation.2 | async-start | bytes 2097152 | tf_op jit(solution)/shard_map/all_to_all | solution.py:301
  70.7 2.0 %collective-permute-start.4 = (bf16[4,256,256]{2,1,0:T(8,128)(2,1)S(1)}, bf16[4,256,256]{2,1,0:T(8,128)(2,1)S(1)}, u32[]{:S(2)}, u32[]{:S(2)}) collective-permute-start(bf16[4,256,256]{2,1,0:T(8,128)(2,1)S(1)} %copy-done.1), channel_id=1, source_target_pairs={{0,8},{8,0},{16,24},{24,16},{32,40},{40,32},{48,56},{56,48},{64,72... | collective-permute-start | bytes 1572872 | tf_op jit(solution)/shard_map/ppermute | solution.py:297
  72.7 0.8 copy-start.2
  74.7 9.4 %collective-permute-start.7 = (bf16[256,256]{1,0:T(8,128)(2,1)S(1)}, bf16[256,256]{1,0:T(8,128)(2,1)S(1)}, u32[]{:S(2)}, u32[]{:S(2)}) collective-permute-start(bf16[256,256]{1,0:T(8,128)(2,1)S(1)} %get-tuple-element.36), channel_id=1, source_target_pairs={{48,0},{56,8},{64,16},{72,24},{80,32},{88,40},{96,48},{104,56},{11... | collective-permute-start | bytes 393224 | tf_op jit(solution)/shard_map/ppermute | solution.py:292
  78.2 10.1 %collective-permute-start.6 = (bf16[256,256]{1,0:T(8,128)(2,1)S(1)}, bf16[256,256]{1,0:T(8,128)(2,1)S(1)}, u32[]{:S(2)}, u32[]{:S(2)}) collective-permute-start(bf16[256,256]{1,0:T(8,128)(2,1)S(1)} %get-tuple-element.37), channel_id=1, source_target_pairs={{32,0},{40,8},{48,16},{56,24},{64,32},{72,40},{80,48},{88,56},{96,... | collective-permute-start | bytes 393224 | tf_op jit(solution)/shard_map/ppermute | solution.py:292
  81.1 8.7 %collective-permute-start.5 = (bf16[256,256]{1,0:T(8,128)(2,1)S(1)}, bf16[256,256]{1,0:T(8,128)(2,1)S(1)}, u32[]{:S(2)}, u32[]{:S(2)}) collective-permute-start(bf16[256,256]{1,0:T(8,128)(2,1)S(1)} %get-tuple-element.38), channel_id=1, source_target_pairs={{16,0},{24,8},{32,16},{40,24},{48,32},{56,40},{64,48},{72,56},{80,... | collective-permute-start | bytes 393224 | tf_op jit(solution)/shard_map/ppermute | solution.py:292
  89.9 12.0 %collective-permute-start.8 = (bf16[32,256]{1,0:T(8,128)(2,1)S(1)}, bf16[32,256]{1,0:T(8,128)(2,1)S(1)}, u32[]{:S(2)}, u32[]{:S(2)}) collective-permute-start(bf16[32,256]{1,0:T(8,128)(2,1)S(1)} %get-tuple-element.25), channel_id=1, source_target_pairs={{0,1},{1,2},{2,3},{3,4},{4,5},{5,6},{6,7},{7,0},{8,9},{9,10},{10,1... | collective-permute-start | bytes 49160 | tf_op jit(solution)/shard_map/ppermute | solution.py:306
  91.8 13.7 %collective-permute-start.9 = (bf16[32,256]{1,0:T(8,128)(2,1)S(1)}, bf16[32,256]{1,0:T(8,128)(2,1)S(1)}, u32[]{:S(2)}, u32[]{:S(2)}) collective-permute-start(bf16[32,256]{1,0:T(8,128)(2,1)S(1)} %get-tuple-element.26), channel_id=1, source_target_pairs={{0,2},{1,3},{2,4},{3,5},{4,6},{5,7},{6,0},{7,1},{8,10},{9,11},{10,... | collective-permute-start | bytes 49160 | tf_op jit(solution)/shard_map/ppermute | solution.py:306
  94.1 12.8 %collective-permute-start.10 = (bf16[32,256]{1,0:T(8,128)(2,1)S(1)}, bf16[32,256]{1,0:T(8,128)(2,1)S(1)}, u32[]{:S(2)}, u32[]{:S(2)}) collective-permute-start(bf16[32,256]{1,0:T(8,128)(2,1)S(1)} %get-tuple-element.27), channel_id=1, source_target_pairs={{0,3},{1,4},{2,5},{3,6},{4,7},{5,0},{6,1},{7,2},{8,11},{9,12},{10,... | collective-permute-start | bytes 49160 | tf_op jit(solution)/shard_map/ppermute | solution.py:306
  96.8 10.1 %collective-permute-start.11 = (bf16[32,256]{1,0:T(8,128)(2,1)S(1)}, bf16[32,256]{1,0:T(8,128)(2,1)S(1)}, u32[]{:S(2)}, u32[]{:S(2)}) collective-permute-start(bf16[32,256]{1,0:T(8,128)(2,1)S(1)} %get-tuple-element.28), channel_id=1, source_target_pairs={{0,4},{1,5},{2,6},{3,7},{4,0},{5,1},{6,2},{7,3},{8,12},{9,13},{10,... | collective-permute-start | bytes 49160 | tf_op jit(solution)/shard_map/ppermute | solution.py:306
  99.2 7.7 %collective-permute-start.12 = (bf16[32,256]{1,0:T(8,128)(2,1)S(1)}, bf16[32,256]{1,0:T(8,128)(2,1)S(1)}, u32[]{:S(2)}, u32[]{:S(2)}) collective-permute-start(bf16[32,256]{1,0:T(8,128)(2,1)S(1)} %get-tuple-element.29), channel_id=1, source_target_pairs={{0,5},{1,6},{2,7},{3,0},{4,1},{5,2},{6,3},{7,4},{8,13},{9,14},{10,... | collective-permute-start | bytes 49160 | tf_op jit(solution)/shard_map/ppermute | solution.py:306
  101.9 5.0 %collective-permute-start.13 = (bf16[32,256]{1,0:T(8,128)(2,1)S(1)}, bf16[32,256]{1,0:T(8,128)(2,1)S(1)}, u32[]{:S(2)}, u32[]{:S(2)}) collective-permute-start(bf16[32,256]{1,0:T(8,128)(2,1)S(1)} %get-tuple-element.30), channel_id=1, source_target_pairs={{0,6},{1,7},{2,0},{3,1},{4,2},{5,3},{6,4},{7,5},{8,14},{9,15},{10,... | collective-permute-start | bytes 49160 | tf_op jit(solution)/shard_map/ppermute | solution.py:306
  105.4 3.7 %collective-permute-start.14 = (bf16[32,256]{1,0:T(8,128)(2,1)S(1)}, bf16[32,256]{1,0:T(8,128)(2,1)S(1)}, u32[]{:S(2)}, u32[]{:S(2)}) collective-permute-start(bf16[32,256]{1,0:T(8,128)(2,1)S(1)} %get-tuple-element.31), channel_id=1, source_target_pairs={{0,7},{1,0},{2,1},{3,2},{4,3},{5,4},{6,5},{7,6},{8,15},{9,8},{10,9... | collective-permute-start | bytes 49160 | tf_op jit(solution)/shard_map/ppermute | solution.py:306

commit v6 on v5

--- a/solution.py
+++ b/solution.py
@@ -16,7 +16,7 @@
 OFFSETS = (0, 2, 4, 6, 1, 3, 5)
 CHUNKS = len(OFFSETS)
 DOC_ROWS = 16
-PIECE = 64
+PIECE = 256
 SCALE = HEAD ** (-0.5)
 EXP2_SCALE = SCALE * math.log2(math.e)
 MASKED = -1e30
@@ -86,6 +86,26 @@
         compiler_params=SMALL,
         cost_estimate=pl.CostEstimate(flops=value.size, bytes_accessed=4 * value.size, transcendentals=0),
     )(value)
+
+
+def pair_body(mine_ref, sent_ref, base_ref, *o_refs):
+    base_ref[...] = mine_ref[0] + sent_ref[0].astype(jnp.float32)
+    for t, o_ref in enumerate(o_refs):
+        o_ref[...] = (mine_ref[t + 1] + sent_ref[t + 1].astype(jnp.float32)).astype(jnp.bfloat16)
+
+
+def pair(mine, sent):
+    slots, rows, columns = mine.shape
+    block = lambda kind: jax.ShapeDtypeStruct((rows, columns), kind)
+    return pl.pallas_call(
+        pair_body,
+        out_shape=(block(jnp.float32),) + (block(jnp.bfloat16),) * (slots - 1),
+        in_specs=[VMEM] * 2,
+        out_specs=(VMEM,) * slots,
+        compiler_params=SMALL,
+        cost_estimate=pl.CostEstimate(flops=mine.size, bytes_accessed=8 * mine.size, transcendentals=0),
+        name="pair",
+    )(mine, sent)
 
 
 def add_cut_body(parts, at_ref, base_ref, one_ref, two_ref, three_ref, *o_refs):
@@ -147,8 +167,8 @@
         key, value = rows[:, :HEAD], rows[:, HEAD:]
         k_s[c] = key
         v_s[c] = value
-        kt_s[c] = key.astype(jnp.float32).T.astype(jnp.bfloat16)
-        vt_s[c] = value.astype(jnp.float32).T.astype(jnp.bfloat16)
+        kt_s[c] = key.T
+        vt_s[c] = value.T
     mine = docs[0]
     by_key = jnp.broadcast_to(mine, (BLOCK, BLOCK)).T
     row = lax.broadcasted_iota(jnp.int32, (BLOCK, BLOCK), 0)
@@ -320,13 +340,14 @@
     y, mine, sent = attention(core, x, own, two, four, six, mate)
     sent = swap(sent)
     y = over_head(y.reshape(parts, -1, y.shape[1]))
-    sums = mine + sent.astype(jnp.float32)
-    rounded = sums.astype(jnp.bfloat16)
+    base, *rounded = pair(mine, sent)
     back = []
     for t in range(1, SLOTS):
-        back.append(shift(rounded[t], -2 * t))
-    pieces = add_cut(at, sums[0], back, parts)
-    pieces = [pieces[0]] + [around(piece, k) for k, piece in enumerate(pieces) if k]
+        back.append(shift(rounded[t - 1], -2 * t))
+    pieces = add_cut(at, base, back, parts)
+    far_first = sorted(range(1, parts), key=lambda k: abs(2 * k - parts))
+    moved = {k: around(pieces[k], k) for k in far_first}
+    pieces = [pieces[0]] + [moved[k] for k in range(1, parts)]
     attended, query_grad = unpack(y, (y.shape[2] // 2,) * 2)
     key_grad, value_grad = join(at, pieces)
     return attended, query_grad, key_grad, value_grad

time: 112 us -> 111 us (level)
  waiting for transfers between devices: 32.3 us -> 33.6 us
  other arithmetic: 1.29 us -> 0.1 us
    ppermute x6, waiting for transfers between devices: 11.8 us -> 13.2 us  [shift(): lax.ppermute(value, 'ctx', [(s, s + steps) for s in range(max(0, -steps),...]
    convert_element_type x1 -> x0, other arithmetic: 1.19 us -> none  [local(): rounded = sums.astype(jnp.bfloat16)]
  transfers between devices with their start and end apart: 18 -> 18, of which waited for: 9 -> 9; matrix products, arithmetic and copies ran while one was open for 1% -> 0% of each run, Pallas kernels for 3% -> 3%
where the time goes in v6:
time: 111 us; the launch traced here: 110 us
  starting transfers between devices  53.5 us (48%)
  waiting for transfers between devices  33.6 us (30%)
  Pallas kernels  21.1 us (19%)
    ppermute x6, starting transfers between devices, shift(): lax.ppermute(value, 'ctx', [(s, s + steps) for s in range(max(0, -steps),...  20.6 us
    ppermute x7, starting transfers between devices, around(): lax.ppermute(value, 'head', [(s, (s + steps) % count) for s in range(coun...  17 us
    all_to_all x3, starting transfers between devices, over_head(): lax.all_to_all(value, 'head', split_axis=0, concat_axis=0, tiled=True)  15.7 us
    pallas_call x1, Pallas kernels, attention(): pl.pallas_call(attention_body, out_shape=(jax.ShapeDtypeStruct(x.shape, j...  15.2 us
    all_to_all x3, waiting for transfers between devices, over_head(): lax.all_to_all(value, 'head', split_axis=0, concat_axis=0, tiled=True)  14.4 us
    ppermute x6, waiting for transfers between devices, shift(): lax.ppermute(value, 'ctx', [(s, s + steps) for s in range(max(0, -steps),...  13.2 us
    pallas_call x2, Pallas kernels, pack(): pl.pallas_call(functools.partial(pack_body, parts), out_shape=jax.ShapeDt...  4.02 us
    ppermute x2, waiting for transfers between devices, swap(): return lax.ppermute(value, 'ctx', [(s, s ^ 1) for s in range(count)])  3.83 us
  transfers between devices with their start and end apart: 18, of which 9 were waited for; matrix products, arithmetic and copies ran while one was open for 0% of the time, Pallas kernels for 3%

profile of v6, /device:TPU:2, one launch (start us, length us, event | category | flops | bytes accessed | tf_op | source)
XLA Modules:
  0.0 110.2 jit_solution(17694854421553798805)
XLA Ops:
  0.6 1.7 %shard_map.85 = bf16[8,32,256]{2,1,0:T(8,128)(2,1)} custom-call(bf16[32,1024]{1,0:T(8,128)(2,1)} %refs_0_.3, bf16[32,1024]{1,0:T(8,128)(2,1)} %refs_1_.3), custom_call_target="tpu_custom_call" | custom-call | flops 65536 | bytes 262144 | tf_op jit(solution)/shard_map/pallas_call | solution.py:55
  2.3 8.5 %all-to-all-start.1 = ((bf16[8,32,256]{2,1,0:T(8,128)(2,1)}), bf16[8,32,256]{2,1,0:T(8,128)(2,1)S(1)}, u32[]{:S(2)}, u32[]{:S(2)}) async-start(bf16[8,32,256]{2,1,0:T(8,128)(2,1)} %shard_map.85), calls=%async_computation.1 | async-start | bytes 262144 | tf_op jit(solution)/shard_map/all_to_all | solution.py:321
  10.8 2.4 %shard_map.84 = bf16[8,32,2048]{2,1,0:T(8,128)(2,1)} custom-call(bf16[32,8192]{1,0:T(8,128)(2,1)} %refs_0_.2, bf16[32,8192]{1,0:T(8,128)(2,1)} %refs_1_.2), custom_call_target="tpu_custom_call" | custom-call | flops 524288 | bytes 2097152 | tf_op jit(solution)/shard_map/pallas_call | solution.py:55
  13.1 0.0 copy-start.2
  13.2 6.7 %all-to-all-done.1 = bf16[8,32,256]{2,1,0:T(8,128)(2,1)S(1)} async-done(((bf16[8,32,256]{2,1,0:T(8,128)(2,1)}), bf16[8,32,256]{2,1,0:T(8,128)(2,1)S(1)}, u32[]{:S(2)}, u32[]{:S(2)}) %all-to-all-start.1) | async-done | bytes 131104 | tf_op jit(solution)/shard_map/all_to_all | solution.py:321
  19.9 3.6 %all-to-all-start = ((bf16[8,32,2048]{2,1,0:T(8,128)(2,1)}), bf16[8,32,2048]{2,1,0:T(8,128)(2,1)S(1)}, u32[]{:S(2)}, u32[]{:S(2)}) async-start(bf16[8,32,2048]{2,1,0:T(8,128)(2,1)} %shard_map.84), calls=%async_computation | async-start | bytes 2097152 | tf_op jit(solution)/shard_map/all_to_all | solution.py:321
  23.4 0.0 copy-done.2
  23.5 4.9 %collective-permute-start.2 = (bf16[272,256]{1,0:T(8,128)(2,1)S(1)}, bf16[272,256]{1,0:T(8,128)(2,1)S(1)}, u32[]{:S(2)}, u32[]{:S(2)}) collective-permute-start(bf16[272,256]{1,0:T(8,128)(2,1)S(1)} %get-tuple-element.43.own), channel_id=1, source_target_pairs={{0,48},{8,56},{16,64},{24,72},{32,80},{40,88},{48,96},{56,104},{64... | collective-permute-start | bytes 417800 | tf_op jit(solution)/shard_map/ppermute | solution.py:312
  28.4 3.5 %collective-permute-start.1 = (bf16[272,256]{1,0:T(8,128)(2,1)S(1)}, bf16[272,256]{1,0:T(8,128)(2,1)S(1)}, u32[]{:S(2)}, u32[]{:S(2)}) collective-permute-start(bf16[272,256]{1,0:T(8,128)(2,1)S(1)} %get-tuple-element.43.own), channel_id=1, source_target_pairs={{0,32},{8,40},{16,48},{24,56},{32,64},{40,72},{48,80},{56,88},{64,... | collective-permute-start | bytes 417800 | tf_op jit(solution)/shard_map/ppermute | solution.py:312
  31.9 2.9 %collective-permute-start = (bf16[272,256]{1,0:T(8,128)(2,1)S(1)}, bf16[272,256]{1,0:T(8,128)(2,1)S(1)}, u32[]{:S(2)}, u32[]{:S(2)}) collective-permute-start(bf16[272,256]{1,0:T(8,128)(2,1)S(1)} %get-tuple-element.43.own), channel_id=1, source_target_pairs={{0,16},{8,24},{16,32},{24,40},{32,48},{40,56},{48,64},{56,72},{64,... | collective-permute-start | bytes 417800 | tf_op jit(solution)/shard_map/ppermute | solution.py:312
  34.8 0.0 collective-permute-done.2.six
  34.8 4.0 %collective-permute-done.1.four = bf16[272,256]{1,0:T(8,128)(2,1)S(1)} collective-permute-done((bf16[272,256]{1,0:T(8,128)(2,1)S(1)}, bf16[272,256]{1,0:T(8,128)(2,1)S(1)}, u32[]{:S(2)}, u32[]{:S(2)}) %collective-permute-start.1) | collective-permute-done | bytes 139296 | tf_op jit(solution)/shard_map/ppermute | solution.py:312
  38.8 2.1 %collective-permute-done.two = bf16[272,256]{1,0:T(8,128)(2,1)S(1)} collective-permute-done((bf16[272,256]{1,0:T(8,128)(2,1)S(1)}, bf16[272,256]{1,0:T(8,128)(2,1)S(1)}, u32[]{:S(2)}, u32[]{:S(2)}) %collective-permute-start) | collective-permute-done | bytes 139296 | tf_op jit(solution)/shard_map/ppermute | solution.py:312
  41.0 0.1 pad_maximum_fusion
  41.0 0.1 collective-permute-start.3
  41.1 1.9 %collective-permute-done.3.mate = bf16[4,272,256]{2,1,0:T(8,128)(2,1)S(1)} collective-permute-done((bf16[4,272,256]{2,1,0:T(8,128)(2,1)S(1)}, bf16[4,272,256]{2,1,0:T(8,128)(2,1)S(1)}, u32[]{:S(2)}, u32[]{:S(2)}) %collective-permute-start.3) | collective-permute-done | bytes 557088 | tf_op jit(solution)/shard_map/ppermute | solution.py:317
  43.1 7.7 %all-to-all-done = bf16[8,32,2048]{2,1,0:T(8,128)(2,1)S(1)} async-done(((bf16[8,32,2048]{2,1,0:T(8,128)(2,1)}), bf16[8,32,2048]{2,1,0:T(8,128)(2,1)S(1)}, u32[]{:S(2)}, u32[]{:S(2)}) %all-to-all-start) | async-done | bytes 1048608 | tf_op jit(solution)/shard_map/all_to_all | solution.py:321
  50.7 15.2 %attention.1 = (bf16[256,2048]{1,0:T(8,128)(2,1)}, f32[4,256,256]{2,1,0:T(8,128)S(1)}, bf16[4,256,256]{2,1,0:T(8,128)(2,1)S(1)}) custom-call(s32[1]{0:T(128)} %bitcast.core_ref, bf16[256,2048]{1,0:T(8,128)(2,1)S(1)} %bitcast.10, bf16[272,256]{1,0:T(8,128)(2,1)S(1)} %get-tuple-element.43.own, bf16[272,256]{1,0:T(8,128)(2,1)S(1)} %collective-permute-done.two, ...), custom_call_target="tpu_custom_call" | custom-call | flops 5637144576 | bytes 5242880 | tf_op jit(solution)/shard_map/attention/pallas_call | solution.py:280
  65.9 0.0 copy-start
  65.9 0.8 copy-done
  66.7 0.0 copy-start.1
  66.7 3.7 %all-to-all-start.2 = ((bf16[8,32,2048]{2,1,0:T(8,128)(2,1)}), bf16[8,32,2048]{2,1,0:T(8,128)(2,1)S(1)}, u32[]{:S(2)}, u32[]{:S(2)}) async-start(bf16[8,32,2048]{2,1,0:T(8,128)(2,1)} %bitcast.7), calls=%async_computation.2 | async-start | bytes 2097152 | tf_op jit(solution)/shard_map/all_to_all | solution.py:321
  70.4 0.0 copy-done.1
  70.4 0.1 collective-permute-start.4
  70.5 1.9 %collective-permute-done.4.sent_ref = bf16[4,256,256]{2,1,0:T(8,128)(2,1)S(1)} collective-permute-done((bf16[4,256,256]{2,1,0:T(8,128)(2,1)S(1)}, bf16[4,256,256]{2,1,0:T(8,128)(2,1)S(1)}, u32[]{:S(2)}, u32[]{:S(2)}) %collective-permute-start.4) | collective-permute-done | bytes 524320 | tf_op jit(solution)/shard_map/ppermute | solution.py:317
  72.4 0.1 pair.1
  72.5 4.9 %collective-permute-start.5 = (bf16[256,256]{1,0:T(8,128)(2,1)S(1)}, bf16[256,256]{1,0:T(8,128)(2,1)S(1)}, u32[]{:S(2)}, u32[]{:S(2)}) collective-permute-start(bf16[256,256]{1,0:T(8,128)(2,1)S(1)} %get-tuple-element.29), channel_id=1, source_target_pairs={{16,0},{24,8},{32,16},{40,24},{48,32},{56,40},{64,48},{72,56},{80,... | collective-permute-start | bytes 393224 | tf_op jit(solution)/shard_map/ppermute | solution.py:312
  77.4 2.5 %collective-permute-start.6 = (bf16[256,256]{1,0:T(8,128)(2,1)S(1)}, bf16[256,256]{1,0:T(8,128)(2,1)S(1)}, u32[]{:S(2)}, u32[]{:S(2)}) collective-permute-start(bf16[256,256]{1,0:T(8,128)(2,1)S(1)} %get-tuple-element.30), channel_id=1, source_target_pairs={{32,0},{40,8},{48,16},{56,24},{64,32},{72,40},{80,48},{88,56},{96,... | collective-permute-start | bytes 393224 | tf_op jit(solution)/shard_map/ppermute | solution.py:312
  80.0 1.9 %collective-permute-start.7 = (bf16[256,256]{1,0:T(8,128)(2,1)S(1)}, bf16[256,256]{1,0:T(8,128)(2,1)S(1)}, u32[]{:S(2)}, u32[]{:S(2)}) collective-permute-start(bf16[256,256]{1,0:T(8,128)(2,1)S(1)} %get-tuple-element.31), channel_id=1, source_target_pairs={{48,0},{56,8},{64,16},{72,24},{80,32},{88,40},{96,48},{104,56},{11... | collective-permute-start | bytes 393224 | tf_op jit(solution)/shard_map/ppermute | solution.py:312
  81.9 0.0 collective-permute-done.5.one_ref
  81.9 4.3 %collective-permute-done.6.two_ref = bf16[256,256]{1,0:T(8,128)(2,1)S(1)} collective-permute-done((bf16[256,256]{1,0:T(8,128)(2,1)S(1)}, bf16[256,256]{1,0:T(8,128)(2,1)S(1)}, u32[]{:S(2)}, u32[]{:S(2)}) %collective-permute-start.6) | collective-permute-done | bytes 131104 | tf_op jit(solution)/shard_map/ppermute | solution.py:312
  86.2 2.7 %collective-permute-done.7.three_ref = bf16[256,256]{1,0:T(8,128)(2,1)S(1)} collective-permute-done((bf16[256,256]{1,0:T(8,128)(2,1)S(1)}, bf16[256,256]{1,0:T(8,128)(2,1)S(1)}, u32[]{:S(2)}, u32[]{:S(2)}) %collective-permute-start.7) | collective-permute-done | bytes 131104 | tf_op jit(solution)/shard_map/ppermute | solution.py:312
  88.9 0.1 add_cut.1
  89.0 1.9 %collective-permute-start.8 = (bf16[32,256]{1,0:T(8,128)(2,1)S(1)}, bf16[32,256]{1,0:T(8,128)(2,1)S(1)}, u32[]{:S(2)}, u32[]{:S(2)}) collective-permute-start(bf16[32,256]{1,0:T(8,128)(2,1)S(1)} %get-tuple-element.33), channel_id=1, source_target_pairs={{0,1},{1,2},{2,3},{3,4},{4,5},{5,6},{6,7},{7,0},{8,9},{9,10},{10,1... | collective-permute-start | bytes 49160 | tf_op jit(solution)/shard_map/ppermute | solution.py:326
  90.9 2.4 %collective-permute-start.9 = (bf16[32,256]{1,0:T(8,128)(2,1)S(1)}, bf16[32,256]{1,0:T(8,128)(2,1)S(1)}, u32[]{:S(2)}, u32[]{:S(2)}) collective-permute-start(bf16[32,256]{1,0:T(8,128)(2,1)S(1)} %get-tuple-element.34), channel_id=1, source_target_pairs={{0,2},{1,3},{2,4},{3,5},{4,6},{5,7},{6,0},{7,1},{8,10},{9,11},{10,... | collective-permute-start | bytes 49160 | tf_op jit(solution)/shard_map/ppermute | solution.py:326
  93.2 2.7 %collective-permute-start.10 = (bf16[32,256]{1,0:T(8,128)(2,1)S(1)}, bf16[32,256]{1,0:T(8,128)(2,1)S(1)}, u32[]{:S(2)}, u32[]{:S(2)}) collective-permute-start(bf16[32,256]{1,0:T(8,128)(2,1)S(1)} %get-tuple-element.35), channel_id=1, source_target_pairs={{0,3},{1,4},{2,5},{3,6},{4,7},{5,0},{6,1},{7,2},{8,11},{9,12},{10,... | collective-permute-start | bytes 49160 | tf_op jit(solution)/shard_map/ppermute | solution.py:326
  95.9 2.3 %collective-permute-start.11 = (bf16[32,256]{1,0:T(8,128)(2,1)S(1)}, bf16[32,256]{1,0:T(8,128)(2,1)S(1)}, u32[]{:S(2)}, u32[]{:S(2)}) collective-permute-start(bf16[32,256]{1,0:T(8,128)(2,1)S(1)} %get-tuple-element.36), channel_id=1, source_target_pairs={{0,4},{1,5},{2,6},{3,7},{4,0},{5,1},{6,2},{7,3},{8,12},{9,13},{10,... | collective-permute-start | bytes 49160 | tf_op jit(solution)/shard_map/ppermute | solution.py:326
  98.3 2.7 %collective-permute-start.12 = (bf16[32,256]{1,0:T(8,128)(2,1)S(1)}, bf16[32,256]{1,0:T(8,128)(2,1)S(1)}, u32[]{:S(2)}, u32[]{:S(2)}) collective-permute-start(bf16[32,256]{1,0:T(8,128)(2,1)S(1)} %get-tuple-element.37), channel_id=1, source_target_pairs={{0,5},{1,6},{2,7},{3,0},{4,1},{5,2},{6,3},{7,4},{8,13},{9,14},{10,... | collective-permute-start | bytes 49160 | tf_op jit(solution)/shard_map/ppermute | solution.py:326
  101.0 0.0 collective-permute-done.8.refs_1_
  101.0 3.6 %collective-permute-start.13 = (bf16[32,256]{1,0:T(8,128)(2,1)S(1)}, bf16[32,256]{1,0:T(8,128)(2,1)S(1)}, u32[]{:S(2)}, u32[]{:S(2)}) collective-permute-start(bf16[32,256]{1,0:T(8,128)(2,1)S(1)} %get-tuple-element.38), channel_id=1, source_target_pairs={{0,6},{1,7},{2,0},{3,1},{4,2},{5,3},{6,4},{7,5},{8,14},{9,15},{10,... | collective-permute-start | bytes 49160 | tf_op jit(solution)/shard_map/ppermute | solution.py:326
  104.5 0.0 collective-permute-done.9.refs_2_
  104.5 1.5 %collective-permute-start.14 = (bf16[32,256]{1,0:T(8,128)(2,1)S(1)}, bf16[32,256]{1,0:T(8,128)(2,1)S(1)}, u32[]{:S(2)}, u32[]{:S(2)}) collective-permute-start(bf16[32,256]{1,0:T(8,128)(2,1)S(1)} %get-tuple-element.39), channel_id=1, source_target_pairs={{0,7},{1,0},{2,1},{3,2},{4,3},{5,4},{6,5},{7,6},{8,15},{9,8},{10,9... | collective-permute-start | bytes 49160 | tf_op jit(solution)/shard_map/ppermute | solution.py:326
  106.0 0.0 collective-permute-done.10.refs_3_
  106.0 0.0 collective-permute-done.11.refs_4_
  106.0 0.0 collective-permute-done.12.refs_5_
  106.0 0.0 collective-permute-done.13.refs_6_
  106.0 2.3 %collective-permute-done.14.refs_7_ = bf16[32,256]{1,0:T(8,128)(2,1)S(1)} collective-permute-done((bf16[32,256]{1,0:T(8,128)(2,1)S(1)}, bf16[32,256]{1,0:T(8,128)(2,1)S(1)}, u32[]{:S(2)}, u32[]{:S(2)}) %collective-permute-start.14) | collective-permute-done | bytes 16416 | tf_op jit(solution)/shard_map/ppermute | solution.py:326
  108.3 0.7 join.1
  109.0 0.0 all-to-all-done.2.i_ref
  109.0 1.1 shard_map.86
  (3 shorter events, 0.0 us)
Async XLA Ops:
  2.3 17.6 %all-to-all-start.1 = ((bf16[8,32,256]{2,1,0:T(8,128)(2,1)}), bf16[8,32,256]{2,1,0:T(8,128)(2,1)S(1)}, u32[]{:S(2)}, u32[]{:S(2)}) async-start(bf16[8,32,256]{2,1,0:T(8,128)(2,1)} %shard_map.85), calls=%async_computation.1 | async-start | bytes 262144 | tf_op jit(solution)/shard_map/all_to_all | solution.py:321
  13.1 10.3 %copy-start.2 = (s32[256]{0:T(256)S(1)}, s32[256]{0:T(256)}, u32[]{:S(2)}) copy-start(s32[256]{0:T(256)} %param.9) | copy-start | bytes 3076
  19.9 30.9 %all-to-all-start = ((bf16[8,32,2048]{2,1,0:T(8,128)(2,1)}), bf16[8,32,2048]{2,1,0:T(8,128)(2,1)S(1)}, u32[]{:S(2)}, u32[]{:S(2)}) async-start(bf16[8,32,2048]{2,1,0:T(8,128)(2,1)} %shard_map.84), calls=%async_computation | async-start | bytes 2097152 | tf_op jit(solution)/shard_map/all_to_all | solution.py:321
  23.5 11.3 %collective-permute-start.2 = (bf16[272,256]{1,0:T(8,128)(2,1)S(1)}, bf16[272,256]{1,0:T(8,128)(2,1)S(1)}, u32[]{:S(2)}, u32[]{:S(2)}) collective-permute-start(bf16[272,256]{1,0:T(8,128)(2,1)S(1)} %get-tuple-element.43.own), channel_id=1, source_target_pairs={{0,48},{8,56},{16,64},{24,72},{32,80},{40,88},{48,96},{56,104},{64... | collective-permute-start | bytes 417800 | tf_op jit(solution)/shard_map/ppermute | solution.py:312
  28.4 10.4 %collective-permute-start.1 = (bf16[272,256]{1,0:T(8,128)(2,1)S(1)}, bf16[272,256]{1,0:T(8,128)(2,1)S(1)}, u32[]{:S(2)}, u32[]{:S(2)}) collective-permute-start(bf16[272,256]{1,0:T(8,128)(2,1)S(1)} %get-tuple-element.43.own), channel_id=1, source_target_pairs={{0,32},{8,40},{16,48},{24,56},{32,64},{40,72},{48,80},{56,88},{64,... | collective-permute-start | bytes 417800 | tf_op jit(solution)/shard_map/ppermute | solution.py:312
  31.9 9.1 %collective-permute-start = (bf16[272,256]{1,0:T(8,128)(2,1)S(1)}, bf16[272,256]{1,0:T(8,128)(2,1)S(1)}, u32[]{:S(2)}, u32[]{:S(2)}) collective-permute-start(bf16[272,256]{1,0:T(8,128)(2,1)S(1)} %get-tuple-element.43.own), channel_id=1, source_target_pairs={{0,16},{8,24},{16,32},{24,40},{32,48},{40,56},{48,64},{56,72},{64,... | collective-permute-start | bytes 417800 | tf_op jit(solution)/shard_map/ppermute | solution.py:312
  41.0 2.0 %collective-permute-start.3 = (bf16[4,272,256]{2,1,0:T(8,128)(2,1)S(1)}, bf16[4,272,256]{2,1,0:T(8,128)(2,1)S(1)}, u32[]{:S(2)}, u32[]{:S(2)}) collective-permute-start(bf16[4,272,256]{2,1,0:T(8,128)(2,1)S(1)} %pad_maximum_fusion), channel_id=1, source_target_pairs={{0,8},{8,0},{16,24},{24,16},{32,40},{40,32},{48,56},{56,48},{64,72... | collective-permute-start | bytes 1671176 | tf_op jit(solution)/shard_map/ppermute | solution.py:317
  65.9 0.8 copy-start
  66.7 3.7 %copy-start.1 = (bf16[4,256,256]{2,1,0:T(8,128)(2,1)S(1)}, bf16[4,256,256]{2,1,0:T(8,128)(2,1)}, u32[]{:S(2)}) copy-start(bf16[4,256,256]{2,1,0:T(8,128)(2,1)} %copy-done) | copy-start | bytes 1572868
  66.7 42.2 %all-to-all-start.2 = ((bf16[8,32,2048]{2,1,0:T(8,128)(2,1)}), bf16[8,32,2048]{2,1,0:T(8,128)(2,1)S(1)}, u32[]{:S(2)}, u32[]{:S(2)}) async-start(bf16[8,32,2048]{2,1,0:T(8,128)(2,1)} %bitcast.7), calls=%async_computation.2 | async-start | bytes 2097152 | tf_op jit(solution)/shard_map/all_to_all | solution.py:321
  70.4 2.0 %collective-permute-start.4 = (bf16[4,256,256]{2,1,0:T(8,128)(2,1)S(1)}, bf16[4,256,256]{2,1,0:T(8,128)(2,1)S(1)}, u32[]{:S(2)}, u32[]{:S(2)}) collective-permute-start(bf16[4,256,256]{2,1,0:T(8,128)(2,1)S(1)} %copy-done.1), channel_id=1, source_target_pairs={{0,8},{8,0},{16,24},{24,16},{32,40},{40,32},{48,56},{56,48},{64,72... | collective-permute-start | bytes 1572872 | tf_op jit(solution)/shard_map/ppermute | solution.py:317
  72.5 9.4 %collective-permute-start.5 = (bf16[256,256]{1,0:T(8,128)(2,1)S(1)}, bf16[256,256]{1,0:T(8,128)(2,1)S(1)}, u32[]{:S(2)}, u32[]{:S(2)}) collective-permute-start(bf16[256,256]{1,0:T(8,128)(2,1)S(1)} %get-tuple-element.29), channel_id=1, source_target_pairs={{16,0},{24,8},{32,16},{40,24},{48,32},{56,40},{64,48},{72,56},{80,... | collective-permute-start | bytes 393224 | tf_op jit(solution)/shard_map/ppermute | solution.py:312
  77.4 8.7 %collective-permute-start.6 = (bf16[256,256]{1,0:T(8,128)(2,1)S(1)}, bf16[256,256]{1,0:T(8,128)(2,1)S(1)}, u32[]{:S(2)}, u32[]{:S(2)}) collective-permute-start(bf16[256,256]{1,0:T(8,128)(2,1)S(1)} %get-tuple-element.30), channel_id=1, source_target_pairs={{32,0},{40,8},{48,16},{56,24},{64,32},{72,40},{80,48},{88,56},{96,... | collective-permute-start | bytes 393224 | tf_op jit(solution)/shard_map/ppermute | solution.py:312
  80.0 8.9 %collective-permute-start.7 = (bf16[256,256]{1,0:T(8,128)(2,1)S(1)}, bf16[256,256]{1,0:T(8,128)(2,1)S(1)}, u32[]{:S(2)}, u32[]{:S(2)}) collective-permute-start(bf16[256,256]{1,0:T(8,128)(2,1)S(1)} %get-tuple-element.31), channel_id=1, source_target_pairs={{48,0},{56,8},{64,16},{72,24},{80,32},{88,40},{96,48},{104,56},{11... | collective-permute-start | bytes 393224 | tf_op jit(solution)/shard_map/ppermute | solution.py:312
  89.0 12.0 %collective-permute-start.8 = (bf16[32,256]{1,0:T(8,128)(2,1)S(1)}, bf16[32,256]{1,0:T(8,128)(2,1)S(1)}, u32[]{:S(2)}, u32[]{:S(2)}) collective-permute-start(bf16[32,256]{1,0:T(8,128)(2,1)S(1)} %get-tuple-element.33), channel_id=1, source_target_pairs={{0,1},{1,2},{2,3},{3,4},{4,5},{5,6},{6,7},{7,0},{8,9},{9,10},{10,1... | collective-permute-start | bytes 49160 | tf_op jit(solution)/shard_map/ppermute | solution.py:326
  90.9 13.7 %collective-permute-start.9 = (bf16[32,256]{1,0:T(8,128)(2,1)S(1)}, bf16[32,256]{1,0:T(8,128)(2,1)S(1)}, u32[]{:S(2)}, u32[]{:S(2)}) collective-permute-start(bf16[32,256]{1,0:T(8,128)(2,1)S(1)} %get-tuple-element.34), channel_id=1, source_target_pairs={{0,2},{1,3},{2,4},{3,5},{4,6},{5,7},{6,0},{7,1},{8,10},{9,11},{10,... | collective-permute-start | bytes 49160 | tf_op jit(solution)/shard_map/ppermute | solution.py:326
  93.2 12.8 %collective-permute-start.10 = (bf16[32,256]{1,0:T(8,128)(2,1)S(1)}, bf16[32,256]{1,0:T(8,128)(2,1)S(1)}, u32[]{:S(2)}, u32[]{:S(2)}) collective-permute-start(bf16[32,256]{1,0:T(8,128)(2,1)S(1)} %get-tuple-element.35), channel_id=1, source_target_pairs={{0,3},{1,4},{2,5},{3,6},{4,7},{5,0},{6,1},{7,2},{8,11},{9,12},{10,... | collective-permute-start | bytes 49160 | tf_op jit(solution)/shard_map/ppermute | solution.py:326
  95.9 10.1 %collective-permute-start.11 = (bf16[32,256]{1,0:T(8,128)(2,1)S(1)}, bf16[32,256]{1,0:T(8,128)(2,1)S(1)}, u32[]{:S(2)}, u32[]{:S(2)}) collective-permute-start(bf16[32,256]{1,0:T(8,128)(2,1)S(1)} %get-tuple-element.36), channel_id=1, source_target_pairs={{0,4},{1,5},{2,6},{3,7},{4,0},{5,1},{6,2},{7,3},{8,12},{9,13},{10,... | collective-permute-start | bytes 49160 | tf_op jit(solution)/shard_map/ppermute | solution.py:326
  98.3 7.7 %collective-permute-start.12 = (bf16[32,256]{1,0:T(8,128)(2,1)S(1)}, bf16[32,256]{1,0:T(8,128)(2,1)S(1)}, u32[]{:S(2)}, u32[]{:S(2)}) collective-permute-start(bf16[32,256]{1,0:T(8,128)(2,1)S(1)} %get-tuple-element.37), channel_id=1, source_target_pairs={{0,5},{1,6},{2,7},{3,0},{4,1},{5,2},{6,3},{7,4},{8,13},{9,14},{10,... | collective-permute-start | bytes 49160 | tf_op jit(solution)/shard_map/ppermute | solution.py:326
  101.0 5.0 %collective-permute-start.13 = (bf16[32,256]{1,0:T(8,128)(2,1)S(1)}, bf16[32,256]{1,0:T(8,128)(2,1)S(1)}, u32[]{:S(2)}, u32[]{:S(2)}) collective-permute-start(bf16[32,256]{1,0:T(8,128)(2,1)S(1)} %get-tuple-element.38), channel_id=1, source_target_pairs={{0,6},{1,7},{2,0},{3,1},{4,2},{5,3},{6,4},{7,5},{8,14},{9,15},{10,... | collective-permute-start | bytes 49160 | tf_op jit(solution)/shard_map/ppermute | solution.py:326
  104.5 3.7 %collective-permute-start.14 = (bf16[32,256]{1,0:T(8,128)(2,1)S(1)}, bf16[32,256]{1,0:T(8,128)(2,1)S(1)}, u32[]{:S(2)}, u32[]{:S(2)}) collective-permute-start(bf16[32,256]{1,0:T(8,128)(2,1)S(1)} %get-tuple-element.39), channel_id=1, source_target_pairs={{0,7},{1,0},{2,1},{3,2},{4,3},{5,4},{6,5},{7,6},{8,15},{9,8},{10,9... | collective-permute-start | bytes 49160 | tf_op jit(solution)/shard_map/ppermute | solution.py:326
